TPU v7x, 256 devices: a whole 4x4x8 slice. The times are simulated.
256 devices in a mesh: tm: 128 (over y, x, z), dp: 2 (over core).
Axes of the slice: x: 4, y: 4, z: 8, core: 2. Of those that a mesh axis runs over, the one named last changes fastest.
Arguments:
- state_feats: bfloat16 [128, 512, 256], P('dp', 'tm'), may hold values from -24 to 24
- achieved: bfloat16 [128, 512, 512], P('dp', 'tm'), may hold values from -24 to 24
- offsets: int32 [128, 512], P('dp', 'tm'), may hold values from 0 to 511, as said below
- w_in: bfloat16 [768, 2048], replicated, may hold values from -0.21875 to 0.21875
- b_in: float32 [2048], replicated, may hold values from -3 to 3
- w_out: float32 [2048], replicated, may hold values from -0.75 to 0.75
- b_out: float32 [1], replicated, may hold values from -1 to 1
Outputs:
- td_error: float32 [128, 512], P('dp', 'tm')
- grad_w_in: float32 [768, 2048], P(('tm', 'dp'))
- grad_b_in: float32 [2048], replicated
- grad_w_out: float32 [2048], replicated
- grad_b_out: float32 [1], replicated
Inputs may be any that keep to these rules, and one draw needn't show every extreme that they name: t + offsets[e, t] <= 511. The transitions held by one device (one index of dp and of tm) ask at most 4 of their goals from any other single index of tm; every device whose tm index is below the last asks exactly 4 goals from the last index, all of them at time 512 - 1.
All inputs are finite; a program needn't handle non-finite values.
Results may differ from a plain program's by a relative error of at most 0.0024.
The roundings to bfloat16 on the way count: a program that leaves them out, or rounds other values in their place, can miss the bound.
Values may be sent and summed in bfloat16 or wider, within the bound.
No kernel may reach another device: no remote copies, remote signals or barrier semaphores. Data moves between devices by JAX's collectives and lax.ppermute only.
A program may use at most 64 MiB of HBM per device.

v0:
```python
import functools
import math

import jax
import jax.numpy as jnp
from jax import lax
from jax.sharding import Mesh
from jax.sharding import PartitionSpec as P

CAP = 4
TM = ("tm_0", "tm_1", "tm_2")
TM_DP = ("tm_0", "tm_1", "tm_2", "dp")


def over_axes(shard, axes):
    return functools.reduce(lax.psum, axes, shard)


def body(state_feats, achieved, offsets, w_in, b_in, w_out, b_out):
    ep_dev, steps, goal_width = achieved.shape
    feat_width = state_feats.shape[2]
    rows = ep_dev * steps
    tm_count = lax.axis_size(TM)
    dp_count = lax.axis_size("dp")
    myself = lax.axis_index(TM)
    capacity = CAP
    times = myself * steps + jnp.arange(steps, dtype=jnp.int32)
    target = times[None, :] + offsets
    owner = (target // steps).reshape(rows)
    episode = jnp.broadcast_to(jnp.arange(ep_dev, dtype=jnp.int32)[:, None], (ep_dev, steps))
    position = (episode * steps + target % steps).reshape(rows)
    table = achieved.reshape(rows, goal_width)
    remote = owner != myself
    peers = jnp.arange(tm_count, dtype=jnp.int32)
    hits = ((owner[:, None] == peers[None, :]) & remote[:, None]).astype(jnp.int32)
    slot = jnp.sum((jnp.cumsum(hits, axis=0) - 1) * hits, axis=1)
    dest = jnp.where(remote, owner, tm_count)
    requests = (
        jnp.full((tm_count, capacity), -1, jnp.int32).at[dest, slot].set(position, mode="drop")
    )
    asked = lax.all_to_all(requests, TM, split_axis=0, concat_axis=0, tiled=True)
    picked = jnp.take(table, jnp.clip(asked, 0, rows - 1), axis=0)
    picked = jnp.where((asked >= 0)[..., None], picked, jnp.zeros((), jnp.bfloat16))
    fetched = lax.all_to_all(picked, TM, split_axis=0, concat_axis=0, tiled=True)
    fetched = fetched.reshape(tm_count * capacity, goal_width)
    far_rows = jnp.take(
        fetched, jnp.clip(owner * capacity + slot, 0, tm_count * capacity - 1), axis=0
    )
    near_rows = jnp.take(table, position, axis=0)
    goal = jnp.where(remote[:, None], far_rows, near_rows)
    inputs = jnp.concatenate([state_feats.reshape(rows, feat_width), goal], axis=1)
    pre = jnp.dot(inputs, w_in, preferred_element_type=jnp.float32) + b_in
    hidden = jax.nn.silu(pre).astype(jnp.bfloat16)
    hidden_wide = hidden.astype(jnp.float32)
    value = jnp.dot(hidden_wide, w_out, precision=lax.Precision.HIGHEST) + b_out[0]
    diff = table.astype(jnp.float32) - goal.astype(jnp.float32)
    reward = -jnp.mean(diff * diff, axis=1)
    error = value - reward
    scale = 1.0 / math.sqrt(rows * tm_count * dp_count)
    grad_value = error * scale
    sig = jax.nn.sigmoid(pre)
    grad_pre = grad_value[:, None] * w_out[None, :] * (sig * (1.0 + pre * (1.0 - sig)))
    grad_low = grad_pre.astype(jnp.bfloat16)
    small = (
        jnp.sum(grad_pre, axis=0),
        jnp.dot(grad_value, hidden_wide, precision=lax.Precision.HIGHEST),
        jnp.sum(grad_value, keepdims=True),
    )
    grad_b_in, grad_w_out, grad_b_out = (
        over_axes(small[0], TM_DP),
        over_axes(small[1], TM_DP),
        over_axes(small[2], TM_DP),
    )
    grad_w_in = lax.psum_scatter(
        lax.dot_general(
            inputs, grad_low, (((0,), (0,)), ((), ())), preferred_element_type=jnp.float32
        ),
        TM_DP,
        scatter_dimension=0,
        tiled=True,
    )
    return (error.reshape(ep_dev, steps), grad_w_in, grad_b_in, grad_w_out, grad_b_out)


def solution(mesh):
    split = Mesh(mesh.devices.reshape(4, 4, 8, mesh.shape["dp"]), ("tm_0", "tm_1", "tm_2", "dp"))
    placed = (P("dp", TM, None), P("dp", TM, None), P("dp", TM), P(), P(), P(), P())
    return jax.shard_map(
        body,
        mesh=split,
        in_specs=placed,
        out_specs=(P("dp", TM), P(TM_DP, None), P(), P(), P()),
        check_vma=False,
    )
```

profile of v0, /device:TPU:2, one launch (start us, length us, event | category | flops | bytes accessed | tf_op | source)
XLA Modules:
  0.0 384.0 jit_solution(8751551317942984027)
XLA Ops:
  7.2 1.4 broadcast_compare_fusion.1
  8.6 0.1 copy.39
  8.7 0.1 eq.28
  8.9 0.1 copy.41
  9.0 0.1 reshape.239
  9.1 0.1 reshape.241
  9.2 0.1 copy.42
  9.3 0.3 fusion.2
  9.7 0.1 add_add_fusion
  9.8 0.1 copy.45
  9.9 0.1 reshape.273
  10.1 0.2 fusion.3
  10.3 0.6 compare_select_fusion.3
  10.8 11.1 %scatter_fusion = s32[128,4]{0,1:T(4,128)S(1)} fusion(s32[128,4]{0,1:T(4,128)S(1)} %broadcast_in_dim.84, s32[256]{0:T(256)S(1)} %bitcast.31, s32[256]{0:T(256)S(1)} %reshape.273), kind=kCustom, calls=%fused_computation.3 | custom fusion | bytes 5120 | tf_op jit(solution)/shard_map/scatter | solution.py:39
  21.9 0.7 copy.46
  22.7 15.4 %all-to-all-start = ((s32[128,1,4]{2,1,0:T(1,128)}), s32[128,1,4]{2,1,0:T(1,128)S(1)}, u32[]{:S(2)}, u32[]{:S(2)}) async-start(s32[128,1,4]{2,1,0:T(1,128)} %copy.46), calls=%async_computation | async-start | bytes 131072 | tf_op jit(solution)/shard_map/all_to_all | solution.py:41
  38.1 1.0 reshape.243
  39.1 10.1 %all-to-all-done = s32[128,1,4]{2,1,0:T(1,128)S(1)} async-done(((s32[128,1,4]{2,1,0:T(1,128)}), s32[128,1,4]{2,1,0:T(1,128)S(1)}, u32[]{:S(2)}, u32[]{:S(2)}) %all-to-all-start) | async-done | bytes 2080 | tf_op jit(solution)/shard_map/all_to_all | solution.py:41
  49.2 0.1 broadcast_clamp_fusion
  49.3 0.6 compare_select_fusion
  49.9 0.9 reshape.249
  50.9 2.6 gather_fusion
  53.5 2.0 reshape.248
  55.5 0.7 broadcast_compare_fusion
  56.2 0.9 copy.47
  57.1 0.1 copy.48
  57.3 2.2 select_select_fusion
  59.5 7.8 %all-to-all-start.1 = ((bf16[128,4,512]{2,1,0:T(4,128)(2,1)}), bf16[128,4,512]{2,1,0:T(4,128)(2,1)}, u32[]{:S(2)}, u32[]{:S(2)}) async-start(bf16[128,4,512]{2,1,0:T(4,128)(2,1)} %select_select_fusion), calls=%async_computation.1 | async-start | bytes 1048576 | tf_op jit(solution)/shard_map/all_to_all | solution.py:44
  67.3 0.2 all-reduce.7.cloned.1.call-start
  67.5 0.1 reshape.245
  67.6 0.7 reduce_sum.42
  68.4 1.9 gather_fusion.2
  70.3 0.7 reshape.238
  70.9 0.8 copy.51
  71.8 0.1 copy.52
  71.9 1.7 gather.20
  73.6 0.8 copy.50
  74.4 1.4 copy.53
  76.4 1.3 pad_clamp_fusion.1
  77.7 1.2 compare_and_fusion.3
  78.9 5.3 %all-to-all-done.1 = bf16[128,4,512]{2,1,0:T(4,128)(2,1)} async-done(((bf16[128,4,512]{2,1,0:T(4,128)(2,1)}), bf16[128,4,512]{2,1,0:T(4,128)(2,1)}, u32[]{:S(2)}, u32[]{:S(2)}) %all-to-all-start.1) | async-done | bytes 524320 | tf_op jit(solution)/shard_map/all_to_all | solution.py:44
  84.2 2.0 reshape.244
  86.2 3.2 gather_fusion.1
  89.4 1.7 gather.19
  91.1 1.7 multiply_reduce_fusion
  92.8 0.6 multiply_negate_fusion
  93.4 0.9 neg.13
  94.3 1.1 select_select_fusion.1
  95.5 1.9 multiply_convert_fusion
  97.4 1.0 copy-done.1
  98.4 0.9 fusion.16
  99.3 0.6 fusion.13
  99.9 4.0 %fusion = f32[768,2048]{1,0:T(8,128)} fusion(bf16[256,512]{1,0:T(8,128)(2,1)S(1)} %select_select_fusion.1, bf16[256,256]{1,0:T(8,128)(2,1)S(1)} %copy-done.7, f32[256,2048]{1,0:T(8,128)S(1)} %get-tuple-element.48, f32[2048]{0:T(1024)S(1)} %copy-done.8, f32[256]{0:T(256)S(1)} %broadcast_multiply_fusion), kind=kOutput, calls=%fused_computation.8 | convolution fusion | flops 811335680 | bytes 8791040 | tf_op jit(solution)/shard_map/dot_general | solution.py:75
  104.0 0.0 all-reduce.7.cloned.1.call-update
  104.0 0.1 reshape.246
  104.1 0.7 copy.54
  104.7 1.7 fusion.17
  106.5 2.4 fusion.14
  108.9 16.3 %all-reduce.3 = (f32[2048]{0:T(1024)S(1)}, f32[2048]{0:T(1024)S(1)}, f32[1]{0:T(128)}) all-reduce(f32[2048]{0:T(1024)S(1)} %fusion.14, f32[2048]{0:T(1024)S(1)} %bitcast.35, f32[1]{0:T(128)} %bitcast.16), channel_id=1, replica_groups=mesh['tm_0'=4,'tm_1'=4,'tm_2'=8,'dp'=2] {'tm_0'}, use_global_device_ids=true, to_apply=%region_7.8 | all-reduce | flops 4097 | bytes 32776 | tf_op jit(solution)/shard_map/psum | solution.py:16
  125.3 17.1 %all-reduce.2 = (f32[2048]{0:T(1024)S(1)}, f32[2048]{0:T(1024)S(1)}, f32[1]{0:T(128)}) all-reduce(f32[2048]{0:T(1024)S(1)} %get-tuple-element.31, f32[2048]{0:T(1024)S(1)} %get-tuple-element.32, f32[1]{0:T(128)} %get-tuple-element.33), channel_id=1, replica_groups=mesh['tm_0'=4,'tm_1'=4,'tm_2'=8,'dp'=2] {'tm_1'}, use_global_device_ids=true, to_apply=%region_8.9 | all-reduce | flops 4097 | bytes 32776 | tf_op jit(solution)/shard_map/psum | solution.py:16
  142.3 28.6 %all-reduce.1 = (f32[2048]{0:T(1024)S(1)}, f32[2048]{0:T(1024)S(1)}, f32[1]{0:T(128)}) all-reduce(f32[2048]{0:T(1024)S(1)} %get-tuple-element.28, f32[2048]{0:T(1024)S(1)} %get-tuple-element.29, f32[1]{0:T(128)} %get-tuple-element.30), channel_id=1, replica_groups=mesh['tm_0'=4,'tm_1'=4,'tm_2'=8,'dp'=2] {'tm_2'}, use_global_device_ids=true, to_apply=%region_9.10 | all-reduce | flops 4097 | bytes 32776 | tf_op jit(solution)/shard_map/psum | solution.py:16
  171.0 4.6 %all-reduce.4 = (f32[2048]{0:T(1024)}, f32[2048]{0:T(1024)}, f32[1]{0:T(128)}) all-reduce(f32[2048]{0:T(1024)S(1)} %get-tuple-element.25, f32[2048]{0:T(1024)S(1)} %get-tuple-element.26, f32[1]{0:T(128)} %get-tuple-element.27), channel_id=1, replica_groups=mesh['tm_0'=4,'tm_1'=4,'tm_2'=8,'dp'=2] {'dp'}, use_global_device_ids=true, to_apply=%region_10.11 | all-reduce | flops 4097 | bytes 32776 | tf_op jit(solution)/shard_map/psum | solution.py:16
  175.5 200.1 %all-reduce.7.cloned.1.call-done = f32[768,2048]{1,0:T(8,128)} async-done(((f32[768,2048]{1,0:T(8,128)}), f32[768,2048]{1,0:T(8,128)}) %all-reduce.7.cloned.1.call-update) | async-done | bytes 6291472
  375.6 1.5 constant_dynamic-slice_fusion
  (40 shorter events, 0.2 us)
Async XLA Ops:
  7.2 88.3 %copy-start = (bf16[768,2048]{1,0:T(8,128)(2,1)S(1)}, bf16[768,2048]{1,0:T(8,128)(2,1)}, u32[]{:S(2)}) copy-start(bf16[768,2048]{1,0:T(8,128)(2,1)} %param.10) | copy-start | bytes 9437188
  9.1 13.6 %copy-start.9 = (s32[256]{0:T(256)}, s32[256]{0:T(256)S(1)}, u32[]{:S(2)}) copy-start(s32[256]{0:T(256)S(1)} %reshape.239) | copy-start | bytes 3076
  9.8 12.8 %copy-start.12 = (pred[256]{0:T(512)(128)(4,1)}, pred[256]{0:T(512)(128)(4,1)S(1)}, u32[]{:S(2)}) copy-start(pred[256]{0:T(512)(128)(4,1)S(1)} %broadcast_compare_fusion.4) | copy-start | bytes 772
  9.9 12.7 %copy-start.4 = (s32[64,4]{1,0:T(8,128)}, s32[64,4]{1,0:T(8,128)S(1)}, u32[]{:S(2)}) copy-start(s32[64,4]{1,0:T(8,128)S(1)} %copy.45) | copy-start | bytes 3076
  10.0 12.6 %copy-start.11 = (s32[256]{0:T(256)}, s32[256]{0:T(256)S(1)}, u32[]{:S(2)}) copy-start(s32[256]{0:T(256)S(1)} %reshape.273) | copy-start | bytes 3076
  10.3 57.4 %copy-start.10 = (s32[256]{0:T(256)}, s32[256]{0:T(256)S(1)}, u32[]{:S(2)}) copy-start(s32[256]{0:T(256)S(1)} %fusion.3) | copy-start | bytes 3076
  22.7 26.5 %all-to-all-start = ((s32[128,1,4]{2,1,0:T(1,128)}), s32[128,1,4]{2,1,0:T(1,128)S(1)}, u32[]{:S(2)}, u32[]{:S(2)}) async-start(s32[128,1,4]{2,1,0:T(1,128)} %copy.46), calls=%async_computation | async-start | bytes 131072 | tf_op jit(solution)/shard_map/all_to_all | solution.py:41
  56.2 11.3 %copy-start.5 = (s32[64,4]{1,0:T(8,128)S(1)}, s32[64,4]{1,0:T(8,128)}, u32[]{:S(2)}) copy-start(s32[64,4]{1,0:T(8,128)} %copy-done.4) | copy-start | bytes 3076
  59.5 24.7 %all-to-all-start.1 = ((bf16[128,4,512]{2,1,0:T(4,128)(2,1)}), bf16[128,4,512]{2,1,0:T(4,128)(2,1)}, u32[]{:S(2)}, u32[]{:S(2)}) async-start(bf16[128,4,512]{2,1,0:T(4,128)(2,1)} %select_select_fusion), calls=%async_computation.1 | async-start | bytes 1048576 | tf_op jit(solution)/shard_map/all_to_all | solution.py:44
  67.3 308.4 %all-reduce.7.cloned.1.call-start = ((), (), s32[]{:S(2)}) async-start(), calls=%async_computation.2 | async-start | bytes 12582912
  67.6 2.6 copy-start.6
  86.2 8.1 %copy-start.2 = (bf16[256,512]{1,0:T(8,128)(2,1)S(1)}, bf16[256,512]{1,0:T(8,128)(2,1)}, u32[]{:S(2)}) copy-start(bf16[256,512]{1,0:T(8,128)(2,1)} %gather_fusion.2) | copy-start | bytes 786436
  86.2 9.3 %copy-start.7 = (bf16[256,256]{1,0:T(8,128)(2,1)S(1)}, bf16[256,256]{1,0:T(8,128)(2,1)}, u32[]{:S(2)}) copy-start(bf16[256,256]{1,0:T(8,128)(2,1)} %reshape.238) | copy-start | bytes 393220
  95.5 2.9 copy-start.8
  97.4 1.0 copy-start.1
  97.4 2.5 copy-start.3
Sparse Core Ops, SparseCore 0:
  104.1 271.5 all-reduce.6
where the time goes:
time: 385 us; the launch traced here: 384 us
  waiting for transfers between devices  216 us (56%)
  blocking collectives  66.6 us (17%)
  local copies, waits for them, and re-layouts  39.5 us (10%)
  starting transfers between devices  23.5 us (6%)
  other arithmetic  15.3 us (4%)
  between operations  15 us (4%)
  matrix products  8.58 us (2%)
    unnamed x2, waiting for transfers between devices  200 us
    psum x4, blocking collectives, over_axes(): return functools.reduce(lax.psum, axes, shard)  66.6 us
    all_to_all x1, starting transfers between devices, body(): lax.all_to_all(requests, TM, split_axis=0, concat_axis=0, tiled=True)  15.4 us
    scatter x1, local copies, waits for them, and re-layouts, body(): jnp.full((tm_count, capacity), -1, jnp.int32).at[dest, slot]  11.1 us
    all_to_all x1, waiting for transfers between devices, body(): lax.all_to_all(requests, TM, split_axis=0, concat_axis=0, tiled=True)  10.1 us
    all_to_all x1, starting transfers between devices, body(): lax.all_to_all(picked, TM, split_axis=0, concat_axis=0, tiled=True)  7.81 us
  transfers between devices with their start and end apart: 3, of which 3 were waited for; matrix products, arithmetic and copies ran while one was open for 4% of the time, Pallas kernels for 0%

commit v1 on v0

v1 whole, which is shorter than its diff:
```python
import functools
import math

import jax
import jax.numpy as jnp
from jax import lax
from jax.experimental import pallas as pl
from jax.experimental.pallas import tpu as pltpu
from jax.sharding import Mesh
from jax.sharding import PartitionSpec as P

CAP = 4
TM = ("tm_0", "tm_1", "tm_2")
TM_DP = ("tm_0", "tm_1", "tm_2", "dp")
PLANE = ("tm_0", "tm_1")
LINE = "tm_2"
N_TM = 128
N_PLANE = 16
N_LINE = 8
ROWS = 256
STEPS = 4
S = 256
G = 512
H = 2048
LANES = 128
HALF = (S + G) // 2
SLAB = HALF // N_PLANE
CHUNK = 256
F32 = jnp.float32
BF16 = jnp.bfloat16
I32 = jnp.int32


def iota(shape, dim):
    return lax.broadcasted_iota(I32, shape, dim)


def dot(a, b, dims=(((1,), (0,)), ((), ()))):
    return lax.dot_general(a, b, dims, preferred_element_type=F32)


def flag(mask):
    return jnp.where(mask, 1.0, 0.0)


def pick_kernel(place_ref, offs_ref, table_ref, out_ref, wide_ref):
    me = place_ref[0]
    offs = offs_ref[...].reshape(N_TM, ROWS)
    peer = iota((N_TM, ROWS), 0)
    row = iota((N_TM, ROWS), 1)
    target = peer * STEPS + (row & (STEPS - 1)) + offs
    hit = ((target >> 2) == me) & (peer != me)
    earlier = flag(iota((ROWS, ROWS), 0) < iota((ROWS, ROWS), 1)).astype(BF16)
    rank = dot(flag(hit).astype(BF16), earlier)
    position = ((row - (row & (STEPS - 1))) + (target & (STEPS - 1)) + 1).astype(F32)
    table = table_ref[...]
    for c in range(CAP):
        place = jnp.sum(
            jnp.where(hit & (rank == float(c)), position, 0.0), axis=1, keepdims=True
        )
        wanted = flag(row.astype(F32) + 1.0 == place).astype(BF16)
        picked = dot(wanted, table)
        for j in range(G // LANES):
            wide_ref[pl.ds(c * (G // LANES) + j, N_TM, stride=16), :] = picked[
                :, j * LANES : (j + 1) * LANES
            ]
    out_ref[...] = wide_ref[...].astype(BF16)


def half_rows(core):
    k = iota((HALF, S + G), 0)
    eighth = k >> 3
    plane = (eighth * 171) >> 9
    within = eighth - plane * 3
    feature = (plane * N_LINE + (k & 7)) * 6 + core * 3 + within
    return flag(iota((HALF, S + G), 1) == feature).astype(BF16)


def three(x):
    high = x.astype(BF16).astype(F32)
    rest = x - high
    middle = rest.astype(BF16).astype(F32)
    return high, middle, rest - middle


def stack_rows(rows, count):
    width = rows[0].shape[1]
    at = iota((count, width), 0)
    total = jnp.zeros((count, width), F32)
    for n, r in enumerate(rows):
        total = jnp.where(at == n, jnp.broadcast_to(r, (count, width)), total)
    return total


def main_kernel(
    scale,
    place_ref,
    b_out_ref,
    offs_ref,
    fetched_ref,
    table_ref,
    state_ref,
    w_in_ref,
    b_in_ref,
    w_out_ref,
    td_ref,
    send_ref,
    keep_ref,
    slope_ref,
    hidden_ref,
    inputs_ref,
):
    me = place_ref[0]
    core = place_ref[1]
    row = iota((ROWS, ROWS), 1)
    col = iota((ROWS, ROWS), 0)
    offs = offs_ref[...]
    lane = iota((1, ROWS), 1)
    target = me * STEPS + (lane & (STEPS - 1)) + offs
    owner_lane = (target >> 2).astype(F32)
    position_lane = ((lane - (lane & (STEPS - 1))) + (target & (STEPS - 1))).astype(F32)

    def to_column(x):
        return jnp.sum(
            jnp.where(row == col, jnp.broadcast_to(x, (ROWS, ROWS)), 0.0),
            axis=1,
            keepdims=True,
        )

    owner = to_column(owner_lane)
    position = to_column(position_lane)
    slot = jnp.sum(flag((owner == owner_lane) & (row < col)), axis=1, keepdims=True)
    remote = owner != me.astype(F32)
    near_at = jnp.where(remote, -1.0, position)
    far_at = jnp.where(remote, owner * 16.0 + slot * 4.0, -100.0).astype(I32)
    near = flag(row.astype(F32) == near_at).astype(BF16)
    spot = iota((ROWS, N_TM * 16), 1)
    inputs_ref[:, :S] = state_ref[...]
    fetched = fetched_ref[...]
    gap = jnp.zeros((ROWS, LANES), F32)
    for j in range(G // LANES):
        far = flag(spot == far_at + j).astype(BF16)
        part = table_ref[:, j * LANES : (j + 1) * LANES]
        goal = dot(far, fetched) + dot(near, part)
        diff = part.astype(F32) - goal
        gap = gap + diff * diff
        inputs_ref[:, S + j * LANES : S + (j + 1) * LANES] = goal.astype(BF16)
    reward = -(jnp.sum(gap, axis=1, keepdims=True) * (1.0 / G))
    inputs = inputs_ref[...]

    def forward(n, total):
        at = pl.ds(pl.multiple_of(n * CHUNK, CHUNK), CHUNK)
        pre = dot(inputs, w_in_ref[:, at]) + b_in_ref[:, at]
        sig = 1.0 / (1.0 + jnp.exp(-pre))
        head = w_out_ref[:, at]
        hidden = (pre * sig).astype(BF16)
        hidden_ref[:, at] = hidden
        slope_ref[:, at] = head * (sig * (1.0 + pre * (1.0 - sig)))
        term = hidden.astype(F32) * head
        return total + term[:, :LANES] + term[:, LANES:]

    total = lax.fori_loop(0, H // CHUNK, forward, jnp.zeros((ROWS, LANES), F32))
    value = jnp.sum(total, axis=1, keepdims=True) + b_out_ref[0]
    error = value - reward
    grad_value = error * scale

    error_lane = jnp.sum(jnp.where(row == col, error, 0.0), axis=0, keepdims=True)
    td = jnp.zeros((ROWS // STEPS, STEPS), F32)
    for s in range(STEPS):
        mine = iota((ROWS // STEPS, ROWS), 1) == iota((ROWS // STEPS, ROWS), 0) * STEPS + s
        column = jnp.sum(jnp.where(mine, error_lane, 0.0), axis=1, keepdims=True)
        td = jnp.where(iota((ROWS // STEPS, STEPS), 1) == s, column, td)
    td_ref[...] = td

    kept = dot(half_rows(core), inputs, (((1,), (1,)), ((), ())))
    keep_ref[...] = kept.astype(BF16)
    sent = dot(half_rows(1 - core), inputs, (((1,), (1,)), ((), ()))).astype(BF16)
    for b in range(H // ROWS):
        send_ref[ROWS : ROWS + 48, b * ROWS : (b + 1) * ROWS] = sent[b * 48 : (b + 1) * 48, :]

    total_value = jnp.sum(grad_value, axis=0, keepdims=True)

    def backward(n, carry):
        at = pl.ds(pl.multiple_of(n * CHUNK, CHUNK), CHUNK)
        grad_pre = grad_value * slope_ref[:, at]
        send_ref[:ROWS, at] = grad_pre.astype(BF16)
        first = jnp.sum(grad_pre, axis=0, keepdims=True)
        second = jnp.sum(grad_value * hidden_ref[:, at].astype(F32), axis=0, keepdims=True)
        third = jnp.broadcast_to(total_value, (1, CHUNK))
        rows = stack_rows(three(first) + three(second) + three(third), 16)
        send_ref[ROWS + 48 : ROWS + 64, at] = rows.astype(BF16)
        return carry

    lax.fori_loop(0, H // CHUNK, backward, 0)


def product_kernel(own_ref, other_ref, keep_ref, out_ref, left_ref):
    for b in range(H // ROWS):
        left_ref[b * 48 : (b + 1) * 48, :] = other_ref[
            ROWS : ROWS + 48, b * ROWS : (b + 1) * ROWS
        ]

    def step(n, carry):
        at = pl.ds(pl.multiple_of(n * CHUNK, CHUNK), CHUNK)
        part = dot(keep_ref[...], own_ref[:ROWS, at]) + dot(left_ref[...], other_ref[:ROWS, at])
        mine = own_ref[ROWS + 48 : ROWS + 64, at].astype(F32)
        theirs = other_ref[ROWS + 48 : ROWS + 64, at].astype(F32)
        sums = []
        for q in range(3):
            a = mine[3 * q : 3 * q + 1] + mine[3 * q + 1 : 3 * q + 2] + mine[3 * q + 2 : 3 * q + 3]
            b = theirs[3 * q : 3 * q + 1] + theirs[3 * q + 1 : 3 * q + 2] + theirs[3 * q + 2 : 3 * q + 3]
            sums.append(three(a + b))
        lane = iota((1, CHUNK), 1)
        last = jnp.where(lane == 0, sums[2][0], jnp.where(lane == 1, sums[2][1], sums[2][2]))
        small = stack_rows(sums[0] + sums[1] + (last,), 8)
        for p in range(N_PLANE):
            slab = jnp.concatenate([part[p * SLAB : (p + 1) * SLAB], small], axis=0)
            out_ref[p * 32 : (p + 1) * 32, at] = slab.astype(BF16)
        return carry

    lax.fori_loop(0, H // CHUNK, step, 0)


BLOCK = 88


def plane_kernel(got_ref, out_ref, sum_ref):
    def step(n, carry):
        at = pl.ds(pl.multiple_of(n * CHUNK, CHUNK), CHUNK)
        total = got_ref[0:32, at].astype(F32)
        for p in range(1, N_PLANE):
            total = total + got_ref[p * 32 : (p + 1) * 32, at].astype(F32)
        sum_ref[:, at] = total
        return carry

    lax.fori_loop(0, H // CHUNK, step, 0)
    for b in range(H // LANES):
        at = slice(b * LANES, (b + 1) * LANES)
        for i in range(3):
            out_ref[pl.ds(i * 16 + b, N_LINE, stride=BLOCK), :] = sum_ref[8 * i : 8 * i + 8, at]
        tail = sum_ref[24:32, at]
        for q in range(2):
            joined = tail[3 * q : 3 * q + 1] + tail[3 * q + 1 : 3 * q + 2] + tail[3 * q + 2 : 3 * q + 3]
            out_ref[pl.ds(48 + q * 16 + b, N_LINE, stride=BLOCK), :] = jnp.broadcast_to(
                joined, (N_LINE, LANES)
            )
    last = sum_ref[30:31, 0:LANES]
    lane = iota((1, LANES), 1)
    whole = jnp.sum(jnp.where(lane < 3, last, 0.0), axis=1, keepdims=True)
    for n in range(80, BLOCK):
        out_ref[pl.ds(n, N_LINE, stride=BLOCK), :] = jnp.broadcast_to(whole, (N_LINE, LANES))


def line_kernel(got_ref, w_ref, b_in_ref, w_out_ref, b_out_ref, sum_ref):
    total = got_ref[0:BLOCK, :]
    for z in range(1, N_LINE):
        total = total + got_ref[z * BLOCK : (z + 1) * BLOCK, :]
    sum_ref[...] = total
    for i in range(3):
        for b in range(H // LANES):
            w_ref[i : i + 1, b * LANES : (b + 1) * LANES] = sum_ref[i * 16 + b : i * 16 + b + 1, :]
    b_in_ref[...] = sum_ref[48:64, :]
    w_out_ref[...] = sum_ref[64:80, :]
    b_out_ref[...] = sum_ref[80:81, :]


def call(kernel, shapes, operands, scratch, flops, in_smem=0):
    specs = [pl.BlockSpec(memory_space=pltpu.SMEM)] * in_smem
    specs += [pl.BlockSpec(memory_space=pltpu.VMEM)] * (len(operands) - in_smem)
    outs = [jax.ShapeDtypeStruct(shape, kind) for shape, kind in shapes]
    return pl.pallas_call(
        kernel,
        out_shape=outs,
        in_specs=specs,
        out_specs=[pl.BlockSpec(memory_space=pltpu.VMEM)] * len(outs),
        scratch_shapes=scratch,
        cost_estimate=pl.CostEstimate(flops=flops, bytes_accessed=1 << 20, transcendentals=0),
    )(*operands)


def body(state_feats, achieved, offsets, w_in, b_in, w_out, b_out):
    place = jnp.stack([lax.axis_index(TM), lax.axis_index("dp")]).astype(I32)
    table = achieved.reshape(ROWS, G)
    state = state_feats.reshape(ROWS, S)
    offs = offsets.reshape(1, ROWS)
    known = lax.all_to_all(
        jnp.broadcast_to(offs[None], (N_TM, 1, ROWS)), TM, split_axis=0, concat_axis=0, tiled=True
    )
    (picked,) = call(
        pick_kernel,
        [((N_TM * 16, LANES), BF16)],
        (place, known, table),
        [pltpu.VMEM((N_TM * 16, LANES), F32)],
        10**8,
        1,
    )
    fetched = lax.all_to_all(
        picked.reshape(N_TM, 16, LANES), TM, split_axis=0, concat_axis=0, tiled=True
    ).reshape(N_TM * 16, LANES)
    scale = 1.0 / math.sqrt(ROWS * N_TM * 2)
    td, send, keep = call(
        functools.partial(main_kernel, scale),
        [((ROWS // STEPS, STEPS), F32), ((ROWS + 64, H), BF16), ((HALF, ROWS), BF16)],
        (place, b_out, offs, fetched, table, state, w_in, b_in.reshape(1, H), w_out.reshape(1, H)),
        [pltpu.VMEM((ROWS, H), F32), pltpu.VMEM((ROWS, H), BF16), pltpu.VMEM((ROWS, S + G), BF16)],
        2 * 10**9,
        2,
    )
    other = lax.ppermute(send, "dp", [(0, 1), (1, 0)])
    (slabs,) = call(
        product_kernel,
        [((N_PLANE * 32, H), BF16)],
        (send, other, keep),
        [pltpu.VMEM((HALF, ROWS), BF16)],
        10**9,
    )
    got = lax.all_to_all(
        slabs.reshape(N_PLANE, 32, H), PLANE, split_axis=0, concat_axis=0, tiled=True
    ).reshape(N_PLANE * 32, H)
    (lines,) = call(
        plane_kernel,
        [((N_LINE * BLOCK, LANES), F32)],
        (got,),
        [pltpu.VMEM((32, H), F32)],
        10**7,
    )
    got = lax.all_to_all(
        lines.reshape(N_LINE, BLOCK, LANES), LINE, split_axis=0, concat_axis=0, tiled=True
    ).reshape(N_LINE * BLOCK, LANES)
    grad_w_in, grad_b_in, grad_w_out, grad_b_out = call(
        line_kernel,
        [((3, H), F32), ((16, LANES), F32), ((16, LANES), F32), ((1, LANES), F32)],
        (got,),
        [pltpu.VMEM((BLOCK, LANES), F32)],
        10**6,
    )
    return td, grad_w_in, grad_b_in.reshape(H), grad_w_out.reshape(H), grad_b_out[0, :1]


def solution(mesh):
    split = Mesh(mesh.devices.reshape(4, 4, 8, mesh.shape["dp"]), TM_DP)
    placed = (P("dp", TM, None), P("dp", TM, None), P("dp", TM), P(), P(), P(), P())
    return jax.shard_map(
        body,
        mesh=split,
        in_specs=placed,
        out_specs=(P("dp", TM), P(TM_DP, None), P(), P(), P()),
        check_vma=False,
    )
```

time: 385 us -> 135 us (0.35)
  waiting for transfers between devices: 216 us -> 40.5 us
  blocking collectives: 66.6 us -> 35.3 us
  local copies, waits for them, and re-layouts: 39.5 us -> 8.63 us
  Pallas kernels: 0 us -> 21.8 us
  other arithmetic: 15.3 us -> 0.58 us
  between operations: 15 us -> 1.35 us
  matrix products: 8.58 us -> 0 us
    unnamed x2 -> x0, waiting for transfers between devices: 200 us -> none
    psum x4 -> x0, blocking collectives: 66.6 us -> none  [over_axes(): return functools.reduce(lax.psum, axes, shard)]
    all_to_all x0 -> x1, blocking collectives: none -> 35.3 us  [body(): lax.all_to_all(slabs.reshape(N_PLANE, 32, H), PLANE, split_axis=0, concat...]
    all_to_all x2 -> x3, waiting for transfers between devices: 15.4 us -> 37.2 us  [the longest x1 15.5 us: body(): lax.all_to_all(picked.reshape(N_TM, 16, LANES), TM, split_axis=0, concat_...]
    pallas_call x0 -> x5, Pallas kernels: none -> 21.8 us  [call(): pl.pallas_call(kernel, out_shape=outs, in_specs=specs, out_specs=[pl.Bloc...]
    gather x6 -> x0, local copies, waits for them, and re-layouts: 13.1 us -> none  [the longest x2 4.91 us: body(): jnp.take(fetched, jnp.clip(owner * capacity + slot, 0, tm_count * capacit...]
    scatter x1 -> x0, local copies, waits for them, and re-layouts: 11.1 us -> none  [body(): jnp.full((tm_count, capacity), -1, jnp.int32).at[dest, slot]]
    dot_general x4 -> x0, matrix products: 8.58 us -> none  [the longest x1 4.01 us: body(): lax.dot_general(inputs, grad_low, (((0,), (0,)), ((), ())), preferred_ele...]
  transfers between devices with their start and end apart: 3 -> 4, of which waited for: 3 -> 4; matrix products, arithmetic and copies ran while one was open for 4% -> 3% of each run, Pallas kernels for 0% -> 0%
where the time goes in v1:
time: 135 us; the launch traced here: 134 us
  waiting for transfers between devices  40.5 us (30%)
  blocking collectives  35.3 us (26%)
  starting transfers between devices  25.9 us (19%)
  Pallas kernels  21.8 us (16%)
  local copies, waits for them, and re-layouts  8.63 us (6%)
  between operations  1.35 us (1%)
    all_to_all x1, blocking collectives, body(): lax.all_to_all(slabs.reshape(N_PLANE, 32, H), PLANE, split_axis=0, concat...  35.3 us
    pallas_call x5, Pallas kernels, call(): pl.pallas_call(kernel, out_shape=outs, in_specs=specs, out_specs=[pl.Bloc...  21.8 us
    all_to_all x1, waiting for transfers between devices, body(): lax.all_to_all(picked.reshape(N_TM, 16, LANES), TM, split_axis=0, concat_...  15.5 us
    all_to_all x1, starting transfers between devices, body(): lax.all_to_all(jnp.broadcast_to(offs[None], (N_TM, 1, ROWS)), TM, split_a...  15.4 us
    all_to_all x1, waiting for transfers between devices, body(): lax.all_to_all(lines.reshape(N_LINE, BLOCK, LANES), LINE, split_axis=0, c...  12.7 us
    all_to_all x1, waiting for transfers between devices, body(): lax.all_to_all(jnp.broadcast_to(offs[None], (N_TM, 1, ROWS)), TM, split_a...  9.03 us
    all_to_all x1, starting transfers between devices, body(): lax.all_to_all(picked.reshape(N_TM, 16, LANES), TM, split_axis=0, concat_...  7.01 us
    unnamed x14, local copies, waits for them, and re-layouts  4.71 us
  transfers between devices with their start and end apart: 4, of which 4 were waited for; matrix products, arithmetic and copies ran while one was open for 3% of the time, Pallas kernels for 0%

profile of v1, /device:TPU:2, one launch (start us, length us, event | category | flops | bytes accessed | tf_op | source)
XLA Modules:
  0.0 134.0 jit_solution(14297800741743752058)
XLA Ops:
  0.6 0.0 copy-start.4
  0.6 0.8 copy.14
  1.4 0.1 broadcast_in_dim.7
  1.6 0.7 broadcast_in_dim.8
  2.3 15.4 %all-to-all-start = ((s32[128,1,256]{2,1,0:T(1,128)}), s32[128,1,256]{2,1,0:T(1,128)S(1)}, u32[]{:S(2)}, u32[]{:S(2)}) async-start(s32[128,1,256]{2,1,0:T(1,128)} %broadcast_in_dim.8), calls=%async_computation | async-start | bytes 262144 | tf_op jit(solution)/shard_map/all_to_all | solution.py:286
  17.7 1.7 %reshape.53.table_ref = bf16[256,512]{1,0:T(8,128)(2,1)} reshape(bf16[64,4,512]{2,1,0:T(4,128)(2,1)} %param.8) | data formatting | bytes 524288 | tf_op jit(solution)/shard_map/reshape | solution.py:283
  19.5 0.6 pad_add_fusion.place_ref
  20.0 9.0 %all-to-all-done.offs_ref = s32[128,1,256]{2,1,0:T(1,128)S(1)} async-done(((s32[128,1,256]{2,1,0:T(1,128)}), s32[128,1,256]{2,1,0:T(1,128)S(1)}, u32[]{:S(2)}, u32[]{:S(2)}) %all-to-all-start) | async-done | bytes 131104 | tf_op jit(solution)/shard_map/all_to_all | solution.py:286
  29.1 0.0 copy-start.2
  29.1 0.6 copy-done.2
  29.7 2.6 %shard_map.110 = bf16[2048,128]{1,0:T(8,128)(2,1)} custom-call(s32[2]{0:T(128)} %pad_add_fusion.place_ref, s32[128,1,256]{2,1,0:T(1,128)} %copy-done.2, bf16[256,512]{1,0:T(8,128)(2,1)} %reshape.53.table_ref), custom_call_target="tpu_custom_call" | custom-call | flops 100000000 | bytes 1048576 | tf_op jit(solution)/shard_map/pallas_call | solution.py:271
  32.3 7.0 %all-to-all-start.1 = ((bf16[128,16,128]{2,1,0:T(8,128)(2,1)}), bf16[128,16,128]{2,1,0:T(8,128)(2,1)S(1)}, u32[]{:S(2)}, u32[]{:S(2)}) async-start(bf16[128,16,128]{2,1,0:T(8,128)(2,1)} %bitcast.16), calls=%async_computation.1 | async-start | bytes 1048576 | tf_op jit(solution)/shard_map/all_to_all | solution.py:297
  39.3 0.7 reshape.52.offs_ref
  40.6 0.0 copy-done.4
  40.7 0.7 reshape.56.state_ref
  41.3 15.5 %all-to-all-done.1 = bf16[128,16,128]{2,1,0:T(8,128)(2,1)S(1)} async-done(((bf16[128,16,128]{2,1,0:T(8,128)(2,1)}), bf16[128,16,128]{2,1,0:T(8,128)(2,1)S(1)}, u32[]{:S(2)}, u32[]{:S(2)}) %all-to-all-start.1) | async-done | bytes 524320 | tf_op jit(solution)/shard_map/all_to_all | solution.py:297
  56.9 0.0 copy-start.3
  56.9 0.8 copy-done.3
  57.7 9.5 %shard_map.111 = (f32[64,4]{1,0:T(8,128)}, bf16[320,2048]{1,0:T(8,128)(2,1)}, bf16[384,256]{1,0:T(8,128)(2,1)}) custom-call(s32[2]{0:T(128)} %pad_add_fusion.place_ref, f32[1]{0:T(128)S(6)} %copy.17.b_out_ref, s32[1,256]{1,0:T(1,128)} %reshape.52.offs_ref, bf16[2048,128]{1,0:T(8,128)(2,1)} %bitcast.19, bf16[256,512]{1,0:T(8,128)(2,1)} %reshape.53.table_ref, ...), custom_call_target="tpu_custom_call" | custom-call | flops 2000000000 | bytes 1048576 | tf_op jit(solution)/shard_map/pallas_call | solution.py:271
  67.1 0.0 collective-permute-start
  67.1 3.2 %collective-permute-done.other_ref = bf16[320,2048]{1,0:T(8,128)(2,1)S(1)} collective-permute-done((bf16[320,2048]{1,0:T(8,128)(2,1)}, bf16[320,2048]{1,0:T(8,128)(2,1)S(1)}, u32[]{:S(2)}, u32[]{:S(2)}) %collective-permute-start) | collective-permute-done | bytes 1310752 | tf_op jit(solution)/shard_map/ppermute | solution.py:309
  70.4 0.0 copy-start.1
  70.4 1.1 copy-done.1
  71.5 5.3 %shard_map.112 = bf16[512,2048]{1,0:T(8,128)(2,1)} custom-call(bf16[320,2048]{1,0:T(8,128)(2,1)} %get-tuple-element.13.own_ref, bf16[320,2048]{1,0:T(8,128)(2,1)} %copy-done.1, bf16[384,256]{1,0:T(8,128)(2,1)} %get-tuple-element.14.keep_ref), custom_call_target="tpu_custom_call" | custom-call | flops 1000000000 | bytes 1048576 | tf_op jit(solution)/shard_map/pallas_call | solution.py:271
  76.8 35.3 %all_to_all.20 = bf16[16,32,2048]{2,1,0:T(8,128)(2,1)} all-to-all(bf16[16,32,2048]{2,1,0:T(8,128)(2,1)} %bitcast.14), channel_id=1, replica_groups=mesh['tm_0'=4,'tm_1'=4,'tm_2'=8,'dp'=2] {'tm_0','tm_1'}, dimensions={0} | all-to-all | bytes 4194304 | tf_op jit(solution)/shard_map/all_to_all | solution.py:317
  112.0 0.0 copy-start.5
  112.0 2.8 %shard_map.113 = f32[704,128]{1,0:T(8,128)} custom-call(bf16[512,2048]{1,0:T(8,128)(2,1)} %bitcast.15), custom_call_target="tpu_custom_call" | custom-call | flops 10000000 | bytes 1048576 | tf_op jit(solution)/shard_map/pallas_call | solution.py:271
  114.8 3.4 %all-to-all-start.3 = ((f32[8,88,128]{2,1,0:T(8,128)}), f32[8,88,128]{2,1,0:T(8,128)S(1)}, u32[]{:S(2)}, u32[]{:S(2)}) async-start(f32[8,88,128]{2,1,0:T(8,128)} %bitcast.17), calls=%async_computation.3 | async-start | bytes 720896 | tf_op jit(solution)/shard_map/all_to_all | solution.py:327
  118.3 0.0 copy-done.5
  118.3 0.7 copy.16
  118.9 12.7 %all-to-all-done.3 = f32[8,88,128]{2,1,0:T(8,128)S(1)} async-done(((f32[8,88,128]{2,1,0:T(8,128)}), f32[8,88,128]{2,1,0:T(8,128)S(1)}, u32[]{:S(2)}, u32[]{:S(2)}) %all-to-all-start.3) | async-done | bytes 360480 | tf_op jit(solution)/shard_map/all_to_all | solution.py:327
  131.6 0.0 copy-start
  131.6 0.7 copy-done
  132.3 1.6 %shard_map.114 = (f32[3,2048]{1,0:T(4,128)}, f32[16,128]{1,0:T(8,128)}, f32[16,128]{1,0:T(8,128)}, f32[1,128]{1,0:T(1,128)}) custom-call(f32[704,128]{1,0:T(8,128)} %bitcast.18), custom_call_target="tpu_custom_call" | custom-call | flops 1000000 | bytes 1048576 | tf_op jit(solution)/shard_map/pallas_call | solution.py:271
Async XLA Ops:
  0.6 40.0 %copy-start.4 = (bf16[64,4,256]{2,1,0:T(4,128)(2,1)S(1)}, bf16[64,4,256]{2,1,0:T(4,128)(2,1)}, u32[]{:S(2)}) copy-start(bf16[64,4,256]{2,1,0:T(4,128)(2,1)} %param.7) | copy-start | bytes 393220
  2.3 26.8 %all-to-all-start = ((s32[128,1,256]{2,1,0:T(1,128)}), s32[128,1,256]{2,1,0:T(1,128)S(1)}, u32[]{:S(2)}, u32[]{:S(2)}) async-start(s32[128,1,256]{2,1,0:T(1,128)} %broadcast_in_dim.8), calls=%async_computation | async-start | bytes 262144 | tf_op jit(solution)/shard_map/all_to_all | solution.py:286
  29.1 0.6 copy-start.2
  32.3 24.6 %all-to-all-start.1 = ((bf16[128,16,128]{2,1,0:T(8,128)(2,1)}), bf16[128,16,128]{2,1,0:T(8,128)(2,1)S(1)}, u32[]{:S(2)}, u32[]{:S(2)}) async-start(bf16[128,16,128]{2,1,0:T(8,128)(2,1)} %bitcast.16), calls=%async_computation.1 | async-start | bytes 1048576 | tf_op jit(solution)/shard_map/all_to_all | solution.py:297
  56.9 0.8 copy-start.3
  67.1 3.2 %collective-permute-start = (bf16[320,2048]{1,0:T(8,128)(2,1)}, bf16[320,2048]{1,0:T(8,128)(2,1)S(1)}, u32[]{:S(2)}, u32[]{:S(2)}) collective-permute-start(bf16[320,2048]{1,0:T(8,128)(2,1)} %get-tuple-element.13.own_ref), channel_id=1, source_target_pairs={{0,1},{1,0},{2,3},{3,2},{4,5},{5,4},{6,7},{7,6},{8,9},{9,8},{10,11... | collective-permute-start | bytes 3932168 | tf_op jit(solution)/shard_map/ppermute | solution.py:309
  70.4 1.1 copy-start.1
  112.0 6.3 %copy-start.5 = (f32[64,4]{1,0:T(8,128)S(1)}, f32[64,4]{1,0:T(8,128)}, u32[]{:S(2)}) copy-start(f32[64,4]{1,0:T(8,128)} %get-tuple-element.24) | copy-start | bytes 3076
  114.8 16.8 %all-to-all-start.3 = ((f32[8,88,128]{2,1,0:T(8,128)}), f32[8,88,128]{2,1,0:T(8,128)S(1)}, u32[]{:S(2)}, u32[]{:S(2)}) async-start(f32[8,88,128]{2,1,0:T(8,128)} %bitcast.17), calls=%async_computation.3 | async-start | bytes 720896 | tf_op jit(solution)/shard_map/all_to_all | solution.py:327
  131.6 0.7 copy-start

commit v2 on v1

--- a/solution.py
+++ b/solution.py
@@ -264,7 +264,7 @@
     b_out_ref[...] = sum_ref[80:81, :]
 
 
-def call(kernel, shapes, operands, scratch, flops, in_smem=0):
+def call(kernel, shapes, operands, scratch, flops, grant, in_smem=0):
     specs = [pl.BlockSpec(memory_space=pltpu.SMEM)] * in_smem
     specs += [pl.BlockSpec(memory_space=pltpu.VMEM)] * (len(operands) - in_smem)
     outs = [jax.ShapeDtypeStruct(shape, kind) for shape, kind in shapes]
@@ -274,6 +274,7 @@
         in_specs=specs,
         out_specs=[pl.BlockSpec(memory_space=pltpu.VMEM)] * len(outs),
         scratch_shapes=scratch,
+        compiler_params=pltpu.CompilerParams(vmem_limit_bytes=grant << 20),
         cost_estimate=pl.CostEstimate(flops=flops, bytes_accessed=1 << 20, transcendentals=0),
     )(*operands)
 
@@ -292,6 +293,7 @@
         (place, known, table),
         [pltpu.VMEM((N_TM * 16, LANES), F32)],
         10**8,
+        6,
         1,
     )
     fetched = lax.all_to_all(
@@ -304,6 +306,7 @@
         (place, b_out, offs, fetched, table, state, w_in, b_in.reshape(1, H), w_out.reshape(1, H)),
         [pltpu.VMEM((ROWS, H), F32), pltpu.VMEM((ROWS, H), BF16), pltpu.VMEM((ROWS, S + G), BF16)],
         2 * 10**9,
+        18,
         2,
     )
     other = lax.ppermute(send, "dp", [(0, 1), (1, 0)])
@@ -313,6 +316,7 @@
         (send, other, keep),
         [pltpu.VMEM((HALF, ROWS), BF16)],
         10**9,
+        12,
     )
     got = lax.all_to_all(
         slabs.reshape(N_PLANE, 32, H), PLANE, split_axis=0, concat_axis=0, tiled=True
@@ -323,6 +327,7 @@
         (got,),
         [pltpu.VMEM((32, H), F32)],
         10**7,
+        6,
     )
     got = lax.all_to_all(
         lines.reshape(N_LINE, BLOCK, LANES), LINE, split_axis=0, concat_axis=0, tiled=True
@@ -333,6 +338,7 @@
         (got,),
         [pltpu.VMEM((BLOCK, LANES), F32)],
         10**6,
+        4,
     )
     return td, grad_w_in, grad_b_in.reshape(H), grad_w_out.reshape(H), grad_b_out[0, :1]
 

time: 135 us -> 122 us (0.904)
  Pallas kernels: 21.8 us -> 12.9 us
  local copies, waits for them, and re-layouts: 8.63 us -> 5.38 us
  waiting for transfers between devices: 40.5 us -> 42.7 us
  blocking collectives: 35.3 us -> 33.5 us
    pallas_call x5, Pallas kernels: 21.8 us -> 12.9 us  [call(): pl.pallas_call(kernel, out_shape=outs, in_specs=specs, out_specs=[pl.Bloc...]
    all_to_all x1, blocking collectives: 35.3 us -> 33.5 us  [body(): lax.all_to_all(slabs.reshape(N_PLANE, 32, H), PLANE, split_axis=0, concat...]
    unnamed x14 -> x10, local copies, waits for them, and re-layouts: 4.71 us -> 3.39 us
  transfers between devices with their start and end apart: 4 -> 4, of which waited for: 4 -> 4; matrix products, arithmetic and copies ran while one was open for 3% -> 2% of each run, Pallas kernels for 0% -> 0%
where the time goes in v2:
time: 122 us
  waiting for transfers between devices  42.7 us (35%)
  blocking collectives  33.5 us (27%)
  starting transfers between devices  26 us (21%)
  Pallas kernels  12.9 us (11%)
  local copies, waits for them, and re-layouts  5.38 us (4%)
  between operations  1.41 us (1%)
    all_to_all x1, blocking collectives, body(): lax.all_to_all(slabs.reshape(N_PLANE, 32, H), PLANE, split_axis=0, concat...  33.5 us
    all_to_all x1, waiting for transfers between devices, body(): lax.all_to_all(picked.reshape(N_TM, 16, LANES), TM, split_axis=0, concat_...  16.8 us
    all_to_all x1, starting transfers between devices, body(): lax.all_to_all(jnp.broadcast_to(offs[None], (N_TM, 1, ROWS)), TM, split_a...  15.4 us
    pallas_call x5, Pallas kernels, call(): pl.pallas_call(kernel, out_shape=outs, in_specs=specs, out_specs=[pl.Bloc...  12.9 us
    all_to_all x1, waiting for transfers between devices, body(): lax.all_to_all(lines.reshape(N_LINE, BLOCK, LANES), LINE, split_axis=0, c...  12.7 us
    all_to_all x1, waiting for transfers between devices, body(): lax.all_to_all(jnp.broadcast_to(offs[None], (N_TM, 1, ROWS)), TM, split_a...  10.2 us
    all_to_all x1, starting transfers between devices, body(): lax.all_to_all(picked.reshape(N_TM, 16, LANES), TM, split_axis=0, concat_...  7 us
    all_to_all x1, starting transfers between devices, body(): lax.all_to_all(lines.reshape(N_LINE, BLOCK, LANES), LINE, split_axis=0, c...  3.44 us
  transfers between devices with their start and end apart: 4, of which 4 were waited for; matrix products, arithmetic and copies ran while one was open for 2% of the time, Pallas kernels for 0%

profile of v2, /device:TPU:2, one launch (start us, length us, event | category | flops | bytes accessed | tf_op | source)
XLA Modules:
  0.0 121.9 jit_solution(10646449770603472879)
XLA Ops:
  0.6 0.0 copy-start.3
  0.6 0.0 copy-start.2
  0.7 0.0 copy-start.1
  0.7 0.8 copy.14
  1.5 0.1 broadcast_in_dim.7
  1.6 0.7 broadcast_in_dim.8
  2.3 15.4 %all-to-all-start = ((s32[128,1,256]{2,1,0:T(1,128)}), s32[128,1,256]{2,1,0:T(1,128)S(1)}, u32[]{:S(2)}, u32[]{:S(2)}) async-start(s32[128,1,256]{2,1,0:T(1,128)} %broadcast_in_dim.8), calls=%async_computation | async-start | bytes 262144 | tf_op jit(solution)/shard_map/all_to_all | solution.py:287
  17.8 1.0 reshape.53.table_ref
  18.8 0.1 pad_add_fusion.place_ref
  18.9 10.2 %all-to-all-done.offs_ref = s32[128,1,256]{2,1,0:T(1,128)S(1)} async-done(((s32[128,1,256]{2,1,0:T(1,128)}), s32[128,1,256]{2,1,0:T(1,128)S(1)}, u32[]{:S(2)}, u32[]{:S(2)}) %all-to-all-start) | async-done | bytes 131104 | tf_op jit(solution)/shard_map/all_to_all | solution.py:287
  29.1 2.1 %shard_map.110 = bf16[2048,128]{1,0:T(8,128)(2,1)} custom-call(s32[2]{0:T(128)S(1)} %pad_add_fusion.place_ref, s32[128,1,256]{2,1,0:T(1,128)S(1)} %all-to-all-done.offs_ref, bf16[256,512]{1,0:T(8,128)(2,1)S(1)} %reshape.53.table_ref), custom_call_target="tpu_custom_call" | custom-call | flops 100000000 | bytes 1048576 | tf_op jit(solution)/shard_map/pallas_call | solution.py:271
  31.2 7.0 %all-to-all-start.1 = ((bf16[128,16,128]{2,1,0:T(8,128)(2,1)}), bf16[128,16,128]{2,1,0:T(8,128)(2,1)S(1)}, u32[]{:S(2)}, u32[]{:S(2)}) async-start(bf16[128,16,128]{2,1,0:T(8,128)(2,1)} %bitcast.2), calls=%async_computation.1 | async-start | bytes 1048576 | tf_op jit(solution)/shard_map/all_to_all | solution.py:299
  38.2 0.1 reshape.52.offs_ref
  39.0 0.0 copy-done.3
  39.0 16.8 %all-to-all-done.1 = bf16[128,16,128]{2,1,0:T(8,128)(2,1)S(1)} async-done(((bf16[128,16,128]{2,1,0:T(8,128)(2,1)}), bf16[128,16,128]{2,1,0:T(8,128)(2,1)S(1)}, u32[]{:S(2)}, u32[]{:S(2)}) %all-to-all-start.1) | async-done | bytes 524320 | tf_op jit(solution)/shard_map/all_to_all | solution.py:299
  55.8 0.0 copy-done.2
  55.8 0.0 copy-done.1
  55.8 0.0 copy-start
  55.8 1.9 %copy-done = bf16[768,2048]{1,0:T(8,128)(2,1)S(1)} copy-done((bf16[768,2048]{1,0:T(8,128)(2,1)S(1)}, bf16[768,2048]{1,0:T(8,128)(2,1)}, u32[]{:S(2)}) %copy-start) | copy-done | bytes 3145752
  57.7 6.7 %shard_map.111 = (f32[64,4]{1,0:T(8,128)S(1)}, bf16[320,2048]{1,0:T(8,128)(2,1)S(1)}, bf16[384,256]{1,0:T(8,128)(2,1)S(1)}) custom-call(s32[2]{0:T(128)S(1)} %pad_add_fusion.place_ref, f32[1]{0:T(128)S(6)} %copy.17.b_out_ref, s32[1,256]{1,0:T(1,128)S(1)} %reshape.52.offs_ref, bf16[2048,128]{1,0:T(8,128)(2,1)S(1)} %bitcast.17, ...), custom_call_target="tpu_custom_call" | custom-call | flops 2000000000 | bytes 1048576 | tf_op jit(solution)/shard_map/pallas_call | solution.py:271
  64.4 0.1 collective-permute-start
  64.5 3.0 %collective-permute-done.other_ref = bf16[320,2048]{1,0:T(8,128)(2,1)S(1)} collective-permute-done((bf16[320,2048]{1,0:T(8,128)(2,1)S(1)}, bf16[320,2048]{1,0:T(8,128)(2,1)S(1)}, u32[]{:S(2)}, u32[]{:S(2)}) %collective-permute-start) | collective-permute-done | bytes 1310752 | tf_op jit(solution)/shard_map/ppermute | solution.py:312
  67.5 2.2 %shard_map.112 = bf16[512,2048]{1,0:T(8,128)(2,1)S(1)} custom-call(bf16[320,2048]{1,0:T(8,128)(2,1)S(1)} %get-tuple-element.13.own_ref, bf16[320,2048]{1,0:T(8,128)(2,1)S(1)} %collective-permute-done.other_ref, bf16[384,256]{1,0:T(8,128)(2,1)S(1)} %get-tuple-element.14.keep_ref), custom_call_target="tpu_custom_call" | custom-call | flops 1000000000 | bytes 1048576 | tf_op jit(solution)/shard_map/pallas_call | solution.py:271
  69.8 33.5 %all_to_all.20 = bf16[16,32,2048]{2,1,0:T(8,128)(2,1)S(1)} all-to-all(bf16[16,32,2048]{2,1,0:T(8,128)(2,1)S(1)} %bitcast.14), channel_id=1, replica_groups=mesh['tm_0'=4,'tm_1'=4,'tm_2'=8,'dp'=2] {'tm_0','tm_1'}, dimensions={0} | all-to-all | bytes 4194304 | tf_op jit(solution)/shard_map/all_to_all | solution.py:321
  103.2 1.2 shard_map.113
  104.4 3.4 %all-to-all-start.3 = ((f32[8,88,128]{2,1,0:T(8,128)}), f32[8,88,128]{2,1,0:T(8,128)S(1)}, u32[]{:S(2)}, u32[]{:S(2)}) async-start(f32[8,88,128]{2,1,0:T(8,128)} %bitcast.8), calls=%async_computation.3 | async-start | bytes 720896 | tf_op jit(solution)/shard_map/all_to_all | solution.py:332
  107.9 0.7 copy.16
  108.5 12.7 %all-to-all-done.3 = f32[8,88,128]{2,1,0:T(8,128)S(1)} async-done(((f32[8,88,128]{2,1,0:T(8,128)}), f32[8,88,128]{2,1,0:T(8,128)S(1)}, u32[]{:S(2)}, u32[]{:S(2)}) %all-to-all-start.3) | async-done | bytes 360480 | tf_op jit(solution)/shard_map/all_to_all | solution.py:332
  121.2 0.7 shard_map.114
  (1 shorter events, 0.0 us)
Async XLA Ops:
  0.6 38.4 %copy-start.3 = (bf16[64,4,256]{2,1,0:T(4,128)(2,1)S(1)}, bf16[64,4,256]{2,1,0:T(4,128)(2,1)}, u32[]{:S(2)}) copy-start(bf16[64,4,256]{2,1,0:T(4,128)(2,1)} %param.7) | copy-start | bytes 393220
  0.6 55.2 %copy-start.2 = (f32[2048]{0:T(1024)S(1)}, f32[2048]{0:T(1024)}, u32[]{:S(2)}) copy-start(f32[2048]{0:T(1024)} %param.12) | copy-start | bytes 24580
  0.7 55.2 %copy-start.1 = (f32[2048]{0:T(1024)S(1)}, f32[2048]{0:T(1024)}, u32[]{:S(2)}) copy-start(f32[2048]{0:T(1024)} %param.11) | copy-start | bytes 24580
  2.3 26.8 %all-to-all-start = ((s32[128,1,256]{2,1,0:T(1,128)}), s32[128,1,256]{2,1,0:T(1,128)S(1)}, u32[]{:S(2)}, u32[]{:S(2)}) async-start(s32[128,1,256]{2,1,0:T(1,128)} %broadcast_in_dim.8), calls=%async_computation | async-start | bytes 262144 | tf_op jit(solution)/shard_map/all_to_all | solution.py:287
  31.2 24.6 %all-to-all-start.1 = ((bf16[128,16,128]{2,1,0:T(8,128)(2,1)}), bf16[128,16,128]{2,1,0:T(8,128)(2,1)S(1)}, u32[]{:S(2)}, u32[]{:S(2)}) async-start(bf16[128,16,128]{2,1,0:T(8,128)(2,1)} %bitcast.2), calls=%async_computation.1 | async-start | bytes 1048576 | tf_op jit(solution)/shard_map/all_to_all | solution.py:299
  55.8 1.9 %copy-start = (bf16[768,2048]{1,0:T(8,128)(2,1)S(1)}, bf16[768,2048]{1,0:T(8,128)(2,1)}, u32[]{:S(2)}) copy-start(bf16[768,2048]{1,0:T(8,128)(2,1)} %w_in_ref.1) | copy-start | bytes 9437188
  64.4 3.1 %collective-permute-start = (bf16[320,2048]{1,0:T(8,128)(2,1)S(1)}, bf16[320,2048]{1,0:T(8,128)(2,1)S(1)}, u32[]{:S(2)}, u32[]{:S(2)}) collective-permute-start(bf16[320,2048]{1,0:T(8,128)(2,1)S(1)} %get-tuple-element.13.own_ref), channel_id=1, source_target_pairs={{0,1},{1,0},{2,3},{3,2},{4,5},{5,4},{6,7},{7,6},{8,9},{9,8},{10,11... | collective-permute-start | bytes 3932168 | tf_op jit(solution)/shard_map/ppermute | solution.py:312
  104.4 16.8 %all-to-all-start.3 = ((f32[8,88,128]{2,1,0:T(8,128)}), f32[8,88,128]{2,1,0:T(8,128)S(1)}, u32[]{:S(2)}, u32[]{:S(2)}) async-start(f32[8,88,128]{2,1,0:T(8,128)} %bitcast.8), calls=%async_computation.3 | async-start | bytes 720896 | tf_op jit(solution)/shard_map/all_to_all | solution.py:332

commit v3 on v2

v3 whole, which is shorter than its diff:
```python
import functools
import math

import jax
import jax.numpy as jnp
from jax import lax
from jax.experimental import pallas as pl
from jax.experimental.pallas import tpu as pltpu
from jax.sharding import Mesh
from jax.sharding import PartitionSpec as P

CAP = 4
TM = ("tm_0", "tm_1", "tm_2")
TM_DP = ("tm_0", "tm_1", "tm_2", "dp")
PLANE = ("tm_0", "tm_1")
LINE = "tm_2"
N_TM = 128
N_PLANE = 16
N_LINE = 8
ROWS = 256
STEPS = 4
S = 256
G = 512
H = 2048
LANES = 128
HALF = (S + G) // 2
SLAB = HALF // N_PLANE
CHUNK = 256
F32 = jnp.float32
BF16 = jnp.bfloat16
I32 = jnp.int32


def iota(shape, dim):
    return lax.broadcasted_iota(I32, shape, dim)


def dot(a, b, dims=(((1,), (0,)), ((), ()))):
    return lax.dot_general(a, b, dims, preferred_element_type=F32)


def flag(mask):
    return jnp.where(mask, 1.0, 0.0)


def spread_kernel(offs_ref, many_ref, row_ref):
    offs = offs_ref[...]
    parts = jnp.concatenate([offs >> 4, offs & 15], axis=0).astype(F32).astype(BF16)
    episode = flag((iota((ROWS // STEPS, ROWS), 1) >> 2) == iota((ROWS // STEPS, ROWS), 0))
    wide = dot(parts, episode.astype(BF16))
    step = iota((2 * STEPS, ROWS), 1) & (STEPS - 1)
    which = iota((2 * STEPS, ROWS), 0)
    mine = (which & (STEPS - 1)) == step
    weight = jnp.where(which < STEPS, 16.0, 1.0)
    row = jnp.sum(jnp.where(mine, wide * weight, 0.0), axis=0, keepdims=True).astype(I32)
    row_ref[...] = row
    many_ref[...] = jnp.broadcast_to(row[None], (N_TM, 1, ROWS))


def pick_kernel(place_ref, offs_ref, table_ref, out_ref, wide_ref):
    me = place_ref[0]
    offs = offs_ref[...].reshape(N_TM, ROWS)
    peer = iota((N_TM, ROWS), 0)
    row = iota((N_TM, ROWS), 1)
    target = peer * STEPS + (row & (STEPS - 1)) + offs
    hit = ((target >> 2) == me) & (peer != me)
    earlier = flag(iota((ROWS, ROWS), 0) < iota((ROWS, ROWS), 1)).astype(BF16)
    rank = dot(flag(hit).astype(BF16), earlier)
    position = ((row - (row & (STEPS - 1))) + (target & (STEPS - 1)) + 1).astype(F32)
    table = table_ref[...]
    for c in range(CAP):
        place = jnp.sum(
            jnp.where(hit & (rank == float(c)), position, 0.0), axis=1, keepdims=True
        )
        wanted = flag(row.astype(F32) + 1.0 == place).astype(BF16)
        picked = dot(wanted, table)
        for j in range(G // LANES):
            wide_ref[pl.ds(c * (G // LANES) + j, N_TM, stride=16), :] = picked[
                :, j * LANES : (j + 1) * LANES
            ]
    out_ref[...] = wide_ref[...].astype(BF16)


def half_rows(core):
    k = iota((HALF, S + G), 0)
    eighth = k >> 3
    plane = (eighth * 171) >> 9
    within = eighth - plane * 3
    feature = (plane * N_LINE + (k & 7)) * 6 + core * 3 + within
    return flag(iota((HALF, S + G), 1) == feature).astype(BF16)


def three(x):
    high = x.astype(BF16).astype(F32)
    rest = x - high
    middle = rest.astype(BF16).astype(F32)
    return high, middle, rest - middle


def two(x):
    high = x.astype(BF16).astype(F32)
    return high, x - high


def stack_rows(rows, count):
    width = rows[0].shape[1]
    at = iota((count, width), 0)
    total = jnp.zeros((count, width), F32)
    for n, r in enumerate(rows):
        total = jnp.where(at == n, jnp.broadcast_to(r, (count, width)), total)
    return total


def ahead_kernel(
    place_ref,
    offs_ref,
    table_ref,
    state_ref,
    w_in_ref,
    b_in_ref,
    base_ref,
    near_ref,
    at_ref,
):
    me = place_ref[0]
    row = iota((ROWS, ROWS), 1)
    col = iota((ROWS, ROWS), 0)
    lane = iota((1, ROWS), 1)
    target = me * STEPS + (lane & (STEPS - 1)) + offs_ref[...]
    owner_lane = (target >> 2).astype(F32)
    position_lane = ((lane - (lane & (STEPS - 1))) + (target & (STEPS - 1))).astype(F32)

    def to_column(x):
        return jnp.sum(
            jnp.where(row == col, jnp.broadcast_to(x, (ROWS, ROWS)), 0.0),
            axis=1,
            keepdims=True,
        )

    owner = to_column(owner_lane)
    position = to_column(position_lane)
    slot = jnp.sum(flag((owner == owner_lane) & (row < col)), axis=1, keepdims=True)
    remote = owner != me.astype(F32)
    near_at = jnp.where(remote, -1.0, position)
    far_at = jnp.where(remote, owner * 16.0 + slot * 4.0, -100.0).astype(I32)
    near = flag(row.astype(F32) == near_at).astype(BF16)
    near_ref[...] = dot(near, table_ref[...]).astype(BF16)
    at_ref[...] = jnp.broadcast_to(far_at, (ROWS, LANES))
    state = state_ref[...]

    def step(n, carry):
        at = pl.ds(pl.multiple_of(n * CHUNK, CHUNK), CHUNK)
        base_ref[:, at] = dot(state, w_in_ref[:S, at]) + b_in_ref[:, at]
        return carry

    lax.fori_loop(0, H // CHUNK, step, 0)


def main_kernel(
    scale,
    place_ref,
    b_out_ref,
    fetched_ref,
    base_ref,
    near_ref,
    at_ref,
    table_ref,
    state_ref,
    w_in_ref,
    w_out_ref,
    td_ref,
    send_ref,
    keep_ref,
    slope_ref,
    hidden_ref,
    inputs_ref,
    goal_w_ref,
    sem,
):
    load = pltpu.make_async_copy(w_in_ref.at[pl.ds(S, G), :], goal_w_ref, sem)
    load.start()
    core = place_ref[1]
    far_at = at_ref[:, 0:1]
    spot = iota((ROWS, N_TM * 16), 1)
    inputs_ref[:, :S] = state_ref[...]
    fetched = fetched_ref[...]
    gap = jnp.zeros((ROWS, LANES), F32)
    for j in range(G // LANES):
        at = slice(j * LANES, (j + 1) * LANES)
        goal = dot(flag(spot == far_at + j).astype(BF16), fetched) + near_ref[:, at].astype(F32)
        diff = table_ref[:, at].astype(F32) - goal
        gap = gap + diff * diff
        inputs_ref[:, S + j * LANES : S + (j + 1) * LANES] = goal.astype(BF16)
    reward = -(jnp.sum(gap, axis=1, keepdims=True) * (1.0 / G))
    inputs = inputs_ref[...]
    load.wait()

    def forward(n, total):
        at = pl.ds(pl.multiple_of(n * CHUNK, CHUNK), CHUNK)
        pre = base_ref[:, at] + dot(inputs[:, S:], goal_w_ref[:, at])
        sig = 1.0 / (1.0 + jnp.exp(-pre))
        head = w_out_ref[:, at]
        hidden = (pre * sig).astype(BF16)
        hidden_ref[:, at] = hidden
        slope_ref[:, at] = head * (sig * (1.0 + pre * (1.0 - sig)))
        term = hidden.astype(F32) * head
        return total + term[:, :LANES] + term[:, LANES:]

    total = lax.fori_loop(0, H // CHUNK, forward, jnp.zeros((ROWS, LANES), F32))
    value = jnp.sum(total, axis=1, keepdims=True) + b_out_ref[0]
    error = value - reward
    grad_value = error * scale

    each = (STEPS * iota((ROWS, ROWS // STEPS), 1)) - iota((ROWS, ROWS // STEPS), 0)
    for s in range(STEPS):
        td_ref[s : s + 1, :] = jnp.sum(
            jnp.where(each + s == 0, error, 0.0), axis=0, keepdims=True
        )

    kept = dot(half_rows(core), inputs, (((1,), (1,)), ((), ())))
    keep_ref[...] = kept.astype(BF16)
    sent = dot(half_rows(1 - core), inputs, (((1,), (1,)), ((), ()))).astype(BF16)
    for b in range(H // ROWS):
        send_ref[ROWS : ROWS + 48, b * ROWS : (b + 1) * ROWS] = sent[b * 48 : (b + 1) * 48, :]

    total_value = jnp.sum(grad_value, axis=0, keepdims=True)

    def backward(n, carry):
        at = pl.ds(pl.multiple_of(n * CHUNK, CHUNK), CHUNK)
        grad_pre = grad_value * slope_ref[:, at]
        send_ref[:ROWS, at] = grad_pre.astype(BF16)
        first = jnp.sum(grad_pre, axis=0, keepdims=True)
        second = jnp.sum(grad_value * hidden_ref[:, at].astype(F32), axis=0, keepdims=True)
        third = jnp.broadcast_to(total_value, (1, CHUNK))
        rows = stack_rows(three(first) + three(second) + three(third), 16)
        send_ref[ROWS + 48 : ROWS + 64, at] = rows.astype(BF16)
        return carry

    lax.fori_loop(0, H // CHUNK, backward, 0)


PACK = 464
BLOCK = 88


def product_kernel(own_ref, other_ref, keep_ref, out_ref, left_ref):
    for b in range(H // ROWS):
        left_ref[b * 48 : (b + 1) * 48, :] = other_ref[
            ROWS : ROWS + 48, b * ROWS : (b + 1) * ROWS
        ]
    keep = keep_ref[...]
    left = left_ref[...]
    for n in range(H // CHUNK):
        at = slice(n * CHUNK, (n + 1) * CHUNK)
        part = dot(keep, own_ref[:ROWS, at]) + dot(left, other_ref[:ROWS, at])
        for p in range(N_PLANE):
            for i in range(3):
                tile = part[p * SLAB + 8 * i : p * SLAB + 8 * i + 8]
                pair = jnp.concatenate([tile[:, :LANES], tile[:, LANES:]], axis=0)
                start = p * PACK + (16 * i + 2 * n) * 8
                out_ref[start : start + 16, :] = pair.astype(BF16)
    mine = own_ref[ROWS + 48 : ROWS + 64, :].astype(F32)
    theirs = other_ref[ROWS + 48 : ROWS + 64, :].astype(F32)
    rows = []
    for q in range(3):
        a = mine[3 * q : 3 * q + 1] + mine[3 * q + 1 : 3 * q + 2] + mine[3 * q + 2 : 3 * q + 3]
        b = theirs[3 * q : 3 * q + 1] + theirs[3 * q + 1 : 3 * q + 2] + theirs[3 * q + 2 : 3 * q + 3]
        rows.append(two(a + b))
    blocks = []
    for q in range(2):
        for r in rows[q]:
            pieces = [r[:, b * LANES : (b + 1) * LANES] for b in range(H // LANES)]
            blocks.append(jnp.concatenate(pieces, axis=0))
    blocks.append(stack_rows([r[:, :LANES] for r in rows[2]], 16))
    small = jnp.concatenate(blocks, axis=0).astype(BF16)
    for p in range(N_PLANE):
        out_ref[p * PACK + HALF : (p + 1) * PACK, :] = small


def plane_kernel(got_ref, out_ref, sum_ref):
    for b in range(PACK // 16):
        total = got_ref[b * 16 : b * 16 + 16, :].astype(F32)
        for p in range(1, N_PLANE):
            total = total + got_ref[p * PACK + b * 16 : p * PACK + b * 16 + 16, :].astype(F32)
        sum_ref[b * 16 : b * 16 + 16, :] = total
    for n in range(48):
        out_ref[pl.ds(n, N_LINE, stride=BLOCK), :] = sum_ref[8 * n : 8 * n + 8, :]
    small = jnp.concatenate(
        [
            sum_ref[384:400, :] + sum_ref[400:416, :],
            sum_ref[416:432, :] + sum_ref[432:448, :],
            jnp.broadcast_to(sum_ref[448:449, :] + sum_ref[449:450, :], (8, LANES)),
        ],
        axis=0,
    )
    for z in range(N_LINE):
        out_ref[z * BLOCK + 48 : (z + 1) * BLOCK, :] = small


def line_kernel(got_ref, w_ref, b_in_ref, w_out_ref, b_out_ref, sum_ref):
    total = got_ref[0:BLOCK, :]
    for z in range(1, N_LINE):
        total = total + got_ref[z * BLOCK : (z + 1) * BLOCK, :]
    sum_ref[...] = total
    for i in range(3):
        for b in range(H // LANES):
            w_ref[i : i + 1, b * LANES : (b + 1) * LANES] = sum_ref[i * 16 + b : i * 16 + b + 1, :]
    b_in_ref[...] = sum_ref[48:64, :]
    w_out_ref[...] = sum_ref[64:80, :]
    b_out_ref[...] = sum_ref[80:81, :]


def call(kernel, shapes, operands, scratch, flops, grant, in_smem=0, in_hbm=()):
    specs = [pl.BlockSpec(memory_space=pltpu.SMEM)] * in_smem
    specs += [pl.BlockSpec(memory_space=pltpu.VMEM)] * (len(operands) - in_smem)
    for n in in_hbm:
        specs[n] = pl.BlockSpec(memory_space=pltpu.HBM)
    outs = [jax.ShapeDtypeStruct(shape, kind) for shape, kind in shapes]
    return pl.pallas_call(
        kernel,
        out_shape=outs,
        in_specs=specs,
        out_specs=[pl.BlockSpec(memory_space=pltpu.VMEM)] * len(outs),
        scratch_shapes=scratch,
        compiler_params=pltpu.CompilerParams(vmem_limit_bytes=grant << 20),
        cost_estimate=pl.CostEstimate(flops=flops, bytes_accessed=1 << 20, transcendentals=0),
    )(*operands)


def body(state_feats, achieved, offsets, w_in, b_in, w_out, b_out):
    place = jnp.stack([lax.axis_index(TM), lax.axis_index("dp")]).astype(I32)
    table = achieved.reshape(ROWS, G)
    state = state_feats.reshape(ROWS, S)
    many, offs = call(
        spread_kernel,
        [((N_TM, 1, ROWS), I32), ((1, ROWS), I32)],
        (offsets.T,),
        [],
        10**6,
        4,
    )
    known = lax.all_to_all(many, TM, split_axis=0, concat_axis=0, tiled=True)
    (picked,) = call(
        pick_kernel,
        [((N_TM * 16, LANES), BF16)],
        (place, known, table),
        [pltpu.VMEM((N_TM * 16, LANES), F32)],
        10**8,
        6,
        1,
    )
    base, near, at = call(
        ahead_kernel,
        [((ROWS, H), F32), ((ROWS, G), BF16), ((ROWS, LANES), I32)],
        (place, offs, table, state, w_in, b_in.reshape(1, H)),
        [],
        10**9,
        12,
        1,
    )
    fetched = lax.all_to_all(
        picked.reshape(N_TM, 16, LANES), TM, split_axis=0, concat_axis=0, tiled=True
    ).reshape(N_TM * 16, LANES)
    scale = 1.0 / math.sqrt(ROWS * N_TM * 2)
    td, send, keep = call(
        functools.partial(main_kernel, scale),
        [((STEPS, ROWS // STEPS), F32), ((ROWS + 64, H), BF16), ((HALF, ROWS), BF16)],
        (place, b_out, fetched, base, near, at, table, state, w_in, w_out.reshape(1, H)),
        [pltpu.VMEM((ROWS, H), F32), pltpu.VMEM((ROWS, H), BF16), pltpu.VMEM((ROWS, S + G), BF16), pltpu.VMEM((G, H), BF16), pltpu.SemaphoreType.DMA],
        2 * 10**9,
        48,
        2,
        (8,),
    )
    other = lax.ppermute(send, "dp", [(0, 1), (1, 0)])
    (packs,) = call(
        product_kernel,
        [((N_PLANE * PACK, LANES), BF16)],
        (send, other, keep),
        [pltpu.VMEM((HALF, ROWS), BF16)],
        10**9,
        12,
    )
    got = lax.all_to_all(
        packs.reshape(N_PLANE, PACK, LANES), PLANE, split_axis=0, concat_axis=0, tiled=True
    ).reshape(N_PLANE * PACK, LANES)
    (lines,) = call(
        plane_kernel,
        [((N_LINE * BLOCK, LANES), F32)],
        (got,),
        [pltpu.VMEM((PACK, LANES), F32)],
        10**7,
        6,
    )
    got = lax.all_to_all(
        lines.reshape(N_LINE, BLOCK, LANES), LINE, split_axis=0, concat_axis=0, tiled=True
    ).reshape(N_LINE * BLOCK, LANES)
    grad_w_in, grad_b_in, grad_w_out, grad_b_out = call(
        line_kernel,
        [((3, H), F32), ((16, LANES), F32), ((16, LANES), F32), ((1, LANES), F32)],
        (got,),
        [pltpu.VMEM((BLOCK, LANES), F32)],
        10**6,
        4,
    )
    return td.T, grad_w_in, grad_b_in.reshape(H), grad_w_out.reshape(H), grad_b_out[0, :1]


def solution(mesh):
    split = Mesh(mesh.devices.reshape(4, 4, 8, mesh.shape["dp"]), TM_DP)
    placed = (P("dp", TM, None), P("dp", TM, None), P("dp", TM), P(), P(), P(), P())
    return jax.shard_map(
        body,
        mesh=split,
        in_specs=placed,
        out_specs=(P("dp", TM), P(TM_DP, None), P(), P(), P()),
        check_vma=False,
    )
```

time: 122 us -> 115 us (0.943)
  waiting for transfers between devices: 42.7 us -> 25.9 us
  blocking collectives: 33.5 us -> 47.1 us
  starting transfers between devices: 26 us -> 22.5 us
  local copies, waits for them, and re-layouts: 5.38 us -> 3.63 us
    all_to_all x1 -> x2, blocking collectives: 33.5 us -> 47.1 us  [the longest x1 31.3 us: body(): lax.all_to_all(packs.reshape(N_PLANE, PACK, LANES), PLANE, split_axis=0,...]
    all_to_all x2 -> x1, waiting for transfers between devices: 22.9 us -> 10.2 us  [body(): known = lax.all_to_all(many, TM, split_axis=0, concat_axis=0, tiled=True)]
    all_to_all x1, waiting for transfers between devices: 16.8 us -> 12.6 us  [body(): lax.all_to_all(picked.reshape(N_TM, 16, LANES), TM, split_axis=0, concat_...]
    all_to_all x2 -> x1, starting transfers between devices: 18.9 us -> 15.4 us  [body(): known = lax.all_to_all(many, TM, split_axis=0, concat_axis=0, tiled=True)]
    pallas_call x5 -> x7, Pallas kernels: 12.9 us -> 13.9 us  [call(): pl.pallas_call(kernel, out_shape=outs, in_specs=specs, out_specs=[pl.Bloc...]
  transfers between devices with their start and end apart: 4 -> 3, of which waited for: 4 -> 3; matrix products, arithmetic and copies ran while one was open for 2% -> 1% of each run, Pallas kernels for 0% -> 2%
where the time goes in v3:
time: 115 us; the launch traced here: 114 us
  blocking collectives  47.1 us (41%)
  waiting for transfers between devices  25.9 us (23%)
  starting transfers between devices  22.5 us (20%)
  Pallas kernels  13.9 us (12%)
  local copies, waits for them, and re-layouts  3.63 us (3%)
  between operations  1.41 us (1%)
    all_to_all x1, blocking collectives, body(): lax.all_to_all(packs.reshape(N_PLANE, PACK, LANES), PLANE, split_axis=0,...  31.3 us
    all_to_all x1, blocking collectives, body(): lax.all_to_all(lines.reshape(N_LINE, BLOCK, LANES), LINE, split_axis=0, c...  15.8 us
    all_to_all x1, starting transfers between devices, body(): known = lax.all_to_all(many, TM, split_axis=0, concat_axis=0, tiled=True)  15.4 us
    pallas_call x7, Pallas kernels, call(): pl.pallas_call(kernel, out_shape=outs, in_specs=specs, out_specs=[pl.Bloc...  13.9 us
    all_to_all x1, waiting for transfers between devices, body(): lax.all_to_all(picked.reshape(N_TM, 16, LANES), TM, split_axis=0, concat_...  12.6 us
    all_to_all x1, waiting for transfers between devices, body(): known = lax.all_to_all(many, TM, split_axis=0, concat_axis=0, tiled=True)  10.2 us
    all_to_all x1, starting transfers between devices, body(): lax.all_to_all(picked.reshape(N_TM, 16, LANES), TM, split_axis=0, concat_...  7.01 us
    ppermute x1, waiting for transfers between devices, body(): other = lax.ppermute(send, 'dp', [(0, 1), (1, 0)])  3.02 us
  transfers between devices with their start and end apart: 3, of which 3 were waited for; matrix products, arithmetic and copies ran while one was open for 1% of the time, Pallas kernels for 2%

profile of v3, /device:TPU:2, one launch (start us, length us, event | category | flops | bytes accessed | tf_op | source)
XLA Modules:
  0.0 114.5 jit_solution(16394898622889040179)
XLA Ops:
  0.6 0.0 copy-start.1
  0.6 0.0 copy-start.3
  0.7 0.7 copy-done.3
  1.3 0.0 copy-start.4
  1.3 0.8 shard_map.110
  2.2 15.4 %all-to-all-start = ((s32[128,1,256]{2,1,0:T(1,128)}), s32[128,1,256]{2,1,0:T(1,128)S(1)}, u32[]{:S(2)}, u32[]{:S(2)}) async-start(s32[128,1,256]{2,1,0:T(1,128)} %get-tuple-element.17), calls=%async_computation | async-start | bytes 262144 | tf_op jit(solution)/shard_map/all_to_all | solution.py:342
  17.6 1.0 reshape.46.table_ref
  18.6 0.1 pad_add_fusion.place_ref
  18.7 10.2 %all-to-all-done.offs_ref = s32[128,1,256]{2,1,0:T(1,128)S(1)} async-done(((s32[128,1,256]{2,1,0:T(1,128)}), s32[128,1,256]{2,1,0:T(1,128)S(1)}, u32[]{:S(2)}, u32[]{:S(2)}) %all-to-all-start) | async-done | bytes 131104 | tf_op jit(solution)/shard_map/all_to_all | solution.py:342
  29.0 2.1 %shard_map.111 = bf16[2048,128]{1,0:T(8,128)(2,1)} custom-call(s32[2]{0:T(128)S(1)} %pad_add_fusion.place_ref, s32[128,1,256]{2,1,0:T(1,128)S(1)} %all-to-all-done.offs_ref, bf16[256,512]{1,0:T(8,128)(2,1)S(1)} %reshape.46.table_ref), custom_call_target="tpu_custom_call" | custom-call | flops 100000000 | bytes 1048576 | tf_op jit(solution)/shard_map/pallas_call | solution.py:319
  31.0 7.0 %all-to-all-start.1 = ((bf16[128,16,128]{2,1,0:T(8,128)(2,1)}), bf16[128,16,128]{2,1,0:T(8,128)(2,1)S(1)}, u32[]{:S(2)}, u32[]{:S(2)}) async-start(bf16[128,16,128]{2,1,0:T(8,128)(2,1)} %bitcast.3), calls=%async_computation.1 | async-start | bytes 1048576 | tf_op jit(solution)/shard_map/all_to_all | solution.py:361
  38.7 0.0 copy-done.4
  38.7 0.0 copy-start.2
  38.8 0.0 copy-done.1
  38.8 0.0 copy-start
  38.8 1.9 %copy-done = bf16[768,2048]{1,0:T(8,128)(2,1)S(1)} copy-done((bf16[768,2048]{1,0:T(8,128)(2,1)S(1)}, bf16[768,2048]{1,0:T(8,128)(2,1)}, u32[]{:S(2)}) %copy-start) | copy-done | bytes 3145752
  40.7 2.4 %shard_map.112 = (f32[256,2048]{1,0:T(8,128)S(1)}, bf16[256,512]{1,0:T(8,128)(2,1)S(1)}, s32[256,128]{1,0:T(8,128)S(1)}) custom-call(s32[2]{0:T(128)S(1)} %pad_add_fusion.place_ref, s32[1,256]{1,0:T(1,128)S(1)} %get-tuple-element.18.offs_ref, bf16[256,512]{1,0:T(8,128)(2,1)S(1)} %reshape.46.table_ref, bf16[256,256]{1,0:T(8,128)(2,1)S(1)} %reshape.49.state_ref, ...), custom_call_target="tpu_custom_call" | custom-call | flops 1000000000 | bytes 1048576 | tf_op jit(solution)/shard_map/pallas_call | solution.py:319
  43.1 12.6 %all-to-all-done.1 = bf16[128,16,128]{2,1,0:T(8,128)(2,1)S(1)} async-done(((bf16[128,16,128]{2,1,0:T(8,128)(2,1)}), bf16[128,16,128]{2,1,0:T(8,128)(2,1)S(1)}, u32[]{:S(2)}, u32[]{:S(2)}) %all-to-all-start.1) | async-done | bytes 524320 | tf_op jit(solution)/shard_map/all_to_all | solution.py:361
  55.7 0.0 copy-done.2
  55.7 6.7 %shard_map.113 = (f32[4,64]{1,0:T(4,128)}, bf16[320,2048]{1,0:T(8,128)(2,1)S(1)}, bf16[384,256]{1,0:T(8,128)(2,1)S(1)}) custom-call(s32[2]{0:T(128)S(1)} %pad_add_fusion.place_ref, f32[1]{0:T(128)S(6)} %copy.12.b_out_ref, bf16[2048,128]{1,0:T(8,128)(2,1)S(1)} %bitcast.20, f32[256,2048]{1,0:T(8,128)S(1)} %get-tuple-element.19.base_ref, ...), custom_call_target="tpu_custom_call" | custom-call | flops 2000000000 | bytes 1048576 | tf_op jit(solution)/shard_map/pallas_call | solution.py:319
  62.3 0.1 collective-permute-start
  62.4 3.0 %collective-permute-done.other_ref = bf16[320,2048]{1,0:T(8,128)(2,1)S(1)} collective-permute-done((bf16[320,2048]{1,0:T(8,128)(2,1)S(1)}, bf16[320,2048]{1,0:T(8,128)(2,1)S(1)}, u32[]{:S(2)}, u32[]{:S(2)}) %collective-permute-start) | collective-permute-done | bytes 1310752 | tf_op jit(solution)/shard_map/ppermute | solution.py:375
  65.4 1.0 shard_map.114
  66.4 31.3 %all_to_all.20 = bf16[16,464,128]{2,1,0:T(8,128)(2,1)S(1)} all-to-all(bf16[16,464,128]{2,1,0:T(8,128)(2,1)S(1)} %bitcast.16), channel_id=1, replica_groups=mesh['tm_0'=4,'tm_1'=4,'tm_2'=8,'dp'=2] {'tm_0','tm_1'}, dimensions={0} | all-to-all | bytes 3801088 | tf_op jit(solution)/shard_map/all_to_all | solution.py:384
  97.8 0.3 shard_map.115
  98.0 15.8 %all_to_all.21 = f32[8,88,128]{2,1,0:T(8,128)S(1)} all-to-all(f32[8,88,128]{2,1,0:T(8,128)S(1)} %bitcast.18), channel_id=1, replica_groups=mesh['tm_0'=4,'tm_1'=4,'tm_2'=8,'dp'=2] {'tm_2'}, dimensions={0} | all-to-all | bytes 720896 | tf_op jit(solution)/shard_map/all_to_all | solution.py:395
  113.8 0.7 shard_map.116
  (1 shorter events, 0.0 us)
Async XLA Ops:
  0.6 38.1 %copy-start.1 = (f32[2048]{0:T(1024)S(1)}, f32[2048]{0:T(1024)}, u32[]{:S(2)}) copy-start(f32[2048]{0:T(1024)} %param.11) | copy-start | bytes 24580
  0.6 0.7 copy-start.3
  1.3 37.4 %copy-start.4 = (bf16[64,4,256]{2,1,0:T(4,128)(2,1)S(1)}, bf16[64,4,256]{2,1,0:T(4,128)(2,1)}, u32[]{:S(2)}) copy-start(bf16[64,4,256]{2,1,0:T(4,128)(2,1)} %param.7) | copy-start | bytes 393220
  2.2 26.8 %all-to-all-start = ((s32[128,1,256]{2,1,0:T(1,128)}), s32[128,1,256]{2,1,0:T(1,128)S(1)}, u32[]{:S(2)}, u32[]{:S(2)}) async-start(s32[128,1,256]{2,1,0:T(1,128)} %get-tuple-element.17), calls=%async_computation | async-start | bytes 262144 | tf_op jit(solution)/shard_map/all_to_all | solution.py:342
  31.0 24.6 %all-to-all-start.1 = ((bf16[128,16,128]{2,1,0:T(8,128)(2,1)}), bf16[128,16,128]{2,1,0:T(8,128)(2,1)S(1)}, u32[]{:S(2)}, u32[]{:S(2)}) async-start(bf16[128,16,128]{2,1,0:T(8,128)(2,1)} %bitcast.3), calls=%async_computation.1 | async-start | bytes 1048576 | tf_op jit(solution)/shard_map/all_to_all | solution.py:361
  38.7 16.9 %copy-start.2 = (f32[2048]{0:T(1024)S(1)}, f32[2048]{0:T(1024)}, u32[]{:S(2)}) copy-start(f32[2048]{0:T(1024)} %param.12) | copy-start | bytes 24580
  38.8 1.9 %copy-start = (bf16[768,2048]{1,0:T(8,128)(2,1)S(1)}, bf16[768,2048]{1,0:T(8,128)(2,1)}, u32[]{:S(2)}) copy-start(bf16[768,2048]{1,0:T(8,128)(2,1)} %w_in_ref.3) | copy-start | bytes 9437188
  62.3 3.1 %collective-permute-start = (bf16[320,2048]{1,0:T(8,128)(2,1)S(1)}, bf16[320,2048]{1,0:T(8,128)(2,1)S(1)}, u32[]{:S(2)}, u32[]{:S(2)}) collective-permute-start(bf16[320,2048]{1,0:T(8,128)(2,1)S(1)} %get-tuple-element.23.own_ref), channel_id=1, source_target_pairs={{0,1},{1,0},{2,3},{3,2},{4,5},{5,4},{6,7},{7,6},{8,9},{9,8},{10,11... | collective-permute-start | bytes 3932168 | tf_op jit(solution)/shard_map/ppermute | solution.py:375

commit v4 on v3

--- a/solution.py
+++ b/solution.py
@@ -142,7 +142,7 @@
     slot = jnp.sum(flag((owner == owner_lane) & (row < col)), axis=1, keepdims=True)
     remote = owner != me.astype(F32)
     near_at = jnp.where(remote, -1.0, position)
-    far_at = jnp.where(remote, owner * 16.0 + slot * 4.0, -100.0).astype(I32)
+    far_at = jnp.where(remote, owner * float(CAP) + slot, -1.0).astype(I32)
     near = flag(row.astype(F32) == near_at).astype(BF16)
     near_ref[...] = dot(near, table_ref[...]).astype(BF16)
     at_ref[...] = jnp.broadcast_to(far_at, (ROWS, LANES))
@@ -175,19 +175,21 @@
     hidden_ref,
     inputs_ref,
     goal_w_ref,
+    wide_ref,
     sem,
 ):
     load = pltpu.make_async_copy(w_in_ref.at[pl.ds(S, G), :], goal_w_ref, sem)
     load.start()
     core = place_ref[1]
     far_at = at_ref[:, 0:1]
-    spot = iota((ROWS, N_TM * 16), 1)
+    far = flag(iota((ROWS, N_TM * CAP), 1) == far_at).astype(BF16)
     inputs_ref[:, :S] = state_ref[...]
-    fetched = fetched_ref[...]
+    wide_ref[...] = fetched_ref[...].astype(F32)
     gap = jnp.zeros((ROWS, LANES), F32)
     for j in range(G // LANES):
         at = slice(j * LANES, (j + 1) * LANES)
-        goal = dot(flag(spot == far_at + j).astype(BF16), fetched) + near_ref[:, at].astype(F32)
+        fetched = wide_ref[pl.ds(j, N_TM * CAP, stride=G // LANES), :].astype(BF16)
+        goal = dot(far, fetched) + near_ref[:, at].astype(F32)
         diff = table_ref[:, at].astype(F32) - goal
         gap = gap + diff * diff
         inputs_ref[:, S + j * LANES : S + (j + 1) * LANES] = goal.astype(BF16)
@@ -240,7 +242,7 @@
 
 
 PACK = 464
-BLOCK = 88
+BLOCK = 128
 
 
 def product_kernel(own_ref, other_ref, keep_ref, out_ref, left_ref):
@@ -277,37 +279,38 @@
         out_ref[p * PACK + HALF : (p + 1) * PACK, :] = small
 
 
-def plane_kernel(got_ref, out_ref, sum_ref):
+def plane_kernel(got_ref, out_ref, sum_ref, wide_ref):
     for b in range(PACK // 16):
         total = got_ref[b * 16 : b * 16 + 16, :].astype(F32)
         for p in range(1, N_PLANE):
             total = total + got_ref[p * PACK + b * 16 : p * PACK + b * 16 + 16, :].astype(F32)
         sum_ref[b * 16 : b * 16 + 16, :] = total
     for n in range(48):
-        out_ref[pl.ds(n, N_LINE, stride=BLOCK), :] = sum_ref[8 * n : 8 * n + 8, :]
+        wide_ref[pl.ds(n, N_LINE, stride=48), :] = sum_ref[8 * n : 8 * n + 8, :]
+    last = sum_ref[448:449, :] + sum_ref[449:450, :]
     small = jnp.concatenate(
-        [
-            sum_ref[384:400, :] + sum_ref[400:416, :],
-            sum_ref[416:432, :] + sum_ref[432:448, :],
-            jnp.broadcast_to(sum_ref[448:449, :] + sum_ref[449:450, :], (8, LANES)),
-        ],
+        two(sum_ref[384:400, :] + sum_ref[400:416, :])
+        + two(sum_ref[416:432, :] + sum_ref[432:448, :])
+        + (stack_rows(two(last), 16),),
         axis=0,
-    )
+    ).astype(BF16)
     for z in range(N_LINE):
+        out_ref[z * BLOCK : z * BLOCK + 48, :] = wide_ref[z * 48 : z * 48 + 48, :].astype(BF16)
         out_ref[z * BLOCK + 48 : (z + 1) * BLOCK, :] = small
 
 
 def line_kernel(got_ref, w_ref, b_in_ref, w_out_ref, b_out_ref, sum_ref):
-    total = got_ref[0:BLOCK, :]
-    for z in range(1, N_LINE):
-        total = total + got_ref[z * BLOCK : (z + 1) * BLOCK, :]
-    sum_ref[...] = total
+    for b in range(BLOCK // 16):
+        total = got_ref[b * 16 : b * 16 + 16, :].astype(F32)
+        for z in range(1, N_LINE):
+            total = total + got_ref[z * BLOCK + b * 16 : z * BLOCK + b * 16 + 16, :].astype(F32)
+        sum_ref[b * 16 : b * 16 + 16, :] = total
     for i in range(3):
         for b in range(H // LANES):
             w_ref[i : i + 1, b * LANES : (b + 1) * LANES] = sum_ref[i * 16 + b : i * 16 + b + 1, :]
-    b_in_ref[...] = sum_ref[48:64, :]
-    w_out_ref[...] = sum_ref[64:80, :]
-    b_out_ref[...] = sum_ref[80:81, :]
+    b_in_ref[...] = sum_ref[48:64, :] + sum_ref[64:80, :]
+    w_out_ref[...] = sum_ref[80:96, :] + sum_ref[96:112, :]
+    b_out_ref[...] = sum_ref[112:113, :] + sum_ref[113:114, :]
 
 
 def call(kernel, shapes, operands, scratch, flops, grant, in_smem=0, in_hbm=()):
@@ -366,7 +369,7 @@
         functools.partial(main_kernel, scale),
         [((STEPS, ROWS // STEPS), F32), ((ROWS + 64, H), BF16), ((HALF, ROWS), BF16)],
         (place, b_out, fetched, base, near, at, table, state, w_in, w_out.reshape(1, H)),
-        [pltpu.VMEM((ROWS, H), F32), pltpu.VMEM((ROWS, H), BF16), pltpu.VMEM((ROWS, S + G), BF16), pltpu.VMEM((G, H), BF16), pltpu.SemaphoreType.DMA],
+        [pltpu.VMEM((ROWS, H), F32), pltpu.VMEM((ROWS, H), BF16), pltpu.VMEM((ROWS, S + G), BF16), pltpu.VMEM((G, H), BF16), pltpu.VMEM((N_TM * 16, LANES), F32), pltpu.SemaphoreType.DMA],
         2 * 10**9,
         48,
         2,
@@ -386,9 +389,9 @@
     ).reshape(N_PLANE * PACK, LANES)
     (lines,) = call(
         plane_kernel,
-        [((N_LINE * BLOCK, LANES), F32)],
+        [((N_LINE * BLOCK, LANES), BF16)],
         (got,),
-        [pltpu.VMEM((PACK, LANES), F32)],
+        [pltpu.VMEM((PACK, LANES), F32), pltpu.VMEM((N_LINE * 48, LANES), F32)],
         10**7,
         6,
     )

time: 115 us -> 113 us (0.983)
  blocking collectives: 47.1 us -> 45 us
    all_to_all x1, blocking collectives: 15.8 us -> 13.7 us  [body(): lax.all_to_all(lines.reshape(N_LINE, BLOCK, LANES), LINE, split_axis=0, c...]
where the time goes in v4:
time: 113 us; the launch traced here: 112 us
  blocking collectives  45 us (40%)
  waiting for transfers between devices  25.9 us (23%)
  starting transfers between devices  22.5 us (20%)
  Pallas kernels  13.9 us (12%)
  local copies, waits for them, and re-layouts  3.63 us (3%)
  between operations  1.41 us (1%)
    all_to_all x1, blocking collectives, body(): lax.all_to_all(packs.reshape(N_PLANE, PACK, LANES), PLANE, split_axis=0,...  31.3 us
    all_to_all x1, starting transfers between devices, body(): known = lax.all_to_all(many, TM, split_axis=0, concat_axis=0, tiled=True)  15.4 us
    pallas_call x7, Pallas kernels, call(): pl.pallas_call(kernel, out_shape=outs, in_specs=specs, out_specs=[pl.Bloc...  13.9 us
    all_to_all x1, blocking collectives, body(): lax.all_to_all(lines.reshape(N_LINE, BLOCK, LANES), LINE, split_axis=0, c...  13.7 us
    all_to_all x1, waiting for transfers between devices, body(): lax.all_to_all(picked.reshape(N_TM, 16, LANES), TM, split_axis=0, concat_...  12.6 us
    all_to_all x1, waiting for transfers between devices, body(): known = lax.all_to_all(many, TM, split_axis=0, concat_axis=0, tiled=True)  10.2 us
    all_to_all x1, starting transfers between devices, body(): lax.all_to_all(picked.reshape(N_TM, 16, LANES), TM, split_axis=0, concat_...  7.01 us
    ppermute x1, waiting for transfers between devices, body(): other = lax.ppermute(send, 'dp', [(0, 1), (1, 0)])  3.02 us
  transfers between devices with their start and end apart: 3, of which 3 were waited for; matrix products, arithmetic and copies ran while one was open for 1% of the time, Pallas kernels for 2%

profile of v4, /device:TPU:2, one launch (start us, length us, event | category | flops | bytes accessed | tf_op | source)
XLA Modules:
  0.0 112.5 jit_solution(8694561356591436821)
XLA Ops:
  0.6 0.0 copy-start.1
  0.6 0.0 copy-start.3
  0.7 0.7 copy-done.3
  1.3 0.0 copy-start.4
  1.3 0.8 shard_map.110
  2.2 15.4 %all-to-all-start = ((s32[128,1,256]{2,1,0:T(1,128)}), s32[128,1,256]{2,1,0:T(1,128)S(1)}, u32[]{:S(2)}, u32[]{:S(2)}) async-start(s32[128,1,256]{2,1,0:T(1,128)} %get-tuple-element.17), calls=%async_computation | async-start | bytes 262144 | tf_op jit(solution)/shard_map/all_to_all | solution.py:345
  17.6 1.0 reshape.46.table_ref
  18.6 0.1 pad_add_fusion.place_ref
  18.7 10.2 %all-to-all-done.offs_ref = s32[128,1,256]{2,1,0:T(1,128)S(1)} async-done(((s32[128,1,256]{2,1,0:T(1,128)}), s32[128,1,256]{2,1,0:T(1,128)S(1)}, u32[]{:S(2)}, u32[]{:S(2)}) %all-to-all-start) | async-done | bytes 131104 | tf_op jit(solution)/shard_map/all_to_all | solution.py:345
  29.0 2.1 %shard_map.111 = bf16[2048,128]{1,0:T(8,128)(2,1)} custom-call(s32[2]{0:T(128)S(1)} %pad_add_fusion.place_ref, s32[128,1,256]{2,1,0:T(1,128)S(1)} %all-to-all-done.offs_ref, bf16[256,512]{1,0:T(8,128)(2,1)S(1)} %reshape.46.table_ref), custom_call_target="tpu_custom_call" | custom-call | flops 100000000 | bytes 1048576 | tf_op jit(solution)/shard_map/pallas_call | solution.py:322
  31.0 7.0 %all-to-all-start.1 = ((bf16[128,16,128]{2,1,0:T(8,128)(2,1)}), bf16[128,16,128]{2,1,0:T(8,128)(2,1)S(1)}, u32[]{:S(2)}, u32[]{:S(2)}) async-start(bf16[128,16,128]{2,1,0:T(8,128)(2,1)} %bitcast.3), calls=%async_computation.1 | async-start | bytes 1048576 | tf_op jit(solution)/shard_map/all_to_all | solution.py:364
  38.7 0.0 copy-done.4
  38.7 0.0 copy-start.2
  38.8 0.0 copy-done.1
  38.8 0.0 copy-start
  38.8 1.9 %copy-done = bf16[768,2048]{1,0:T(8,128)(2,1)S(1)} copy-done((bf16[768,2048]{1,0:T(8,128)(2,1)S(1)}, bf16[768,2048]{1,0:T(8,128)(2,1)}, u32[]{:S(2)}) %copy-start) | copy-done | bytes 3145752
  40.7 2.4 %shard_map.112 = (f32[256,2048]{1,0:T(8,128)S(1)}, bf16[256,512]{1,0:T(8,128)(2,1)S(1)}, s32[256,128]{1,0:T(8,128)S(1)}) custom-call(s32[2]{0:T(128)S(1)} %pad_add_fusion.place_ref, s32[1,256]{1,0:T(1,128)S(1)} %get-tuple-element.18.offs_ref, bf16[256,512]{1,0:T(8,128)(2,1)S(1)} %reshape.46.table_ref, bf16[256,256]{1,0:T(8,128)(2,1)S(1)} %reshape.49.state_ref, ...), custom_call_target="tpu_custom_call" | custom-call | flops 1000000000 | bytes 1048576 | tf_op jit(solution)/shard_map/pallas_call | solution.py:322
  43.1 12.6 %all-to-all-done.1 = bf16[128,16,128]{2,1,0:T(8,128)(2,1)S(1)} async-done(((bf16[128,16,128]{2,1,0:T(8,128)(2,1)}), bf16[128,16,128]{2,1,0:T(8,128)(2,1)S(1)}, u32[]{:S(2)}, u32[]{:S(2)}) %all-to-all-start.1) | async-done | bytes 524320 | tf_op jit(solution)/shard_map/all_to_all | solution.py:364
  55.7 0.0 copy-done.2
  55.7 6.7 %shard_map.113 = (f32[4,64]{1,0:T(4,128)}, bf16[320,2048]{1,0:T(8,128)(2,1)S(1)}, bf16[384,256]{1,0:T(8,128)(2,1)S(1)}) custom-call(s32[2]{0:T(128)S(1)} %pad_add_fusion.place_ref, f32[1]{0:T(128)S(6)} %copy.12.b_out_ref, bf16[2048,128]{1,0:T(8,128)(2,1)S(1)} %bitcast.20, f32[256,2048]{1,0:T(8,128)S(1)} %get-tuple-element.19.base_ref, ...), custom_call_target="tpu_custom_call" | custom-call | flops 2000000000 | bytes 1048576 | tf_op jit(solution)/shard_map/pallas_call | solution.py:322
  62.3 0.1 collective-permute-start
  62.4 3.0 %collective-permute-done.other_ref = bf16[320,2048]{1,0:T(8,128)(2,1)S(1)} collective-permute-done((bf16[320,2048]{1,0:T(8,128)(2,1)S(1)}, bf16[320,2048]{1,0:T(8,128)(2,1)S(1)}, u32[]{:S(2)}, u32[]{:S(2)}) %collective-permute-start) | collective-permute-done | bytes 1310752 | tf_op jit(solution)/shard_map/ppermute | solution.py:378
  65.5 1.0 shard_map.114
  66.5 31.3 %all_to_all.20 = bf16[16,464,128]{2,1,0:T(8,128)(2,1)S(1)} all-to-all(bf16[16,464,128]{2,1,0:T(8,128)(2,1)S(1)} %bitcast.16), channel_id=1, replica_groups=mesh['tm_0'=4,'tm_1'=4,'tm_2'=8,'dp'=2] {'tm_0','tm_1'}, dimensions={0} | all-to-all | bytes 3801088 | tf_op jit(solution)/shard_map/all_to_all | solution.py:387
  97.8 0.3 shard_map.115
  98.1 13.7 %all_to_all.21 = bf16[8,128,128]{2,1,0:T(8,128)(2,1)S(1)} all-to-all(bf16[8,128,128]{2,1,0:T(8,128)(2,1)S(1)} %bitcast.18), channel_id=1, replica_groups=mesh['tm_0'=4,'tm_1'=4,'tm_2'=8,'dp'=2] {'tm_2'}, dimensions={0} | all-to-all | bytes 524288 | tf_op jit(solution)/shard_map/all_to_all | solution.py:398
  111.8 0.7 shard_map.116
  (1 shorter events, 0.0 us)
Async XLA Ops:
  0.6 38.1 %copy-start.1 = (f32[2048]{0:T(1024)S(1)}, f32[2048]{0:T(1024)}, u32[]{:S(2)}) copy-start(f32[2048]{0:T(1024)} %param.11) | copy-start | bytes 24580
  0.6 0.7 copy-start.3
  1.3 37.4 %copy-start.4 = (bf16[64,4,256]{2,1,0:T(4,128)(2,1)S(1)}, bf16[64,4,256]{2,1,0:T(4,128)(2,1)}, u32[]{:S(2)}) copy-start(bf16[64,4,256]{2,1,0:T(4,128)(2,1)} %param.7) | copy-start | bytes 393220
  2.2 26.8 %all-to-all-start = ((s32[128,1,256]{2,1,0:T(1,128)}), s32[128,1,256]{2,1,0:T(1,128)S(1)}, u32[]{:S(2)}, u32[]{:S(2)}) async-start(s32[128,1,256]{2,1,0:T(1,128)} %get-tuple-element.17), calls=%async_computation | async-start | bytes 262144 | tf_op jit(solution)/shard_map/all_to_all | solution.py:345
  31.0 24.6 %all-to-all-start.1 = ((bf16[128,16,128]{2,1,0:T(8,128)(2,1)}), bf16[128,16,128]{2,1,0:T(8,128)(2,1)S(1)}, u32[]{:S(2)}, u32[]{:S(2)}) async-start(bf16[128,16,128]{2,1,0:T(8,128)(2,1)} %bitcast.3), calls=%async_computation.1 | async-start | bytes 1048576 | tf_op jit(solution)/shard_map/all_to_all | solution.py:364
  38.7 16.9 %copy-start.2 = (f32[2048]{0:T(1024)S(1)}, f32[2048]{0:T(1024)}, u32[]{:S(2)}) copy-start(f32[2048]{0:T(1024)} %param.12) | copy-start | bytes 24580
  38.8 1.9 %copy-start = (bf16[768,2048]{1,0:T(8,128)(2,1)S(1)}, bf16[768,2048]{1,0:T(8,128)(2,1)}, u32[]{:S(2)}) copy-start(bf16[768,2048]{1,0:T(8,128)(2,1)} %w_in_ref.3) | copy-start | bytes 9437188
  62.3 3.1 %collective-permute-start = (bf16[320,2048]{1,0:T(8,128)(2,1)S(1)}, bf16[320,2048]{1,0:T(8,128)(2,1)S(1)}, u32[]{:S(2)}, u32[]{:S(2)}) collective-permute-start(bf16[320,2048]{1,0:T(8,128)(2,1)S(1)} %get-tuple-element.23.own_ref), channel_id=1, source_target_pairs={{0,1},{1,0},{2,3},{3,2},{4,5},{5,4},{6,7},{7,6},{8,9},{9,8},{10,11... | collective-permute-start | bytes 3932168 | tf_op jit(solution)/shard_map/ppermute | solution.py:378

commit v5 on v4

--- a/solution.py
+++ b/solution.py
@@ -58,7 +58,7 @@
 
 
 def pick_kernel(place_ref, offs_ref, table_ref, out_ref, wide_ref):
-    me = place_ref[0]
+    me = place_ref[0:1, 0:1]
     offs = offs_ref[...].reshape(N_TM, ROWS)
     peer = iota((N_TM, ROWS), 0)
     row = iota((N_TM, ROWS), 1)
@@ -122,7 +122,7 @@
     near_ref,
     at_ref,
 ):
-    me = place_ref[0]
+    me = place_ref[0:1, 0:1]
     row = iota((ROWS, ROWS), 1)
     col = iota((ROWS, ROWS), 0)
     lane = iota((1, ROWS), 1)
@@ -176,11 +176,18 @@
     inputs_ref,
     goal_w_ref,
     wide_ref,
-    sem,
+    total_ref,
+    sems,
 ):
-    load = pltpu.make_async_copy(w_in_ref.at[pl.ds(S, G), :], goal_w_ref, sem)
-    load.start()
-    core = place_ref[1]
+    def load(n):
+        at = pl.ds(pl.multiple_of(n * CHUNK, CHUNK), CHUNK)
+        return pltpu.make_async_copy(
+            w_in_ref.at[pl.ds(S, G), at], goal_w_ref.at[:, at], sems.at[n]
+        )
+
+    for n in range(H // CHUNK):
+        load(n).start()
+    core = place_ref[1:2, 0:1]
     far_at = at_ref[:, 0:1]
     far = flag(iota((ROWS, N_TM * CAP), 1) == far_at).astype(BF16)
     inputs_ref[:, :S] = state_ref[...]
@@ -195,21 +202,24 @@
         inputs_ref[:, S + j * LANES : S + (j + 1) * LANES] = goal.astype(BF16)
     reward = -(jnp.sum(gap, axis=1, keepdims=True) * (1.0 / G))
     inputs = inputs_ref[...]
-    load.wait()
-
-    def forward(n, total):
+    total_ref[...] = jnp.zeros((ROWS, LANES), F32)
+
+    def forward(n, carry):
         at = pl.ds(pl.multiple_of(n * CHUNK, CHUNK), CHUNK)
+        load(n).wait()
         pre = base_ref[:, at] + dot(inputs[:, S:], goal_w_ref[:, at])
         sig = 1.0 / (1.0 + jnp.exp(-pre))
         head = w_out_ref[:, at]
-        hidden = (pre * sig).astype(BF16)
+        act = pre * sig
+        hidden = act.astype(BF16)
         hidden_ref[:, at] = hidden
-        slope_ref[:, at] = head * (sig * (1.0 + pre * (1.0 - sig)))
+        slope_ref[:, at] = head * (sig + act * (1.0 - sig))
         term = hidden.astype(F32) * head
-        return total + term[:, :LANES] + term[:, LANES:]
-
-    total = lax.fori_loop(0, H // CHUNK, forward, jnp.zeros((ROWS, LANES), F32))
-    value = jnp.sum(total, axis=1, keepdims=True) + b_out_ref[0]
+        total_ref[...] += term[:, :LANES] + term[:, LANES:]
+        return carry
+
+    lax.fori_loop(0, H // CHUNK, forward, 0)
+    value = jnp.sum(total_ref[...], axis=1, keepdims=True) + b_out_ref[:, 0:1]
     error = value - reward
     grad_value = error * scale
 
@@ -313,9 +323,8 @@
     b_out_ref[...] = sum_ref[112:113, :] + sum_ref[113:114, :]
 
 
-def call(kernel, shapes, operands, scratch, flops, grant, in_smem=0, in_hbm=()):
-    specs = [pl.BlockSpec(memory_space=pltpu.SMEM)] * in_smem
-    specs += [pl.BlockSpec(memory_space=pltpu.VMEM)] * (len(operands) - in_smem)
+def call(kernel, shapes, operands, scratch, flops, grant, in_hbm=()):
+    specs = [pl.BlockSpec(memory_space=pltpu.VMEM)] * len(operands)
     for n in in_hbm:
         specs[n] = pl.BlockSpec(memory_space=pltpu.HBM)
     outs = [jax.ShapeDtypeStruct(shape, kind) for shape, kind in shapes]
@@ -332,6 +341,7 @@
 
 def body(state_feats, achieved, offsets, w_in, b_in, w_out, b_out):
     place = jnp.stack([lax.axis_index(TM), lax.axis_index("dp")]).astype(I32)
+    place = jnp.broadcast_to(place[:, None], (2, LANES))
     table = achieved.reshape(ROWS, G)
     state = state_feats.reshape(ROWS, S)
     many, offs = call(
@@ -350,7 +360,6 @@
         [pltpu.VMEM((N_TM * 16, LANES), F32)],
         10**8,
         6,
-        1,
     )
     base, near, at = call(
         ahead_kernel,
@@ -359,20 +368,19 @@
         [],
         10**9,
         12,
-        1,
     )
     fetched = lax.all_to_all(
         picked.reshape(N_TM, 16, LANES), TM, split_axis=0, concat_axis=0, tiled=True
     ).reshape(N_TM * 16, LANES)
+    head_bias = jnp.broadcast_to(b_out[None], (1, LANES))
     scale = 1.0 / math.sqrt(ROWS * N_TM * 2)
     td, send, keep = call(
         functools.partial(main_kernel, scale),
         [((STEPS, ROWS // STEPS), F32), ((ROWS + 64, H), BF16), ((HALF, ROWS), BF16)],
-        (place, b_out, fetched, base, near, at, table, state, w_in, w_out.reshape(1, H)),
-        [pltpu.VMEM((ROWS, H), F32), pltpu.VMEM((ROWS, H), BF16), pltpu.VMEM((ROWS, S + G), BF16), pltpu.VMEM((G, H), BF16), pltpu.VMEM((N_TM * 16, LANES), F32), pltpu.SemaphoreType.DMA],
+        (place, head_bias, fetched, base, near, at, table, state, w_in, w_out.reshape(1, H)),
+        [pltpu.VMEM((ROWS, H), F32), pltpu.VMEM((ROWS, H), BF16), pltpu.VMEM((ROWS, S + G), BF16), pltpu.VMEM((G, H), BF16), pltpu.VMEM((N_TM * 16, LANES), F32), pltpu.VMEM((ROWS, LANES), F32), pltpu.SemaphoreType.DMA((H // CHUNK,))],
         2 * 10**9,
         48,
-        2,
         (8,),
     )
     other = lax.ppermute(send, "dp", [(0, 1), (1, 0)])

time: 113 us -> 111 us (0.982)
  Pallas kernels: 13.9 us -> 12.2 us
    pallas_call x7, Pallas kernels: 13.9 us -> 12.2 us  [call(): pl.pallas_call(kernel, out_shape=outs, in_specs=specs, out_specs=[pl.Bloc...]
where the time goes in v5:
time: 111 us
  blocking collectives  45 us (41%)
  waiting for transfers between devices  26.2 us (24%)
  starting transfers between devices  22.5 us (20%)
  Pallas kernels  12.2 us (11%)
  local copies, waits for them, and re-layouts  3.7 us (3%)
  between operations  1.41 us (1%)
    all_to_all x1, blocking collectives, body(): lax.all_to_all(packs.reshape(N_PLANE, PACK, LANES), PLANE, split_axis=0,...  31.3 us
    all_to_all x1, starting transfers between devices, body(): known = lax.all_to_all(many, TM, split_axis=0, concat_axis=0, tiled=True)  15.4 us
    all_to_all x1, blocking collectives, body(): lax.all_to_all(lines.reshape(N_LINE, BLOCK, LANES), LINE, split_axis=0, c...  13.7 us
    all_to_all x1, waiting for transfers between devices, body(): lax.all_to_all(picked.reshape(N_TM, 16, LANES), TM, split_axis=0, concat_...  12.9 us
    pallas_call x7, Pallas kernels, call(): pl.pallas_call(kernel, out_shape=outs, in_specs=specs, out_specs=[pl.Bloc...  12.2 us
    all_to_all x1, waiting for transfers between devices, body(): known = lax.all_to_all(many, TM, split_axis=0, concat_axis=0, tiled=True)  10.2 us
    all_to_all x1, starting transfers between devices, body(): lax.all_to_all(picked.reshape(N_TM, 16, LANES), TM, split_axis=0, concat_...  7 us
    ppermute x1, waiting for transfers between devices, body(): other = lax.ppermute(send, 'dp', [(0, 1), (1, 0)])  3.02 us
  transfers between devices with their start and end apart: 3, of which 3 were waited for; matrix products, arithmetic and copies ran while one was open for 1% of the time, Pallas kernels for 2%

profile of v5, /device:TPU:2, one launch (start us, length us, event | category | flops | bytes accessed | tf_op | source)
XLA Modules:
  0.0 111.1 jit_solution(3555599596688487251)
XLA Ops:
  0.6 0.0 copy-start.1
  0.6 0.0 copy-start.3
  0.7 0.7 copy-done.3
  1.3 0.0 copy-start.4
  1.3 0.8 shard_map.110
  2.2 15.4 %all-to-all-start = ((s32[128,1,256]{2,1,0:T(1,128)}), s32[128,1,256]{2,1,0:T(1,128)S(1)}, u32[]{:S(2)}, u32[]{:S(2)}) async-start(s32[128,1,256]{2,1,0:T(1,128)} %get-tuple-element.17), calls=%async_computation | async-start | bytes 262144 | tf_op jit(solution)/shard_map/all_to_all | solution.py:355
  17.6 1.0 reshape.50.table_ref
  18.6 0.1 pad_add_fusion
  18.7 10.2 %all-to-all-done.offs_ref = s32[128,1,256]{2,1,0:T(1,128)S(1)} async-done(((s32[128,1,256]{2,1,0:T(1,128)}), s32[128,1,256]{2,1,0:T(1,128)S(1)}, u32[]{:S(2)}, u32[]{:S(2)}) %all-to-all-start) | async-done | bytes 131104 | tf_op jit(solution)/shard_map/all_to_all | solution.py:355
  29.0 0.1 broadcast_in_dim.6.place_ref
  29.0 1.6 %shard_map.111 = bf16[2048,128]{1,0:T(8,128)(2,1)} custom-call(s32[2,128]{1,0:T(2,128)S(1)} %broadcast_in_dim.6.place_ref, s32[128,1,256]{2,1,0:T(1,128)S(1)} %all-to-all-done.offs_ref, bf16[256,512]{1,0:T(8,128)(2,1)S(1)} %reshape.50.table_ref), custom_call_target="tpu_custom_call" | custom-call | flops 100000000 | bytes 1048576 | tf_op jit(solution)/shard_map/pallas_call | solution.py:331
  30.6 7.0 %all-to-all-start.1 = ((bf16[128,16,128]{2,1,0:T(8,128)(2,1)}), bf16[128,16,128]{2,1,0:T(8,128)(2,1)S(1)}, u32[]{:S(2)}, u32[]{:S(2)}) async-start(bf16[128,16,128]{2,1,0:T(8,128)(2,1)} %bitcast.4), calls=%async_computation.1 | async-start | bytes 1048576 | tf_op jit(solution)/shard_map/all_to_all | solution.py:372
  38.3 0.0 copy-done.4
  38.3 0.0 copy-start.2
  38.3 0.0 copy-done.1
  38.3 0.0 copy-start
  38.3 1.9 %copy-done = bf16[768,2048]{1,0:T(8,128)(2,1)S(1)} copy-done((bf16[768,2048]{1,0:T(8,128)(2,1)S(1)}, bf16[768,2048]{1,0:T(8,128)(2,1)}, u32[]{:S(2)}) %copy-start) | copy-done | bytes 3145752
  40.2 2.0 %shard_map.112 = (f32[256,2048]{1,0:T(8,128)S(1)}, bf16[256,512]{1,0:T(8,128)(2,1)S(1)}, s32[256,128]{1,0:T(8,128)S(1)}) custom-call(s32[2,128]{1,0:T(2,128)S(1)} %broadcast_in_dim.6.place_ref, s32[1,256]{1,0:T(1,128)S(1)} %get-tuple-element.18.offs_ref, bf16[256,512]{1,0:T(8,128)(2,1)S(1)} %reshape.50.table_ref, bf16[256,256]{1,0:T(8,128)(2,1)S(1)} %reshape.53.state_ref, ...), custom_call_target="tpu_custom_call" | custom-call | flops 1000000000 | bytes 1048576 | tf_op jit(solution)/shard_map/pallas_call | solution.py:331
  42.3 12.9 %all-to-all-done.1 = bf16[128,16,128]{2,1,0:T(8,128)(2,1)S(1)} async-done(((bf16[128,16,128]{2,1,0:T(8,128)(2,1)}), bf16[128,16,128]{2,1,0:T(8,128)(2,1)S(1)}, u32[]{:S(2)}, u32[]{:S(2)}) %all-to-all-start.1) | async-done | bytes 524320 | tf_op jit(solution)/shard_map/all_to_all | solution.py:372
  55.2 0.0 copy-done.2
  55.2 5.8 %shard_map.113 = (f32[4,64]{1,0:T(4,128)}, bf16[320,2048]{1,0:T(8,128)(2,1)S(1)}, bf16[384,256]{1,0:T(8,128)(2,1)S(1)}) custom-call(s32[2,128]{1,0:T(2,128)S(1)} %broadcast_in_dim.6.place_ref, f32[1,128]{1,0:T(1,128)S(1)} %broadcast_in_dim.16.b_out_ref, bf16[2048,128]{1,0:T(8,128)(2,1)S(1)} %bitcast.22, f32[256,2048]{1,0:T(8,128)S(1)} %get-tuple-element.19.base_ref, ...), custom_call_target="tpu_custom_call" | custom-call | flops 2000000000 | bytes 1048576 | tf_op jit(solution)/shard_map/pallas_call | solution.py:331
  61.0 0.1 collective-permute-start
  61.1 3.0 %collective-permute-done.other_ref = bf16[320,2048]{1,0:T(8,128)(2,1)S(1)} collective-permute-done((bf16[320,2048]{1,0:T(8,128)(2,1)S(1)}, bf16[320,2048]{1,0:T(8,128)(2,1)S(1)}, u32[]{:S(2)}, u32[]{:S(2)}) %collective-permute-start) | collective-permute-done | bytes 1310752 | tf_op jit(solution)/shard_map/ppermute | solution.py:386
  64.1 1.0 shard_map.114
  65.1 31.3 %all_to_all.20 = bf16[16,464,128]{2,1,0:T(8,128)(2,1)S(1)} all-to-all(bf16[16,464,128]{2,1,0:T(8,128)(2,1)S(1)} %bitcast.18), channel_id=1, replica_groups=mesh['tm_0'=4,'tm_1'=4,'tm_2'=8,'dp'=2] {'tm_0','tm_1'}, dimensions={0} | all-to-all | bytes 3801088 | tf_op jit(solution)/shard_map/all_to_all | solution.py:395
  96.4 0.3 shard_map.115
  96.7 13.7 %all_to_all.21 = bf16[8,128,128]{2,1,0:T(8,128)(2,1)S(1)} all-to-all(bf16[8,128,128]{2,1,0:T(8,128)(2,1)S(1)} %bitcast.20), channel_id=1, replica_groups=mesh['tm_0'=4,'tm_1'=4,'tm_2'=8,'dp'=2] {'tm_2'}, dimensions={0} | all-to-all | bytes 524288 | tf_op jit(solution)/shard_map/all_to_all | solution.py:406
  110.4 0.7 shard_map.116
  (2 shorter events, 0.0 us)
Async XLA Ops:
  0.6 37.7 %copy-start.1 = (f32[2048]{0:T(1024)S(1)}, f32[2048]{0:T(1024)}, u32[]{:S(2)}) copy-start(f32[2048]{0:T(1024)} %param.11) | copy-start | bytes 24580
  0.6 0.7 copy-start.3
  1.3 36.9 %copy-start.4 = (bf16[64,4,256]{2,1,0:T(4,128)(2,1)S(1)}, bf16[64,4,256]{2,1,0:T(4,128)(2,1)}, u32[]{:S(2)}) copy-start(bf16[64,4,256]{2,1,0:T(4,128)(2,1)} %param.7) | copy-start | bytes 393220
  2.2 26.8 %all-to-all-start = ((s32[128,1,256]{2,1,0:T(1,128)}), s32[128,1,256]{2,1,0:T(1,128)S(1)}, u32[]{:S(2)}, u32[]{:S(2)}) async-start(s32[128,1,256]{2,1,0:T(1,128)} %get-tuple-element.17), calls=%async_computation | async-start | bytes 262144 | tf_op jit(solution)/shard_map/all_to_all | solution.py:355
  30.6 24.6 %all-to-all-start.1 = ((bf16[128,16,128]{2,1,0:T(8,128)(2,1)}), bf16[128,16,128]{2,1,0:T(8,128)(2,1)S(1)}, u32[]{:S(2)}, u32[]{:S(2)}) async-start(bf16[128,16,128]{2,1,0:T(8,128)(2,1)} %bitcast.4), calls=%async_computation.1 | async-start | bytes 1048576 | tf_op jit(solution)/shard_map/all_to_all | solution.py:372
  38.3 16.9 %copy-start.2 = (f32[2048]{0:T(1024)S(1)}, f32[2048]{0:T(1024)}, u32[]{:S(2)}) copy-start(f32[2048]{0:T(1024)} %param.12) | copy-start | bytes 24580
  38.3 1.9 %copy-start = (bf16[768,2048]{1,0:T(8,128)(2,1)S(1)}, bf16[768,2048]{1,0:T(8,128)(2,1)}, u32[]{:S(2)}) copy-start(bf16[768,2048]{1,0:T(8,128)(2,1)} %w_in_ref.3) | copy-start | bytes 9437188
  61.0 3.1 %collective-permute-start = (bf16[320,2048]{1,0:T(8,128)(2,1)S(1)}, bf16[320,2048]{1,0:T(8,128)(2,1)S(1)}, u32[]{:S(2)}, u32[]{:S(2)}) collective-permute-start(bf16[320,2048]{1,0:T(8,128)(2,1)S(1)} %get-tuple-element.23.own_ref), channel_id=1, source_target_pairs={{0,1},{1,0},{2,3},{3,2},{4,5},{5,4},{6,7},{7,6},{8,9},{9,8},{10,11... | collective-permute-start | bytes 3932168 | tf_op jit(solution)/shard_map/ppermute | solution.py:386

commit v6 on v5

--- a/solution.py
+++ b/solution.py
@@ -57,7 +57,7 @@
     many_ref[...] = jnp.broadcast_to(row[None], (N_TM, 1, ROWS))
 
 
-def pick_kernel(place_ref, offs_ref, table_ref, out_ref, wide_ref):
+def pick_kernel(place_ref, offs_ref, table_ref, out_ref, wide_ref, ready_ref, sems):
     me = place_ref[0:1, 0:1]
     offs = offs_ref[...].reshape(N_TM, ROWS)
     peer = iota((N_TM, ROWS), 0)
@@ -67,18 +67,32 @@
     earlier = flag(iota((ROWS, ROWS), 0) < iota((ROWS, ROWS), 1)).astype(BF16)
     rank = dot(flag(hit).astype(BF16), earlier)
     position = ((row - (row & (STEPS - 1))) + (target & (STEPS - 1)) + 1).astype(F32)
-    table = table_ref[...]
+    wanted = []
     for c in range(CAP):
         place = jnp.sum(
             jnp.where(hit & (rank == float(c)), position, 0.0), axis=1, keepdims=True
         )
-        wanted = flag(row.astype(F32) + 1.0 == place).astype(BF16)
-        picked = dot(wanted, table)
-        for j in range(G // LANES):
-            wide_ref[pl.ds(c * (G // LANES) + j, N_TM, stride=16), :] = picked[
-                :, j * LANES : (j + 1) * LANES
-            ]
-    out_ref[...] = wide_ref[...].astype(BF16)
+        wanted.append(flag(row.astype(F32) + 1.0 == place).astype(BF16))
+    half = N_TM // 2
+    copies = []
+    for h in range(2):
+        part = jnp.concatenate([w[h * half : (h + 1) * half] for w in wanted], axis=0)
+        picked = dot(part, table_ref[...])
+        for c in range(CAP):
+            for j in range(G // LANES):
+                at = pl.ds(h * half * 16 + c * (G // LANES) + j, half, stride=16)
+                wide_ref[at, :] = picked[
+                    c * half : (c + 1) * half, j * LANES : (j + 1) * LANES
+                ]
+        rows = slice(h * half * 16, (h + 1) * half * 16)
+        ready_ref[rows, :] = wide_ref[rows, :].astype(BF16)
+        there = pl.ds(h * half * 16, half * 16)
+        copies.append(
+            pltpu.make_async_copy(ready_ref.at[there, :], out_ref.at[there, :], sems.at[h])
+        )
+        copies[-1].start()
+    for copy in copies:
+        copy.wait()
 
 
 def half_rows(core):
@@ -115,10 +129,8 @@
     place_ref,
     offs_ref,
     table_ref,
-    state_ref,
     w_in_ref,
-    b_in_ref,
-    base_ref,
+    goal_w_ref,
     near_ref,
     at_ref,
 ):
@@ -146,14 +158,7 @@
     near = flag(row.astype(F32) == near_at).astype(BF16)
     near_ref[...] = dot(near, table_ref[...]).astype(BF16)
     at_ref[...] = jnp.broadcast_to(far_at, (ROWS, LANES))
-    state = state_ref[...]
-
-    def step(n, carry):
-        at = pl.ds(pl.multiple_of(n * CHUNK, CHUNK), CHUNK)
-        base_ref[:, at] = dot(state, w_in_ref[:S, at]) + b_in_ref[:, at]
-        return carry
-
-    lax.fori_loop(0, H // CHUNK, step, 0)
+    goal_w_ref[...] = w_in_ref[S:, :]
 
 
 def main_kernel(
@@ -161,12 +166,13 @@
     place_ref,
     b_out_ref,
     fetched_ref,
-    base_ref,
+    goal_w_ref,
     near_ref,
     at_ref,
     table_ref,
     state_ref,
     w_in_ref,
+    b_in_ref,
     w_out_ref,
     td_ref,
     send_ref,
@@ -174,19 +180,24 @@
     slope_ref,
     hidden_ref,
     inputs_ref,
-    goal_w_ref,
+    state_w_ref,
     wide_ref,
     total_ref,
+    td_rows_ref,
     sems,
+    td_sem,
 ):
     def load(n):
         at = pl.ds(pl.multiple_of(n * CHUNK, CHUNK), CHUNK)
         return pltpu.make_async_copy(
-            w_in_ref.at[pl.ds(S, G), at], goal_w_ref.at[:, at], sems.at[n]
+            w_in_ref.at[pl.ds(0, S), at], state_w_ref.at[:, at], sems.at[n]
         )
 
-    for n in range(H // CHUNK):
+    def begin(n, carry):
         load(n).start()
+        return carry
+
+    lax.fori_loop(0, H // CHUNK, begin, 0)
     core = place_ref[1:2, 0:1]
     far_at = at_ref[:, 0:1]
     far = flag(iota((ROWS, N_TM * CAP), 1) == far_at).astype(BF16)
@@ -207,7 +218,8 @@
     def forward(n, carry):
         at = pl.ds(pl.multiple_of(n * CHUNK, CHUNK), CHUNK)
         load(n).wait()
-        pre = base_ref[:, at] + dot(inputs[:, S:], goal_w_ref[:, at])
+        pre = dot(inputs[:, :S], state_w_ref[:, at]) + dot(inputs[:, S:], goal_w_ref[:, at])
+        pre = pre + b_in_ref[:, at]
         sig = 1.0 / (1.0 + jnp.exp(-pre))
         head = w_out_ref[:, at]
         act = pre * sig
@@ -225,9 +237,12 @@
 
     each = (STEPS * iota((ROWS, ROWS // STEPS), 1)) - iota((ROWS, ROWS // STEPS), 0)
     for s in range(STEPS):
-        td_ref[s : s + 1, :] = jnp.sum(
+        td_rows_ref[s : s + 1, :] = jnp.sum(
             jnp.where(each + s == 0, error, 0.0), axis=0, keepdims=True
         )
+
+    td_copy = pltpu.make_async_copy(td_rows_ref, td_ref, td_sem)
+    td_copy.start()
 
     kept = dot(half_rows(core), inputs, (((1,), (1,)), ((), ())))
     keep_ref[...] = kept.astype(BF16)
@@ -249,9 +264,10 @@
         return carry
 
     lax.fori_loop(0, H // CHUNK, backward, 0)
-
-
-PACK = 464
+    td_copy.wait()
+
+
+PACK = 432
 BLOCK = 128
 
 
@@ -277,13 +293,12 @@
     for q in range(3):
         a = mine[3 * q : 3 * q + 1] + mine[3 * q + 1 : 3 * q + 2] + mine[3 * q + 2 : 3 * q + 3]
         b = theirs[3 * q : 3 * q + 1] + theirs[3 * q + 1 : 3 * q + 2] + theirs[3 * q + 2 : 3 * q + 3]
-        rows.append(two(a + b))
+        rows.append(a + b)
     blocks = []
-    for q in range(2):
-        for r in rows[q]:
-            pieces = [r[:, b * LANES : (b + 1) * LANES] for b in range(H // LANES)]
-            blocks.append(jnp.concatenate(pieces, axis=0))
-    blocks.append(stack_rows([r[:, :LANES] for r in rows[2]], 16))
+    for r in rows[:2]:
+        pieces = [r[:, b * LANES : (b + 1) * LANES] for b in range(H // LANES)]
+        blocks.append(jnp.concatenate(pieces, axis=0))
+    blocks.append(stack_rows(two(rows[2][:, :LANES]), 16))
     small = jnp.concatenate(blocks, axis=0).astype(BF16)
     for p in range(N_PLANE):
         out_ref[p * PACK + HALF : (p + 1) * PACK, :] = small
@@ -297,11 +312,9 @@
         sum_ref[b * 16 : b * 16 + 16, :] = total
     for n in range(48):
         wide_ref[pl.ds(n, N_LINE, stride=48), :] = sum_ref[8 * n : 8 * n + 8, :]
-    last = sum_ref[448:449, :] + sum_ref[449:450, :]
+    last = sum_ref[416:417, :] + sum_ref[417:418, :]
     small = jnp.concatenate(
-        two(sum_ref[384:400, :] + sum_ref[400:416, :])
-        + two(sum_ref[416:432, :] + sum_ref[432:448, :])
-        + (stack_rows(two(last), 16),),
+        two(sum_ref[384:400, :]) + two(sum_ref[400:416, :]) + (stack_rows(two(last), 16),),
         axis=0,
     ).astype(BF16)
     for z in range(N_LINE):
@@ -323,16 +336,19 @@
     b_out_ref[...] = sum_ref[112:113, :] + sum_ref[113:114, :]
 
 
-def call(kernel, shapes, operands, scratch, flops, grant, in_hbm=()):
+def call(kernel, shapes, operands, scratch, flops, grant, in_hbm=(), out_hbm=()):
     specs = [pl.BlockSpec(memory_space=pltpu.VMEM)] * len(operands)
     for n in in_hbm:
         specs[n] = pl.BlockSpec(memory_space=pltpu.HBM)
+    back = [pl.BlockSpec(memory_space=pltpu.VMEM)] * len(shapes)
+    for n in out_hbm:
+        back[n] = pl.BlockSpec(memory_space=pltpu.HBM)
     outs = [jax.ShapeDtypeStruct(shape, kind) for shape, kind in shapes]
     return pl.pallas_call(
         kernel,
         out_shape=outs,
         in_specs=specs,
-        out_specs=[pl.BlockSpec(memory_space=pltpu.VMEM)] * len(outs),
+        out_specs=back,
         scratch_shapes=scratch,
         compiler_params=pltpu.CompilerParams(vmem_limit_bytes=grant << 20),
         cost_estimate=pl.CostEstimate(flops=flops, bytes_accessed=1 << 20, transcendentals=0),
@@ -357,14 +373,20 @@
         pick_kernel,
         [((N_TM * 16, LANES), BF16)],
         (place, known, table),
-        [pltpu.VMEM((N_TM * 16, LANES), F32)],
+        [
+            pltpu.VMEM((N_TM * 16, LANES), F32),
+            pltpu.VMEM((N_TM * 16, LANES), BF16),
+            pltpu.SemaphoreType.DMA((2,)),
+        ],
         10**8,
-        6,
-    )
-    base, near, at = call(
+        8,
+        (),
+        (0,),
+    )
+    goal_w, near, at = call(
         ahead_kernel,
-        [((ROWS, H), F32), ((ROWS, G), BF16), ((ROWS, LANES), I32)],
-        (place, offs, table, state, w_in, b_in.reshape(1, H)),
+        [((G, H), BF16), ((ROWS, G), BF16), ((ROWS, LANES), I32)],
+        (place, offs, table, w_in),
         [],
         10**9,
         12,
@@ -377,11 +399,34 @@
     td, send, keep = call(
         functools.partial(main_kernel, scale),
         [((STEPS, ROWS // STEPS), F32), ((ROWS + 64, H), BF16), ((HALF, ROWS), BF16)],
-        (place, head_bias, fetched, base, near, at, table, state, w_in, w_out.reshape(1, H)),
-        [pltpu.VMEM((ROWS, H), F32), pltpu.VMEM((ROWS, H), BF16), pltpu.VMEM((ROWS, S + G), BF16), pltpu.VMEM((G, H), BF16), pltpu.VMEM((N_TM * 16, LANES), F32), pltpu.VMEM((ROWS, LANES), F32), pltpu.SemaphoreType.DMA((H // CHUNK,))],
+        (
+            place,
+            head_bias,
+            fetched,
+            goal_w,
+            near,
+            at,
+            table,
+            state,
+            w_in,
+            b_in.reshape(1, H),
+            w_out.reshape(1, H),
+        ),
+        [
+            pltpu.VMEM((ROWS, H), F32),
+            pltpu.VMEM((ROWS, H), BF16),
+            pltpu.VMEM((ROWS, S + G), BF16),
+            pltpu.VMEM((S, H), BF16),
+            pltpu.VMEM((N_TM * 16, LANES), F32),
+            pltpu.VMEM((ROWS, LANES), F32),
+            pltpu.VMEM((STEPS, ROWS // STEPS), F32),
+            pltpu.SemaphoreType.DMA((H // CHUNK,)),
+            pltpu.SemaphoreType.DMA,
+        ],
         2 * 10**9,
         48,
         (8,),
+        (0,),
     )
     other = lax.ppermute(send, "dp", [(0, 1), (1, 0)])
     (packs,) = call(

time: 111 us -> 110 us (level)
  Pallas kernels: 12.2 us -> 10.3 us
  waiting for transfers between devices: 26.2 us -> 27.7 us
    pallas_call x7, Pallas kernels: 12.2 us -> 10.3 us  [call(): pl.pallas_call(kernel, out_shape=outs, in_specs=specs, out_specs=back, sc...]
    all_to_all x1, waiting for transfers between devices: 12.9 us -> 14.4 us  [body(): lax.all_to_all(picked.reshape(N_TM, 16, LANES), TM, split_axis=0, concat_...]
    all_to_all x1, blocking collectives: 31.3 us -> 29.9 us  [body(): lax.all_to_all(packs.reshape(N_PLANE, PACK, LANES), PLANE, split_axis=0,...]
  transfers between devices with their start and end apart: 3 -> 3, of which waited for: 3 -> 3; matrix products, arithmetic and copies ran while one was open for 1% -> 1% of each run, Pallas kernels for 2% -> 1%
where the time goes in v6:
time: 110 us
  blocking collectives  43.9 us (40%)
  waiting for transfers between devices  27.7 us (25%)
  starting transfers between devices  22.5 us (20%)
  Pallas kernels  10.3 us (9%)
  local copies, waits for them, and re-layouts  3.7 us (3%)
  between operations  1.39 us (1%)
    all_to_all x1, blocking collectives, body(): lax.all_to_all(packs.reshape(N_PLANE, PACK, LANES), PLANE, split_axis=0,...  29.9 us
    all_to_all x1, starting transfers between devices, body(): known = lax.all_to_all(many, TM, split_axis=0, concat_axis=0, tiled=True)  15.4 us
    all_to_all x1, waiting for transfers between devices, body(): lax.all_to_all(picked.reshape(N_TM, 16, LANES), TM, split_axis=0, concat_...  14.4 us
    all_to_all x1, blocking collectives, body(): lax.all_to_all(lines.reshape(N_LINE, BLOCK, LANES), LINE, split_axis=0, c...  14 us
    pallas_call x7, Pallas kernels, call(): pl.pallas_call(kernel, out_shape=outs, in_specs=specs, out_specs=back, sc...  10.3 us
    all_to_all x1, waiting for transfers between devices, body(): known = lax.all_to_all(many, TM, split_axis=0, concat_axis=0, tiled=True)  10.2 us
    all_to_all x1, starting transfers between devices, body(): lax.all_to_all(picked.reshape(N_TM, 16, LANES), TM, split_axis=0, concat_...  7.01 us
    ppermute x1, waiting for transfers between devices, body(): other = lax.ppermute(send, 'dp', [(0, 1), (1, 0)])  3.02 us
  transfers between devices with their start and end apart: 3, of which 3 were waited for; matrix products, arithmetic and copies ran while one was open for 1% of the time, Pallas kernels for 1%

profile of v6, /device:TPU:2, one launch (start us, length us, event | category | flops | bytes accessed | tf_op | source)
XLA Modules:
  0.0 109.6 jit_solution(12890744181444903586)
XLA Ops:
  0.6 0.0 copy-start.3
  0.6 0.7 copy-done.3
  1.3 0.0 copy-start.4
  1.3 0.8 shard_map.110
  2.1 15.4 %all-to-all-start = ((s32[128,1,256]{2,1,0:T(1,128)}), s32[128,1,256]{2,1,0:T(1,128)S(1)}, u32[]{:S(2)}, u32[]{:S(2)}) async-start(s32[128,1,256]{2,1,0:T(1,128)} %get-tuple-element.17), calls=%async_computation | async-start | bytes 262144 | tf_op jit(solution)/shard_map/all_to_all | solution.py:371
  17.6 1.0 reshape.50.table_ref
  18.6 0.1 pad_add_fusion
  18.7 10.2 %all-to-all-done.offs_ref = s32[128,1,256]{2,1,0:T(1,128)S(1)} async-done(((s32[128,1,256]{2,1,0:T(1,128)}), s32[128,1,256]{2,1,0:T(1,128)S(1)}, u32[]{:S(2)}, u32[]{:S(2)}) %all-to-all-start) | async-done | bytes 131104 | tf_op jit(solution)/shard_map/all_to_all | solution.py:371
  28.9 0.1 broadcast_in_dim.6.place_ref
  29.0 1.5 %shard_map.111 = bf16[2048,128]{1,0:T(8,128)(2,1)} custom-call(s32[2,128]{1,0:T(2,128)S(1)} %broadcast_in_dim.6.place_ref, s32[128,1,256]{2,1,0:T(1,128)S(1)} %all-to-all-done.offs_ref, bf16[256,512]{1,0:T(8,128)(2,1)S(1)} %reshape.50.table_ref), custom_call_target="tpu_custom_call" | custom-call | flops 100000000 | bytes 1048576 | tf_op jit(solution)/shard_map/pallas_call | solution.py:347
  30.5 7.0 %all-to-all-start.1 = ((bf16[128,16,128]{2,1,0:T(8,128)(2,1)}), bf16[128,16,128]{2,1,0:T(8,128)(2,1)S(1)}, u32[]{:S(2)}, u32[]{:S(2)}) async-start(bf16[128,16,128]{2,1,0:T(8,128)(2,1)} %bitcast.4), calls=%async_computation.1 | async-start | bytes 1048576 | tf_op jit(solution)/shard_map/all_to_all | solution.py:394
  38.1 0.0 copy-done.4
  38.2 0.0 copy-start
  38.2 1.9 %copy-done = bf16[768,2048]{1,0:T(8,128)(2,1)S(1)} copy-done((bf16[768,2048]{1,0:T(8,128)(2,1)S(1)}, bf16[768,2048]{1,0:T(8,128)(2,1)}, u32[]{:S(2)}) %copy-start) | copy-done | bytes 3145752
  40.1 0.0 copy-start.1
  40.1 0.0 copy-start.2
  40.1 0.6 shard_map.112
  40.7 14.4 %all-to-all-done.1 = bf16[128,16,128]{2,1,0:T(8,128)(2,1)S(1)} async-done(((bf16[128,16,128]{2,1,0:T(8,128)(2,1)}), bf16[128,16,128]{2,1,0:T(8,128)(2,1)S(1)}, u32[]{:S(2)}, u32[]{:S(2)}) %all-to-all-start.1) | async-done | bytes 524320 | tf_op jit(solution)/shard_map/all_to_all | solution.py:394
  55.1 0.0 copy-done.1
  55.1 0.0 copy-done.2
  55.1 5.5 %shard_map.113 = (f32[4,64]{1,0:T(4,128)}, bf16[320,2048]{1,0:T(8,128)(2,1)S(1)}, bf16[384,256]{1,0:T(8,128)(2,1)S(1)}) custom-call(s32[2,128]{1,0:T(2,128)S(1)} %broadcast_in_dim.6.place_ref, f32[1,128]{1,0:T(1,128)S(1)} %broadcast_in_dim.16.b_out_ref, bf16[2048,128]{1,0:T(8,128)(2,1)S(1)} %bitcast.22, bf16[512,2048]{1,0:T(8,128)(2,1)S(1)} %get-tuple-element.19.goal_w_ref, ...), custom_call_target="tpu_custom_call" | custom-call | flops 2000000000 | bytes 1048576 | tf_op jit(solution)/shard_map/pallas_call | solution.py:347
  60.6 0.1 collective-permute-start
  60.7 3.0 %collective-permute-done.other_ref = bf16[320,2048]{1,0:T(8,128)(2,1)S(1)} collective-permute-done((bf16[320,2048]{1,0:T(8,128)(2,1)S(1)}, bf16[320,2048]{1,0:T(8,128)(2,1)S(1)}, u32[]{:S(2)}, u32[]{:S(2)}) %collective-permute-start) | collective-permute-done | bytes 1310752 | tf_op jit(solution)/shard_map/ppermute | solution.py:431
  63.7 1.0 shard_map.114
  64.7 29.9 %all_to_all.20 = bf16[16,432,128]{2,1,0:T(8,128)(2,1)S(1)} all-to-all(bf16[16,432,128]{2,1,0:T(8,128)(2,1)S(1)} %bitcast.18), channel_id=1, replica_groups=mesh['tm_0'=4,'tm_1'=4,'tm_2'=8,'dp'=2] {'tm_0','tm_1'}, dimensions={0} | all-to-all | bytes 3538944 | tf_op jit(solution)/shard_map/all_to_all | solution.py:440
  94.6 0.3 shard_map.115
  94.9 14.0 %all_to_all.21 = bf16[8,128,128]{2,1,0:T(8,128)(2,1)S(1)} all-to-all(bf16[8,128,128]{2,1,0:T(8,128)(2,1)S(1)} %bitcast.21), channel_id=1, replica_groups=mesh['tm_0'=4,'tm_1'=4,'tm_2'=8,'dp'=2] {'tm_2'}, dimensions={0} | all-to-all | bytes 524288 | tf_op jit(solution)/shard_map/all_to_all | solution.py:451
  108.9 0.7 shard_map.116
  (2 shorter events, 0.0 us)
Async XLA Ops:
  0.6 0.7 copy-start.3
  1.3 36.8 %copy-start.4 = (bf16[64,4,256]{2,1,0:T(4,128)(2,1)S(1)}, bf16[64,4,256]{2,1,0:T(4,128)(2,1)}, u32[]{:S(2)}) copy-start(bf16[64,4,256]{2,1,0:T(4,128)(2,1)} %param.7) | copy-start | bytes 393220
  2.1 26.8 %all-to-all-start = ((s32[128,1,256]{2,1,0:T(1,128)}), s32[128,1,256]{2,1,0:T(1,128)S(1)}, u32[]{:S(2)}, u32[]{:S(2)}) async-start(s32[128,1,256]{2,1,0:T(1,128)} %get-tuple-element.17), calls=%async_computation | async-start | bytes 262144 | tf_op jit(solution)/shard_map/all_to_all | solution.py:371
  30.5 24.6 %all-to-all-start.1 = ((bf16[128,16,128]{2,1,0:T(8,128)(2,1)}), bf16[128,16,128]{2,1,0:T(8,128)(2,1)S(1)}, u32[]{:S(2)}, u32[]{:S(2)}) async-start(bf16[128,16,128]{2,1,0:T(8,128)(2,1)} %bitcast.4), calls=%async_computation.1 | async-start | bytes 1048576 | tf_op jit(solution)/shard_map/all_to_all | solution.py:394
  38.2 1.9 %copy-start = (bf16[768,2048]{1,0:T(8,128)(2,1)S(1)}, bf16[768,2048]{1,0:T(8,128)(2,1)}, u32[]{:S(2)}) copy-start(bf16[768,2048]{1,0:T(8,128)(2,1)} %w_in_ref.3) | copy-start | bytes 9437188
  40.1 15.0 %copy-start.1 = (f32[2048]{0:T(1024)S(1)}, f32[2048]{0:T(1024)}, u32[]{:S(2)}) copy-start(f32[2048]{0:T(1024)} %param.11) | copy-start | bytes 24580
  40.1 15.0 %copy-start.2 = (f32[2048]{0:T(1024)S(1)}, f32[2048]{0:T(1024)}, u32[]{:S(2)}) copy-start(f32[2048]{0:T(1024)} %param.12) | copy-start | bytes 24580
  60.6 3.1 %collective-permute-start = (bf16[320,2048]{1,0:T(8,128)(2,1)S(1)}, bf16[320,2048]{1,0:T(8,128)(2,1)S(1)}, u32[]{:S(2)}, u32[]{:S(2)}) collective-permute-start(bf16[320,2048]{1,0:T(8,128)(2,1)S(1)} %get-tuple-element.23.own_ref), channel_id=1, source_target_pairs={{0,1},{1,0},{2,3},{3,2},{4,5},{5,4},{6,7},{7,6},{8,9},{9,8},{10,11... | collective-permute-start | bytes 3932168 | tf_op jit(solution)/shard_map/ppermute | solution.py:431

commit v7 on v6

--- a/solution.py
+++ b/solution.py
@@ -213,6 +213,13 @@
         inputs_ref[:, S + j * LANES : S + (j + 1) * LANES] = goal.astype(BF16)
     reward = -(jnp.sum(gap, axis=1, keepdims=True) * (1.0 / G))
     inputs = inputs_ref[...]
+
+    kept = dot(half_rows(core), inputs, (((1,), (1,)), ((), ())))
+    keep_ref[...] = kept.astype(BF16)
+    sent = dot(half_rows(1 - core), inputs, (((1,), (1,)), ((), ()))).astype(BF16)
+    for b in range(H // ROWS):
+        send_ref[ROWS : ROWS + 48, b * ROWS : (b + 1) * ROWS] = sent[b * 48 : (b + 1) * 48, :]
+
     total_ref[...] = jnp.zeros((ROWS, LANES), F32)
 
     def forward(n, carry):
@@ -244,12 +251,6 @@
     td_copy = pltpu.make_async_copy(td_rows_ref, td_ref, td_sem)
     td_copy.start()
 
-    kept = dot(half_rows(core), inputs, (((1,), (1,)), ((), ())))
-    keep_ref[...] = kept.astype(BF16)
-    sent = dot(half_rows(1 - core), inputs, (((1,), (1,)), ((), ()))).astype(BF16)
-    for b in range(H // ROWS):
-        send_ref[ROWS : ROWS + 48, b * ROWS : (b + 1) * ROWS] = sent[b * 48 : (b + 1) * 48, :]
-
     total_value = jnp.sum(grad_value, axis=0, keepdims=True)
 
     def backward(n, carry):
@@ -268,7 +269,7 @@
 
 
 PACK = 432
-BLOCK = 128
+BLOCK = 96
 
 
 def product_kernel(own_ref, other_ref, keep_ref, out_ref, left_ref):
@@ -314,7 +315,7 @@
         wide_ref[pl.ds(n, N_LINE, stride=48), :] = sum_ref[8 * n : 8 * n + 8, :]
     last = sum_ref[416:417, :] + sum_ref[417:418, :]
     small = jnp.concatenate(
-        two(sum_ref[384:400, :]) + two(sum_ref[400:416, :]) + (stack_rows(two(last), 16),),
+        (sum_ref[384:416, :], stack_rows(two(last), 16)),
         axis=0,
     ).astype(BF16)
     for z in range(N_LINE):
@@ -331,9 +332,9 @@
     for i in range(3):
         for b in range(H // LANES):
             w_ref[i : i + 1, b * LANES : (b + 1) * LANES] = sum_ref[i * 16 + b : i * 16 + b + 1, :]
-    b_in_ref[...] = sum_ref[48:64, :] + sum_ref[64:80, :]
-    w_out_ref[...] = sum_ref[80:96, :] + sum_ref[96:112, :]
-    b_out_ref[...] = sum_ref[112:113, :] + sum_ref[113:114, :]
+    b_in_ref[...] = sum_ref[48:64, :]
+    w_out_ref[...] = sum_ref[64:80, :]
+    b_out_ref[...] = sum_ref[80:81, :] + sum_ref[81:82, :]
 
 
 def call(kernel, shapes, operands, scratch, flops, grant, in_hbm=(), out_hbm=()):

time: 110 us -> 108 us (0.982)
  blocking collectives: 43.9 us -> 42.5 us
    all_to_all x1, blocking collectives: 14 us -> 12.6 us  [body(): lax.all_to_all(lines.reshape(N_LINE, BLOCK, LANES), LINE, split_axis=0, c...]
where the time goes in v7:
time: 108 us
  blocking collectives  42.5 us (39%)
  waiting for transfers between devices  27.7 us (26%)
  starting transfers between devices  22.5 us (21%)
  Pallas kernels  10.1 us (9%)
  local copies, waits for them, and re-layouts  3.7 us (3%)
  between operations  1.39 us (1%)
    all_to_all x1, blocking collectives, body(): lax.all_to_all(packs.reshape(N_PLANE, PACK, LANES), PLANE, split_axis=0,...  29.9 us
    all_to_all x1, starting transfers between devices, body(): known = lax.all_to_all(many, TM, split_axis=0, concat_axis=0, tiled=True)  15.4 us
    all_to_all x1, waiting for transfers between devices, body(): lax.all_to_all(picked.reshape(N_TM, 16, LANES), TM, split_axis=0, concat_...  14.4 us
    all_to_all x1, blocking collectives, body(): lax.all_to_all(lines.reshape(N_LINE, BLOCK, LANES), LINE, split_axis=0, c...  12.6 us
    all_to_all x1, waiting for transfers between devices, body(): known = lax.all_to_all(many, TM, split_axis=0, concat_axis=0, tiled=True)  10.2 us
    pallas_call x7, Pallas kernels, call(): pl.pallas_call(kernel, out_shape=outs, in_specs=specs, out_specs=back, sc...  10.1 us
    all_to_all x1, starting transfers between devices, body(): lax.all_to_all(picked.reshape(N_TM, 16, LANES), TM, split_axis=0, concat_...  7.01 us
    ppermute x1, waiting for transfers between devices, body(): other = lax.ppermute(send, 'dp', [(0, 1), (1, 0)])  3.02 us
  transfers between devices with their start and end apart: 3, of which 3 were waited for; matrix products, arithmetic and copies ran while one was open for 1% of the time, Pallas kernels for 1%

profile of v7, /device:TPU:2, one launch (start us, length us, event | category | flops | bytes accessed | tf_op | source)
XLA Modules:
  0.0 107.9 jit_solution(1128498500639915932)
XLA Ops:
  0.6 0.0 copy-start.3
  0.6 0.7 copy-done.3
  1.3 0.0 copy-start.4
  1.3 0.8 shard_map.110
  2.1 15.4 %all-to-all-start = ((s32[128,1,256]{2,1,0:T(1,128)}), s32[128,1,256]{2,1,0:T(1,128)S(1)}, u32[]{:S(2)}, u32[]{:S(2)}) async-start(s32[128,1,256]{2,1,0:T(1,128)} %get-tuple-element.17), calls=%async_computation | async-start | bytes 262144 | tf_op jit(solution)/shard_map/all_to_all | solution.py:372
  17.6 1.0 reshape.50.table_ref
  18.6 0.1 pad_add_fusion
  18.7 10.2 %all-to-all-done.offs_ref = s32[128,1,256]{2,1,0:T(1,128)S(1)} async-done(((s32[128,1,256]{2,1,0:T(1,128)}), s32[128,1,256]{2,1,0:T(1,128)S(1)}, u32[]{:S(2)}, u32[]{:S(2)}) %all-to-all-start) | async-done | bytes 131104 | tf_op jit(solution)/shard_map/all_to_all | solution.py:372
  28.9 0.1 broadcast_in_dim.6.place_ref
  29.0 1.5 %shard_map.111 = bf16[2048,128]{1,0:T(8,128)(2,1)} custom-call(s32[2,128]{1,0:T(2,128)S(1)} %broadcast_in_dim.6.place_ref, s32[128,1,256]{2,1,0:T(1,128)S(1)} %all-to-all-done.offs_ref, bf16[256,512]{1,0:T(8,128)(2,1)S(1)} %reshape.50.table_ref), custom_call_target="tpu_custom_call" | custom-call | flops 100000000 | bytes 1048576 | tf_op jit(solution)/shard_map/pallas_call | solution.py:348
  30.5 7.0 %all-to-all-start.1 = ((bf16[128,16,128]{2,1,0:T(8,128)(2,1)}), bf16[128,16,128]{2,1,0:T(8,128)(2,1)S(1)}, u32[]{:S(2)}, u32[]{:S(2)}) async-start(bf16[128,16,128]{2,1,0:T(8,128)(2,1)} %bitcast.4), calls=%async_computation.1 | async-start | bytes 1048576 | tf_op jit(solution)/shard_map/all_to_all | solution.py:395
  38.1 0.0 copy-done.4
  38.2 0.0 copy-start
  38.2 1.9 %copy-done = bf16[768,2048]{1,0:T(8,128)(2,1)S(1)} copy-done((bf16[768,2048]{1,0:T(8,128)(2,1)S(1)}, bf16[768,2048]{1,0:T(8,128)(2,1)}, u32[]{:S(2)}) %copy-start) | copy-done | bytes 3145752
  40.1 0.0 copy-start.1
  40.1 0.0 copy-start.2
  40.1 0.6 shard_map.112
  40.7 14.4 %all-to-all-done.1 = bf16[128,16,128]{2,1,0:T(8,128)(2,1)S(1)} async-done(((bf16[128,16,128]{2,1,0:T(8,128)(2,1)}), bf16[128,16,128]{2,1,0:T(8,128)(2,1)S(1)}, u32[]{:S(2)}, u32[]{:S(2)}) %all-to-all-start.1) | async-done | bytes 524320 | tf_op jit(solution)/shard_map/all_to_all | solution.py:395
  55.1 0.0 copy-done.1
  55.1 0.0 copy-done.2
  55.1 5.3 %shard_map.113 = (f32[4,64]{1,0:T(4,128)}, bf16[320,2048]{1,0:T(8,128)(2,1)S(1)}, bf16[384,256]{1,0:T(8,128)(2,1)S(1)}) custom-call(s32[2,128]{1,0:T(2,128)S(1)} %broadcast_in_dim.6.place_ref, f32[1,128]{1,0:T(1,128)S(1)} %broadcast_in_dim.16.b_out_ref, bf16[2048,128]{1,0:T(8,128)(2,1)S(1)} %bitcast.22, bf16[512,2048]{1,0:T(8,128)(2,1)S(1)} %get-tuple-element.19.goal_w_ref, ...), custom_call_target="tpu_custom_call" | custom-call | flops 2000000000 | bytes 1048576 | tf_op jit(solution)/shard_map/pallas_call | solution.py:348
  60.4 0.1 collective-permute-start
  60.5 3.0 %collective-permute-done.other_ref = bf16[320,2048]{1,0:T(8,128)(2,1)S(1)} collective-permute-done((bf16[320,2048]{1,0:T(8,128)(2,1)S(1)}, bf16[320,2048]{1,0:T(8,128)(2,1)S(1)}, u32[]{:S(2)}, u32[]{:S(2)}) %collective-permute-start) | collective-permute-done | bytes 1310752 | tf_op jit(solution)/shard_map/ppermute | solution.py:432
  63.5 1.0 shard_map.114
  64.5 29.9 %all_to_all.20 = bf16[16,432,128]{2,1,0:T(8,128)(2,1)S(1)} all-to-all(bf16[16,432,128]{2,1,0:T(8,128)(2,1)S(1)} %bitcast.18), channel_id=1, replica_groups=mesh['tm_0'=4,'tm_1'=4,'tm_2'=8,'dp'=2] {'tm_0','tm_1'}, dimensions={0} | all-to-all | bytes 3538944 | tf_op jit(solution)/shard_map/all_to_all | solution.py:441
  94.4 0.3 shard_map.115
  94.7 12.6 %all_to_all.21 = bf16[8,96,128]{2,1,0:T(8,128)(2,1)S(1)} all-to-all(bf16[8,96,128]{2,1,0:T(8,128)(2,1)S(1)} %bitcast.21), channel_id=1, replica_groups=mesh['tm_0'=4,'tm_1'=4,'tm_2'=8,'dp'=2] {'tm_2'}, dimensions={0} | all-to-all | bytes 393216 | tf_op jit(solution)/shard_map/all_to_all | solution.py:452
  107.3 0.7 shard_map.116
  (2 shorter events, 0.0 us)
Async XLA Ops:
  0.6 0.7 copy-start.3
  1.3 36.8 %copy-start.4 = (bf16[64,4,256]{2,1,0:T(4,128)(2,1)S(1)}, bf16[64,4,256]{2,1,0:T(4,128)(2,1)}, u32[]{:S(2)}) copy-start(bf16[64,4,256]{2,1,0:T(4,128)(2,1)} %param.7) | copy-start | bytes 393220
  2.1 26.8 %all-to-all-start = ((s32[128,1,256]{2,1,0:T(1,128)}), s32[128,1,256]{2,1,0:T(1,128)S(1)}, u32[]{:S(2)}, u32[]{:S(2)}) async-start(s32[128,1,256]{2,1,0:T(1,128)} %get-tuple-element.17), calls=%async_computation | async-start | bytes 262144 | tf_op jit(solution)/shard_map/all_to_all | solution.py:372
  30.5 24.6 %all-to-all-start.1 = ((bf16[128,16,128]{2,1,0:T(8,128)(2,1)}), bf16[128,16,128]{2,1,0:T(8,128)(2,1)S(1)}, u32[]{:S(2)}, u32[]{:S(2)}) async-start(bf16[128,16,128]{2,1,0:T(8,128)(2,1)} %bitcast.4), calls=%async_computation.1 | async-start | bytes 1048576 | tf_op jit(solution)/shard_map/all_to_all | solution.py:395
  38.2 1.9 %copy-start = (bf16[768,2048]{1,0:T(8,128)(2,1)S(1)}, bf16[768,2048]{1,0:T(8,128)(2,1)}, u32[]{:S(2)}) copy-start(bf16[768,2048]{1,0:T(8,128)(2,1)} %w_in_ref.3) | copy-start | bytes 9437188
  40.1 15.0 %copy-start.1 = (f32[2048]{0:T(1024)S(1)}, f32[2048]{0:T(1024)}, u32[]{:S(2)}) copy-start(f32[2048]{0:T(1024)} %param.11) | copy-start | bytes 24580
  40.1 15.0 %copy-start.2 = (f32[2048]{0:T(1024)S(1)}, f32[2048]{0:T(1024)}, u32[]{:S(2)}) copy-start(f32[2048]{0:T(1024)} %param.12) | copy-start | bytes 24580
  60.4 3.1 %collective-permute-start = (bf16[320,2048]{1,0:T(8,128)(2,1)S(1)}, bf16[320,2048]{1,0:T(8,128)(2,1)S(1)}, u32[]{:S(2)}, u32[]{:S(2)}) collective-permute-start(bf16[320,2048]{1,0:T(8,128)(2,1)S(1)} %get-tuple-element.23.own_ref), channel_id=1, source_target_pairs={{0,1},{1,0},{2,3},{3,2},{4,5},{5,4},{6,7},{7,6},{8,9},{9,8},{10,11... | collective-permute-start | bytes 3932168 | tf_op jit(solution)/shard_map/ppermute | solution.py:432

commit v8 on v7

--- a/solution.py
+++ b/solution.py
@@ -268,8 +268,8 @@
     td_copy.wait()
 
 
-PACK = 432
-BLOCK = 96
+PACK = 424
+BLOCK = 88
 
 
 def product_kernel(own_ref, other_ref, keep_ref, out_ref, left_ref):
@@ -299,23 +299,23 @@
     for r in rows[:2]:
         pieces = [r[:, b * LANES : (b + 1) * LANES] for b in range(H // LANES)]
         blocks.append(jnp.concatenate(pieces, axis=0))
-    blocks.append(stack_rows(two(rows[2][:, :LANES]), 16))
+    blocks.append(stack_rows(two(rows[2][:, :LANES]), 8))
     small = jnp.concatenate(blocks, axis=0).astype(BF16)
     for p in range(N_PLANE):
         out_ref[p * PACK + HALF : (p + 1) * PACK, :] = small
 
 
 def plane_kernel(got_ref, out_ref, sum_ref, wide_ref):
-    for b in range(PACK // 16):
-        total = got_ref[b * 16 : b * 16 + 16, :].astype(F32)
+    for b in range(PACK // 8):
+        total = got_ref[b * 8 : b * 8 + 8, :].astype(F32)
         for p in range(1, N_PLANE):
-            total = total + got_ref[p * PACK + b * 16 : p * PACK + b * 16 + 16, :].astype(F32)
-        sum_ref[b * 16 : b * 16 + 16, :] = total
+            total = total + got_ref[p * PACK + b * 8 : p * PACK + b * 8 + 8, :].astype(F32)
+        sum_ref[b * 8 : b * 8 + 8, :] = total
     for n in range(48):
         wide_ref[pl.ds(n, N_LINE, stride=48), :] = sum_ref[8 * n : 8 * n + 8, :]
     last = sum_ref[416:417, :] + sum_ref[417:418, :]
     small = jnp.concatenate(
-        (sum_ref[384:416, :], stack_rows(two(last), 16)),
+        (sum_ref[384:416, :], stack_rows(two(last), 8)),
         axis=0,
     ).astype(BF16)
     for z in range(N_LINE):
@@ -324,11 +324,11 @@
 
 
 def line_kernel(got_ref, w_ref, b_in_ref, w_out_ref, b_out_ref, sum_ref):
-    for b in range(BLOCK // 16):
-        total = got_ref[b * 16 : b * 16 + 16, :].astype(F32)
+    for b in range(BLOCK // 8):
+        total = got_ref[b * 8 : b * 8 + 8, :].astype(F32)
         for z in range(1, N_LINE):
-            total = total + got_ref[z * BLOCK + b * 16 : z * BLOCK + b * 16 + 16, :].astype(F32)
-        sum_ref[b * 16 : b * 16 + 16, :] = total
+            total = total + got_ref[z * BLOCK + b * 8 : z * BLOCK + b * 8 + 8, :].astype(F32)
+        sum_ref[b * 8 : b * 8 + 8, :] = total
     for i in range(3):
         for b in range(H // LANES):
             w_ref[i : i + 1, b * LANES : (b + 1) * LANES] = sum_ref[i * 16 + b : i * 16 + b + 1, :]
@@ -367,7 +367,7 @@
         (offsets.T,),
         [],
         10**6,
-        4,
+        60,
     )
     known = lax.all_to_all(many, TM, split_axis=0, concat_axis=0, tiled=True)
     (picked,) = call(

time: 108 us -> 108 us (level)
  no operation moved by 1% of the time
where the time goes in v8:
time: 108 us; the launch traced here: 107 us
  blocking collectives  41.8 us (39%)
  waiting for transfers between devices  27.7 us (26%)
  starting transfers between devices  22.7 us (21%)
  Pallas kernels  10.8 us (10%)
  local copies, waits for them, and re-layouts  3.03 us (3%)
  between operations  1.4 us (1%)
    all_to_all x1, blocking collectives, body(): lax.all_to_all(packs.reshape(N_PLANE, PACK, LANES), PLANE, split_axis=0,...  29.5 us
    all_to_all x1, starting transfers between devices, body(): known = lax.all_to_all(many, TM, split_axis=0, concat_axis=0, tiled=True)  15.6 us
    all_to_all x1, waiting for transfers between devices, body(): lax.all_to_all(picked.reshape(N_TM, 16, LANES), TM, split_axis=0, concat_...  14.4 us
    all_to_all x1, blocking collectives, body(): lax.all_to_all(lines.reshape(N_LINE, BLOCK, LANES), LINE, split_axis=0, c...  12.2 us
    pallas_call x7, Pallas kernels, call(): pl.pallas_call(kernel, out_shape=outs, in_specs=specs, out_specs=back, sc...  10.8 us
    all_to_all x1, waiting for transfers between devices, body(): known = lax.all_to_all(many, TM, split_axis=0, concat_axis=0, tiled=True)  10.2 us
    all_to_all x1, starting transfers between devices, body(): lax.all_to_all(picked.reshape(N_TM, 16, LANES), TM, split_axis=0, concat_...  7.01 us
    ppermute x1, waiting for transfers between devices, body(): other = lax.ppermute(send, 'dp', [(0, 1), (1, 0)])  3.02 us
  transfers between devices with their start and end apart: 3, of which 3 were waited for; matrix products, arithmetic and copies ran while one was open for 1% of the time, Pallas kernels for 1%

profile of v8, /device:TPU:2, one launch (start us, length us, event | category | flops | bytes accessed | tf_op | source)
XLA Modules:
  0.0 107.4 jit_solution(8391804482532577098)
XLA Ops:
  0.6 0.0 copy-start.4
  0.6 1.5 %shard_map.110 = (s32[128,1,256]{2,1,0:T(1,128)}, s32[1,256]{1,0:T(1,128)}) custom-call(s32[4,64]{1,0:T(4,128)} %bitcast.27), custom_call_target="tpu_custom_call" | custom-call | flops 1000000 | bytes 1048576 | tf_op jit(solution)/shard_map/pallas_call | solution.py:348
  2.2 0.0 copy-start.3
  2.2 15.6 %all-to-all-start = ((s32[128,1,256]{2,1,0:T(1,128)}), s32[128,1,256]{2,1,0:T(1,128)S(1)}, u32[]{:S(2)}, u32[]{:S(2)}) async-start(s32[128,1,256]{2,1,0:T(1,128)} %get-tuple-element.17), calls=%async_computation | async-start | bytes 262144 | tf_op jit(solution)/shard_map/all_to_all | solution.py:372
  17.8 1.0 reshape.50.table_ref
  18.8 0.1 pad_add_fusion
  18.9 10.2 %all-to-all-done.offs_ref = s32[128,1,256]{2,1,0:T(1,128)S(1)} async-done(((s32[128,1,256]{2,1,0:T(1,128)}), s32[128,1,256]{2,1,0:T(1,128)S(1)}, u32[]{:S(2)}, u32[]{:S(2)}) %all-to-all-start) | async-done | bytes 131104 | tf_op jit(solution)/shard_map/all_to_all | solution.py:372
  29.1 0.1 broadcast_in_dim.6.place_ref
  29.2 1.5 %shard_map.111 = bf16[2048,128]{1,0:T(8,128)(2,1)} custom-call(s32[2,128]{1,0:T(2,128)S(1)} %broadcast_in_dim.6.place_ref, s32[128,1,256]{2,1,0:T(1,128)S(1)} %all-to-all-done.offs_ref, bf16[256,512]{1,0:T(8,128)(2,1)S(1)} %reshape.50.table_ref), custom_call_target="tpu_custom_call" | custom-call | flops 100000000 | bytes 1048576 | tf_op jit(solution)/shard_map/pallas_call | solution.py:348
  30.7 7.0 %all-to-all-start.1 = ((bf16[128,16,128]{2,1,0:T(8,128)(2,1)}), bf16[128,16,128]{2,1,0:T(8,128)(2,1)S(1)}, u32[]{:S(2)}, u32[]{:S(2)}) async-start(bf16[128,16,128]{2,1,0:T(8,128)(2,1)} %bitcast.4), calls=%async_computation.1 | async-start | bytes 1048576 | tf_op jit(solution)/shard_map/all_to_all | solution.py:395
  38.3 0.0 copy-done.4
  38.4 0.0 copy-done.3
  38.4 0.0 copy-start
  38.4 1.9 %copy-done = bf16[768,2048]{1,0:T(8,128)(2,1)S(1)} copy-done((bf16[768,2048]{1,0:T(8,128)(2,1)S(1)}, bf16[768,2048]{1,0:T(8,128)(2,1)}, u32[]{:S(2)}) %copy-start) | copy-done | bytes 3145752
  40.3 0.0 copy-start.1
  40.3 0.0 copy-start.2
  40.3 0.6 shard_map.112
  40.9 14.4 %all-to-all-done.1 = bf16[128,16,128]{2,1,0:T(8,128)(2,1)S(1)} async-done(((bf16[128,16,128]{2,1,0:T(8,128)(2,1)}), bf16[128,16,128]{2,1,0:T(8,128)(2,1)S(1)}, u32[]{:S(2)}, u32[]{:S(2)}) %all-to-all-start.1) | async-done | bytes 524320 | tf_op jit(solution)/shard_map/all_to_all | solution.py:395
  55.3 0.0 copy-done.1
  55.3 0.0 copy-done.2
  55.3 5.3 %shard_map.113 = (f32[4,64]{1,0:T(4,128)}, bf16[320,2048]{1,0:T(8,128)(2,1)S(1)}, bf16[384,256]{1,0:T(8,128)(2,1)S(1)}) custom-call(s32[2,128]{1,0:T(2,128)S(1)} %broadcast_in_dim.6.place_ref, f32[1,128]{1,0:T(1,128)S(1)} %broadcast_in_dim.16.b_out_ref, bf16[2048,128]{1,0:T(8,128)(2,1)S(1)} %bitcast.22, bf16[512,2048]{1,0:T(8,128)(2,1)S(1)} %get-tuple-element.19.goal_w_ref, ...), custom_call_target="tpu_custom_call" | custom-call | flops 2000000000 | bytes 1048576 | tf_op jit(solution)/shard_map/pallas_call | solution.py:348
  60.6 0.1 collective-permute-start
  60.7 3.0 %collective-permute-done.other_ref = bf16[320,2048]{1,0:T(8,128)(2,1)S(1)} collective-permute-done((bf16[320,2048]{1,0:T(8,128)(2,1)S(1)}, bf16[320,2048]{1,0:T(8,128)(2,1)S(1)}, u32[]{:S(2)}, u32[]{:S(2)}) %collective-permute-start) | collective-permute-done | bytes 1310752 | tf_op jit(solution)/shard_map/ppermute | solution.py:432
  63.7 1.0 shard_map.114
  64.7 29.5 %all_to_all.20 = bf16[16,424,128]{2,1,0:T(8,128)(2,1)S(1)} all-to-all(bf16[16,424,128]{2,1,0:T(8,128)(2,1)S(1)} %bitcast.18), channel_id=1, replica_groups=mesh['tm_0'=4,'tm_1'=4,'tm_2'=8,'dp'=2] {'tm_0','tm_1'}, dimensions={0} | all-to-all | bytes 3473408 | tf_op jit(solution)/shard_map/all_to_all | solution.py:441
  94.3 0.3 shard_map.115
  94.5 12.2 %all_to_all.21 = bf16[8,88,128]{2,1,0:T(8,128)(2,1)S(1)} all-to-all(bf16[8,88,128]{2,1,0:T(8,128)(2,1)S(1)} %bitcast.21), channel_id=1, replica_groups=mesh['tm_0'=4,'tm_1'=4,'tm_2'=8,'dp'=2] {'tm_2'}, dimensions={0} | all-to-all | bytes 360448 | tf_op jit(solution)/shard_map/all_to_all | solution.py:452
  106.8 0.7 shard_map.116
  (2 shorter events, 0.0 us)
Async XLA Ops:
  0.6 37.7 %copy-start.4 = (bf16[64,4,256]{2,1,0:T(4,128)(2,1)S(1)}, bf16[64,4,256]{2,1,0:T(4,128)(2,1)}, u32[]{:S(2)}) copy-start(bf16[64,4,256]{2,1,0:T(4,128)(2,1)} %param.7) | copy-start | bytes 393220
  2.2 36.2 %copy-start.3 = (s32[1,256]{1,0:T(1,128)S(1)}, s32[1,256]{1,0:T(1,128)}, u32[]{:S(2)}) copy-start(s32[1,256]{1,0:T(1,128)} %get-tuple-element.18.offs_ref) | copy-start | bytes 3076
  2.2 26.9 %all-to-all-start = ((s32[128,1,256]{2,1,0:T(1,128)}), s32[128,1,256]{2,1,0:T(1,128)S(1)}, u32[]{:S(2)}, u32[]{:S(2)}) async-start(s32[128,1,256]{2,1,0:T(1,128)} %get-tuple-element.17), calls=%async_computation | async-start | bytes 262144 | tf_op jit(solution)/shard_map/all_to_all | solution.py:372
  30.7 24.6 %all-to-all-start.1 = ((bf16[128,16,128]{2,1,0:T(8,128)(2,1)}), bf16[128,16,128]{2,1,0:T(8,128)(2,1)S(1)}, u32[]{:S(2)}, u32[]{:S(2)}) async-start(bf16[128,16,128]{2,1,0:T(8,128)(2,1)} %bitcast.4), calls=%async_computation.1 | async-start | bytes 1048576 | tf_op jit(solution)/shard_map/all_to_all | solution.py:395
  38.4 1.9 %copy-start = (bf16[768,2048]{1,0:T(8,128)(2,1)S(1)}, bf16[768,2048]{1,0:T(8,128)(2,1)}, u32[]{:S(2)}) copy-start(bf16[768,2048]{1,0:T(8,128)(2,1)} %w_in_ref.3) | copy-start | bytes 9437188
  40.3 15.0 %copy-start.1 = (f32[2048]{0:T(1024)S(1)}, f32[2048]{0:T(1024)}, u32[]{:S(2)}) copy-start(f32[2048]{0:T(1024)} %param.11) | copy-start | bytes 24580
  40.3 15.0 %copy-start.2 = (f32[2048]{0:T(1024)S(1)}, f32[2048]{0:T(1024)}, u32[]{:S(2)}) copy-start(f32[2048]{0:T(1024)} %param.12) | copy-start | bytes 24580
  60.6 3.1 %collective-permute-start = (bf16[320,2048]{1,0:T(8,128)(2,1)S(1)}, bf16[320,2048]{1,0:T(8,128)(2,1)S(1)}, u32[]{:S(2)}, u32[]{:S(2)}) collective-permute-start(bf16[320,2048]{1,0:T(8,128)(2,1)S(1)} %get-tuple-element.23.own_ref), channel_id=1, source_target_pairs={{0,1},{1,0},{2,3},{3,2},{4,5},{5,4},{6,7},{7,6},{8,9},{9,8},{10,11... | collective-permute-start | bytes 3932168 | tf_op jit(solution)/shard_map/ppermute | solution.py:432

commit v9 on v8

--- a/solution.py
+++ b/solution.py
@@ -184,6 +184,8 @@
     wide_ref,
     total_ref,
     td_rows_ref,
+    even_ref,
+    odd_ref,
     sems,
     td_sem,
 ):
@@ -202,7 +204,7 @@
     far_at = at_ref[:, 0:1]
     far = flag(iota((ROWS, N_TM * CAP), 1) == far_at).astype(BF16)
     inputs_ref[:, :S] = state_ref[...]
-    wide_ref[...] = fetched_ref[...].astype(F32)
+    wide_ref[: N_TM * 16, :] = fetched_ref[...].astype(F32)
     gap = jnp.zeros((ROWS, LANES), F32)
     for j in range(G // LANES):
         at = slice(j * LANES, (j + 1) * LANES)
@@ -222,12 +224,16 @@
 
     total_ref[...] = jnp.zeros((ROWS, LANES), F32)
 
-    def forward(n, carry):
+    def product(n, buffer_ref):
         at = pl.ds(pl.multiple_of(n * CHUNK, CHUNK), CHUNK)
-        load(n).wait()
-        pre = dot(inputs[:, :S], state_w_ref[:, at]) + dot(inputs[:, S:], goal_w_ref[:, at])
-        pre = pre + b_in_ref[:, at]
-        sig = 1.0 / (1.0 + jnp.exp(-pre))
+        buffer_ref[...] = dot(inputs[:, :S], state_w_ref[:, at]) + dot(
+            inputs[:, S:], goal_w_ref[:, at]
+        )
+
+    def activate(n, buffer_ref):
+        at = pl.ds(pl.multiple_of(n * CHUNK, CHUNK), CHUNK)
+        pre = buffer_ref[...] + b_in_ref[:, at]
+        sig = 0.5 * jnp.tanh(0.5 * pre) + 0.5
         head = w_out_ref[:, at]
         act = pre * sig
         hidden = act.astype(BF16)
@@ -235,9 +241,25 @@
         slope_ref[:, at] = head * (sig + act * (1.0 - sig))
         term = hidden.astype(F32) * head
         total_ref[...] += term[:, :LANES] + term[:, LANES:]
+
+    count = H // CHUNK
+    load(0).wait()
+    product(0, even_ref)
+
+    def forward(m, carry):
+        load(2 * m + 1).wait()
+
+        @pl.when(2 * m + 2 < count)
+        def _():
+            load(2 * m + 2).wait()
+
+        product(2 * m + 1, odd_ref)
+        activate(2 * m, even_ref)
+        product(jnp.minimum(2 * m + 2, count - 1), even_ref)
+        activate(2 * m + 1, odd_ref)
         return carry
 
-    lax.fori_loop(0, H // CHUNK, forward, 0)
+    lax.fori_loop(0, count // 2, forward, 0)
     value = jnp.sum(total_ref[...], axis=1, keepdims=True) + b_out_ref[:, 0:1]
     error = value - reward
     grad_value = error * scale
@@ -375,7 +397,7 @@
         [((N_TM * 16, LANES), BF16)],
         (place, known, table),
         [
-            pltpu.VMEM((N_TM * 16, LANES), F32),
+            pltpu.VMEM((N_TM * 16 + 16, LANES), F32),
             pltpu.VMEM((N_TM * 16, LANES), BF16),
             pltpu.SemaphoreType.DMA((2,)),
         ],
@@ -418,9 +440,11 @@
             pltpu.VMEM((ROWS, H), BF16),
             pltpu.VMEM((ROWS, S + G), BF16),
             pltpu.VMEM((S, H), BF16),
-            pltpu.VMEM((N_TM * 16, LANES), F32),
+            pltpu.VMEM((N_TM * 16 + 16, LANES), F32),
             pltpu.VMEM((ROWS, LANES), F32),
             pltpu.VMEM((STEPS, ROWS // STEPS), F32),
+            pltpu.VMEM((ROWS, CHUNK), F32),
+            pltpu.VMEM((ROWS, CHUNK), F32),
             pltpu.SemaphoreType.DMA((H // CHUNK,)),
             pltpu.SemaphoreType.DMA,
         ],
@@ -445,7 +469,7 @@
         plane_kernel,
         [((N_LINE * BLOCK, LANES), BF16)],
         (got,),
-        [pltpu.VMEM((PACK, LANES), F32), pltpu.VMEM((N_LINE * 48, LANES), F32)],
+        [pltpu.VMEM((PACK, LANES), F32), pltpu.VMEM((N_LINE * 48 + 48, LANES), F32)],
         10**7,
         6,
     )

time: 108 us -> 107 us (level)
  no operation moved by 1% of the time
where the time goes in v9:
time: 107 us
  blocking collectives  41.8 us (39%)
  waiting for transfers between devices  27.7 us (26%)
  starting transfers between devices  22.7 us (21%)
  Pallas kernels  10.5 us (10%)
  local copies, waits for them, and re-layouts  3.03 us (3%)
  between operations  1.4 us (1%)
    all_to_all x1, blocking collectives, body(): lax.all_to_all(packs.reshape(N_PLANE, PACK, LANES), PLANE, split_axis=0,...  29.5 us
    all_to_all x1, starting transfers between devices, body(): known = lax.all_to_all(many, TM, split_axis=0, concat_axis=0, tiled=True)  15.6 us
    all_to_all x1, waiting for transfers between devices, body(): lax.all_to_all(picked.reshape(N_TM, 16, LANES), TM, split_axis=0, concat_...  14.4 us
    all_to_all x1, blocking collectives, body(): lax.all_to_all(lines.reshape(N_LINE, BLOCK, LANES), LINE, split_axis=0, c...  12.2 us
    pallas_call x7, Pallas kernels, call(): pl.pallas_call(kernel, out_shape=outs, in_specs=specs, out_specs=back, sc...  10.5 us
    all_to_all x1, waiting for transfers between devices, body(): known = lax.all_to_all(many, TM, split_axis=0, concat_axis=0, tiled=True)  10.2 us
    all_to_all x1, starting transfers between devices, body(): lax.all_to_all(picked.reshape(N_TM, 16, LANES), TM, split_axis=0, concat_...  7.01 us
    ppermute x1, waiting for transfers between devices, body(): other = lax.ppermute(send, 'dp', [(0, 1), (1, 0)])  3.02 us
  transfers between devices with their start and end apart: 3, of which 3 were waited for; matrix products, arithmetic and copies ran while one was open for 1% of the time, Pallas kernels for 1%

profile of v9, /device:TPU:2, one launch (start us, length us, event | category | flops | bytes accessed | tf_op | source)
XLA Modules:
  0.0 107.1 jit_solution(5780193455380049493)
XLA Ops:
  0.6 0.0 copy-start.4
  0.6 1.5 %shard_map.110 = (s32[128,1,256]{2,1,0:T(1,128)}, s32[1,256]{1,0:T(1,128)}) custom-call(s32[4,64]{1,0:T(4,128)} %bitcast.27), custom_call_target="tpu_custom_call" | custom-call | flops 1000000 | bytes 1048576 | tf_op jit(solution)/shard_map/pallas_call | solution.py:370
  2.2 0.0 copy-start.3
  2.2 15.6 %all-to-all-start = ((s32[128,1,256]{2,1,0:T(1,128)}), s32[128,1,256]{2,1,0:T(1,128)S(1)}, u32[]{:S(2)}, u32[]{:S(2)}) async-start(s32[128,1,256]{2,1,0:T(1,128)} %get-tuple-element.17), calls=%async_computation | async-start | bytes 262144 | tf_op jit(solution)/shard_map/all_to_all | solution.py:394
  17.8 1.0 reshape.50.table_ref
  18.8 0.1 pad_add_fusion
  18.9 10.2 %all-to-all-done.offs_ref = s32[128,1,256]{2,1,0:T(1,128)S(1)} async-done(((s32[128,1,256]{2,1,0:T(1,128)}), s32[128,1,256]{2,1,0:T(1,128)S(1)}, u32[]{:S(2)}, u32[]{:S(2)}) %all-to-all-start) | async-done | bytes 131104 | tf_op jit(solution)/shard_map/all_to_all | solution.py:394
  29.1 0.1 broadcast_in_dim.6.place_ref
  29.2 1.5 %shard_map.111 = bf16[2048,128]{1,0:T(8,128)(2,1)} custom-call(s32[2,128]{1,0:T(2,128)S(1)} %broadcast_in_dim.6.place_ref, s32[128,1,256]{2,1,0:T(1,128)S(1)} %all-to-all-done.offs_ref, bf16[256,512]{1,0:T(8,128)(2,1)S(1)} %reshape.50.table_ref), custom_call_target="tpu_custom_call" | custom-call | flops 100000000 | bytes 1048576 | tf_op jit(solution)/shard_map/pallas_call | solution.py:370
  30.7 7.0 %all-to-all-start.1 = ((bf16[128,16,128]{2,1,0:T(8,128)(2,1)}), bf16[128,16,128]{2,1,0:T(8,128)(2,1)S(1)}, u32[]{:S(2)}, u32[]{:S(2)}) async-start(bf16[128,16,128]{2,1,0:T(8,128)(2,1)} %bitcast.4), calls=%async_computation.1 | async-start | bytes 1048576 | tf_op jit(solution)/shard_map/all_to_all | solution.py:417
  38.3 0.0 copy-done.4
  38.4 0.0 copy-done.3
  38.4 0.0 copy-start
  38.4 1.9 %copy-done = bf16[768,2048]{1,0:T(8,128)(2,1)S(1)} copy-done((bf16[768,2048]{1,0:T(8,128)(2,1)S(1)}, bf16[768,2048]{1,0:T(8,128)(2,1)}, u32[]{:S(2)}) %copy-start) | copy-done | bytes 3145752
  40.3 0.0 copy-start.1
  40.3 0.0 copy-start.2
  40.3 0.6 shard_map.112
  40.9 14.4 %all-to-all-done.1 = bf16[128,16,128]{2,1,0:T(8,128)(2,1)S(1)} async-done(((bf16[128,16,128]{2,1,0:T(8,128)(2,1)}), bf16[128,16,128]{2,1,0:T(8,128)(2,1)S(1)}, u32[]{:S(2)}, u32[]{:S(2)}) %all-to-all-start.1) | async-done | bytes 524320 | tf_op jit(solution)/shard_map/all_to_all | solution.py:417
  55.3 0.0 copy-done.1
  55.3 0.0 copy-done.2
  55.3 5.0 %shard_map.113 = (f32[4,64]{1,0:T(4,128)}, bf16[320,2048]{1,0:T(8,128)(2,1)S(1)}, bf16[384,256]{1,0:T(8,128)(2,1)S(1)}) custom-call(s32[2,128]{1,0:T(2,128)S(1)} %broadcast_in_dim.6.place_ref, f32[1,128]{1,0:T(1,128)S(1)} %broadcast_in_dim.16.b_out_ref, bf16[2048,128]{1,0:T(8,128)(2,1)S(1)} %bitcast.22, bf16[512,2048]{1,0:T(8,128)(2,1)S(1)} %get-tuple-element.19.goal_w_ref, ...), custom_call_target="tpu_custom_call" | custom-call | flops 2000000000 | bytes 1048576 | tf_op jit(solution)/shard_map/pallas_call | solution.py:370
  60.2 0.1 collective-permute-start
  60.3 3.0 %collective-permute-done.other_ref = bf16[320,2048]{1,0:T(8,128)(2,1)S(1)} collective-permute-done((bf16[320,2048]{1,0:T(8,128)(2,1)S(1)}, bf16[320,2048]{1,0:T(8,128)(2,1)S(1)}, u32[]{:S(2)}, u32[]{:S(2)}) %collective-permute-start) | collective-permute-done | bytes 1310752 | tf_op jit(solution)/shard_map/ppermute | solution.py:456
  63.4 1.0 shard_map.114
  64.4 29.5 %all_to_all.20 = bf16[16,424,128]{2,1,0:T(8,128)(2,1)S(1)} all-to-all(bf16[16,424,128]{2,1,0:T(8,128)(2,1)S(1)} %bitcast.18), channel_id=1, replica_groups=mesh['tm_0'=4,'tm_1'=4,'tm_2'=8,'dp'=2] {'tm_0','tm_1'}, dimensions={0} | all-to-all | bytes 3473408 | tf_op jit(solution)/shard_map/all_to_all | solution.py:465
  93.9 0.3 shard_map.115
  94.2 12.2 %all_to_all.21 = bf16[8,88,128]{2,1,0:T(8,128)(2,1)S(1)} all-to-all(bf16[8,88,128]{2,1,0:T(8,128)(2,1)S(1)} %bitcast.21), channel_id=1, replica_groups=mesh['tm_0'=4,'tm_1'=4,'tm_2'=8,'dp'=2] {'tm_2'}, dimensions={0} | all-to-all | bytes 360448 | tf_op jit(solution)/shard_map/all_to_all | solution.py:476
  106.4 0.7 shard_map.116
  (2 shorter events, 0.0 us)
Async XLA Ops:
  0.6 37.7 %copy-start.4 = (bf16[64,4,256]{2,1,0:T(4,128)(2,1)S(1)}, bf16[64,4,256]{2,1,0:T(4,128)(2,1)}, u32[]{:S(2)}) copy-start(bf16[64,4,256]{2,1,0:T(4,128)(2,1)} %param.7) | copy-start | bytes 393220
  2.2 36.2 %copy-start.3 = (s32[1,256]{1,0:T(1,128)S(1)}, s32[1,256]{1,0:T(1,128)}, u32[]{:S(2)}) copy-start(s32[1,256]{1,0:T(1,128)} %get-tuple-element.18.offs_ref) | copy-start | bytes 3076
  2.2 26.9 %all-to-all-start = ((s32[128,1,256]{2,1,0:T(1,128)}), s32[128,1,256]{2,1,0:T(1,128)S(1)}, u32[]{:S(2)}, u32[]{:S(2)}) async-start(s32[128,1,256]{2,1,0:T(1,128)} %get-tuple-element.17), calls=%async_computation | async-start | bytes 262144 | tf_op jit(solution)/shard_map/all_to_all | solution.py:394
  30.7 24.6 %all-to-all-start.1 = ((bf16[128,16,128]{2,1,0:T(8,128)(2,1)}), bf16[128,16,128]{2,1,0:T(8,128)(2,1)S(1)}, u32[]{:S(2)}, u32[]{:S(2)}) async-start(bf16[128,16,128]{2,1,0:T(8,128)(2,1)} %bitcast.4), calls=%async_computation.1 | async-start | bytes 1048576 | tf_op jit(solution)/shard_map/all_to_all | solution.py:417
  38.4 1.9 %copy-start = (bf16[768,2048]{1,0:T(8,128)(2,1)S(1)}, bf16[768,2048]{1,0:T(8,128)(2,1)}, u32[]{:S(2)}) copy-start(bf16[768,2048]{1,0:T(8,128)(2,1)} %w_in_ref.3) | copy-start | bytes 9437188
  40.3 15.0 %copy-start.1 = (f32[2048]{0:T(1024)S(1)}, f32[2048]{0:T(1024)}, u32[]{:S(2)}) copy-start(f32[2048]{0:T(1024)} %param.11) | copy-start | bytes 24580
  40.3 15.0 %copy-start.2 = (f32[2048]{0:T(1024)S(1)}, f32[2048]{0:T(1024)}, u32[]{:S(2)}) copy-start(f32[2048]{0:T(1024)} %param.12) | copy-start | bytes 24580
  60.2 3.1 %collective-permute-start = (bf16[320,2048]{1,0:T(8,128)(2,1)S(1)}, bf16[320,2048]{1,0:T(8,128)(2,1)S(1)}, u32[]{:S(2)}, u32[]{:S(2)}) collective-permute-start(bf16[320,2048]{1,0:T(8,128)(2,1)S(1)} %get-tuple-element.23.own_ref), channel_id=1, source_target_pairs={{0,1},{1,0},{2,3},{3,2},{4,5},{5,4},{6,7},{7,6},{8,9},{9,8},{10,11... | collective-permute-start | bytes 3932168 | tf_op jit(solution)/shard_map/ppermute | solution.py:456

commit v10 on v9

--- a/solution.py
+++ b/solution.py
@@ -176,16 +176,16 @@
     w_out_ref,
     td_ref,
     send_ref,
-    keep_ref,
+    inputs_ref,
     slope_ref,
     hidden_ref,
-    inputs_ref,
     state_w_ref,
     wide_ref,
     total_ref,
     td_rows_ref,
     even_ref,
     odd_ref,
+    sums_ref,
     sems,
     td_sem,
 ):
@@ -216,8 +216,6 @@
     reward = -(jnp.sum(gap, axis=1, keepdims=True) * (1.0 / G))
     inputs = inputs_ref[...]
 
-    kept = dot(half_rows(core), inputs, (((1,), (1,)), ((), ())))
-    keep_ref[...] = kept.astype(BF16)
     sent = dot(half_rows(1 - core), inputs, (((1,), (1,)), ((), ()))).astype(BF16)
     for b in range(H // ROWS):
         send_ref[ROWS : ROWS + 48, b * ROWS : (b + 1) * ROWS] = sent[b * 48 : (b + 1) * 48, :]
@@ -281,13 +279,20 @@
         send_ref[:ROWS, at] = grad_pre.astype(BF16)
         first = jnp.sum(grad_pre, axis=0, keepdims=True)
         second = jnp.sum(grad_value * hidden_ref[:, at].astype(F32), axis=0, keepdims=True)
-        third = jnp.broadcast_to(total_value, (1, CHUNK))
-        rows = stack_rows(three(first) + three(second) + three(third), 16)
-        send_ref[ROWS + 48 : ROWS + 64, at] = rows.astype(BF16)
+        sums_ref[0:1, at] = first
+        sums_ref[1:2, at] = second
         return carry
 
     lax.fori_loop(0, H // CHUNK, backward, 0)
+    third = jnp.broadcast_to(total_value, (1, H))
+    rows = three(sums_ref[0:1, :]) + three(sums_ref[1:2, :]) + three(third)
+    send_ref[ROWS + 48 : ROWS + 64, :] = stack_rows(rows, 16).astype(BF16)
     td_copy.wait()
+
+
+def keep_kernel(place_ref, inputs_ref, keep_ref):
+    core = place_ref[1:2, 0:1]
+    keep_ref[...] = dot(half_rows(core), inputs_ref[...], (((1,), (1,)), ((), ()))).astype(BF16)
 
 
 PACK = 424
@@ -419,9 +424,9 @@
     ).reshape(N_TM * 16, LANES)
     head_bias = jnp.broadcast_to(b_out[None], (1, LANES))
     scale = 1.0 / math.sqrt(ROWS * N_TM * 2)
-    td, send, keep = call(
+    td, send, inputs = call(
         functools.partial(main_kernel, scale),
-        [((STEPS, ROWS // STEPS), F32), ((ROWS + 64, H), BF16), ((HALF, ROWS), BF16)],
+        [((STEPS, ROWS // STEPS), F32), ((ROWS + 64, H), BF16), ((ROWS, S + G), BF16)],
         (
             place,
             head_bias,
@@ -438,13 +443,13 @@
         [
             pltpu.VMEM((ROWS, H), F32),
             pltpu.VMEM((ROWS, H), BF16),
-            pltpu.VMEM((ROWS, S + G), BF16),
             pltpu.VMEM((S, H), BF16),
             pltpu.VMEM((N_TM * 16 + 16, LANES), F32),
             pltpu.VMEM((ROWS, LANES), F32),
             pltpu.VMEM((STEPS, ROWS // STEPS), F32),
             pltpu.VMEM((ROWS, CHUNK), F32),
             pltpu.VMEM((ROWS, CHUNK), F32),
+            pltpu.VMEM((8, H), F32),
             pltpu.SemaphoreType.DMA((H // CHUNK,)),
             pltpu.SemaphoreType.DMA,
         ],
@@ -454,6 +459,9 @@
         (0,),
     )
     other = lax.ppermute(send, "dp", [(0, 1), (1, 0)])
+    (keep,) = call(
+        keep_kernel, [((HALF, ROWS), BF16)], (place, inputs), [], 10**9, 8
+    )
     (packs,) = call(
         product_kernel,
         [((N_PLANE * PACK, LANES), BF16)],

time: 107 us -> 107 us (level)
    pallas_call x7 -> x8, Pallas kernels: 10.5 us -> 10.7 us  [call(): pl.pallas_call(kernel, out_shape=outs, in_specs=specs, out_specs=back, sc...]
where the time goes in v10:
time: 107 us
  blocking collectives  41.8 us (39%)
  waiting for transfers between devices  27.3 us (26%)
  starting transfers between devices  22.7 us (21%)
  Pallas kernels  10.7 us (10%)
  local copies, waits for them, and re-layouts  3.03 us (3%)
  between operations  1.41 us (1%)
    all_to_all x1, blocking collectives, body(): lax.all_to_all(packs.reshape(N_PLANE, PACK, LANES), PLANE, split_axis=0,...  29.5 us
    all_to_all x1, starting transfers between devices, body(): known = lax.all_to_all(many, TM, split_axis=0, concat_axis=0, tiled=True)  15.6 us
    all_to_all x1, waiting for transfers between devices, body(): lax.all_to_all(picked.reshape(N_TM, 16, LANES), TM, split_axis=0, concat_...  14.4 us
    all_to_all x1, blocking collectives, body(): lax.all_to_all(lines.reshape(N_LINE, BLOCK, LANES), LINE, split_axis=0, c...  12.2 us
    pallas_call x8, Pallas kernels, call(): pl.pallas_call(kernel, out_shape=outs, in_specs=specs, out_specs=back, sc...  10.7 us
    all_to_all x1, waiting for transfers between devices, body(): known = lax.all_to_all(many, TM, split_axis=0, concat_axis=0, tiled=True)  10.2 us
    all_to_all x1, starting transfers between devices, body(): lax.all_to_all(picked.reshape(N_TM, 16, LANES), TM, split_axis=0, concat_...  7.01 us
    ppermute x1, waiting for transfers between devices, body(): other = lax.ppermute(send, 'dp', [(0, 1), (1, 0)])  2.63 us
  transfers between devices with their start and end apart: 3, of which 3 were waited for; matrix products, arithmetic and copies ran while one was open for 1% of the time, Pallas kernels for 1%

profile of v10, /device:TPU:2, one launch (start us, length us, event | category | flops | bytes accessed | tf_op | source)
XLA Modules:
  0.0 107.0 jit_solution(8500448725575578738)
XLA Ops:
  0.6 0.0 copy-start.4
  0.6 1.5 %shard_map.110 = (s32[128,1,256]{2,1,0:T(1,128)}, s32[1,256]{1,0:T(1,128)}) custom-call(s32[4,64]{1,0:T(4,128)} %bitcast.27), custom_call_target="tpu_custom_call" | custom-call | flops 1000000 | bytes 1048576 | tf_op jit(solution)/shard_map/pallas_call | solution.py:375
  2.2 0.0 copy-start.3
  2.2 15.6 %all-to-all-start = ((s32[128,1,256]{2,1,0:T(1,128)}), s32[128,1,256]{2,1,0:T(1,128)S(1)}, u32[]{:S(2)}, u32[]{:S(2)}) async-start(s32[128,1,256]{2,1,0:T(1,128)} %get-tuple-element.17), calls=%async_computation | async-start | bytes 262144 | tf_op jit(solution)/shard_map/all_to_all | solution.py:399
  17.8 1.0 reshape.50.table_ref
  18.8 0.1 pad_add_fusion
  18.9 10.2 %all-to-all-done.offs_ref = s32[128,1,256]{2,1,0:T(1,128)S(1)} async-done(((s32[128,1,256]{2,1,0:T(1,128)}), s32[128,1,256]{2,1,0:T(1,128)S(1)}, u32[]{:S(2)}, u32[]{:S(2)}) %all-to-all-start) | async-done | bytes 131104 | tf_op jit(solution)/shard_map/all_to_all | solution.py:399
  29.1 0.1 broadcast_in_dim.6.place_ref
  29.2 1.5 %shard_map.111 = bf16[2048,128]{1,0:T(8,128)(2,1)} custom-call(s32[2,128]{1,0:T(2,128)S(1)} %broadcast_in_dim.6.place_ref, s32[128,1,256]{2,1,0:T(1,128)S(1)} %all-to-all-done.offs_ref, bf16[256,512]{1,0:T(8,128)(2,1)S(1)} %reshape.50.table_ref), custom_call_target="tpu_custom_call" | custom-call | flops 100000000 | bytes 1048576 | tf_op jit(solution)/shard_map/pallas_call | solution.py:375
  30.7 7.0 %all-to-all-start.1 = ((bf16[128,16,128]{2,1,0:T(8,128)(2,1)}), bf16[128,16,128]{2,1,0:T(8,128)(2,1)S(1)}, u32[]{:S(2)}, u32[]{:S(2)}) async-start(bf16[128,16,128]{2,1,0:T(8,128)(2,1)} %bitcast.4), calls=%async_computation.1 | async-start | bytes 1048576 | tf_op jit(solution)/shard_map/all_to_all | solution.py:422
  38.3 0.0 copy-done.4
  38.4 0.0 copy-done.3
  38.4 0.0 copy-start
  38.4 1.9 %copy-done = bf16[768,2048]{1,0:T(8,128)(2,1)S(1)} copy-done((bf16[768,2048]{1,0:T(8,128)(2,1)S(1)}, bf16[768,2048]{1,0:T(8,128)(2,1)}, u32[]{:S(2)}) %copy-start) | copy-done | bytes 3145752
  40.3 0.0 copy-start.1
  40.3 0.0 copy-start.2
  40.3 0.6 shard_map.112
  40.9 14.4 %all-to-all-done.1 = bf16[128,16,128]{2,1,0:T(8,128)(2,1)S(1)} async-done(((bf16[128,16,128]{2,1,0:T(8,128)(2,1)}), bf16[128,16,128]{2,1,0:T(8,128)(2,1)S(1)}, u32[]{:S(2)}, u32[]{:S(2)}) %all-to-all-start.1) | async-done | bytes 524320 | tf_op jit(solution)/shard_map/all_to_all | solution.py:422
  55.3 0.0 copy-done.1
  55.3 0.0 copy-done.2
  55.3 4.9 %shard_map.113 = (f32[4,64]{1,0:T(4,128)}, bf16[320,2048]{1,0:T(8,128)(2,1)S(1)}, bf16[256,768]{1,0:T(8,128)(2,1)S(1)}) custom-call(s32[2,128]{1,0:T(2,128)S(1)} %broadcast_in_dim.6.place_ref, f32[1,128]{1,0:T(1,128)S(1)} %broadcast_in_dim.16.b_out_ref, bf16[2048,128]{1,0:T(8,128)(2,1)S(1)} %bitcast.22, bf16[512,2048]{1,0:T(8,128)(2,1)S(1)} %get-tuple-element.19.goal_w_ref, ...), custom_call_target="tpu_custom_call" | custom-call | flops 2000000000 | bytes 1048576 | tf_op jit(solution)/shard_map/pallas_call | solution.py:375
  60.2 0.1 collective-permute-start
  60.3 0.4 shard_map.114.keep_ref
  60.6 2.6 %collective-permute-done.other_ref = bf16[320,2048]{1,0:T(8,128)(2,1)S(1)} collective-permute-done((bf16[320,2048]{1,0:T(8,128)(2,1)S(1)}, bf16[320,2048]{1,0:T(8,128)(2,1)S(1)}, u32[]{:S(2)}, u32[]{:S(2)}) %collective-permute-start) | collective-permute-done | bytes 1310752 | tf_op jit(solution)/shard_map/ppermute | solution.py:461
  63.3 1.0 shard_map.115
  64.3 29.5 %all_to_all.20 = bf16[16,424,128]{2,1,0:T(8,128)(2,1)S(1)} all-to-all(bf16[16,424,128]{2,1,0:T(8,128)(2,1)S(1)} %bitcast.18), channel_id=1, replica_groups=mesh['tm_0'=4,'tm_1'=4,'tm_2'=8,'dp'=2] {'tm_0','tm_1'}, dimensions={0} | all-to-all | bytes 3473408 | tf_op jit(solution)/shard_map/all_to_all | solution.py:473
  93.8 0.3 shard_map.116
  94.1 12.2 %all_to_all.21 = bf16[8,88,128]{2,1,0:T(8,128)(2,1)S(1)} all-to-all(bf16[8,88,128]{2,1,0:T(8,128)(2,1)S(1)} %bitcast.21), channel_id=1, replica_groups=mesh['tm_0'=4,'tm_1'=4,'tm_2'=8,'dp'=2] {'tm_2'}, dimensions={0} | all-to-all | bytes 360448 | tf_op jit(solution)/shard_map/all_to_all | solution.py:484
  106.3 0.7 shard_map.117
  (2 shorter events, 0.0 us)
Async XLA Ops:
  0.6 37.7 %copy-start.4 = (bf16[64,4,256]{2,1,0:T(4,128)(2,1)S(1)}, bf16[64,4,256]{2,1,0:T(4,128)(2,1)}, u32[]{:S(2)}) copy-start(bf16[64,4,256]{2,1,0:T(4,128)(2,1)} %param.7) | copy-start | bytes 393220
  2.2 36.2 %copy-start.3 = (s32[1,256]{1,0:T(1,128)S(1)}, s32[1,256]{1,0:T(1,128)}, u32[]{:S(2)}) copy-start(s32[1,256]{1,0:T(1,128)} %get-tuple-element.18.offs_ref) | copy-start | bytes 3076
  2.2 26.9 %all-to-all-start = ((s32[128,1,256]{2,1,0:T(1,128)}), s32[128,1,256]{2,1,0:T(1,128)S(1)}, u32[]{:S(2)}, u32[]{:S(2)}) async-start(s32[128,1,256]{2,1,0:T(1,128)} %get-tuple-element.17), calls=%async_computation | async-start | bytes 262144 | tf_op jit(solution)/shard_map/all_to_all | solution.py:399
  30.7 24.6 %all-to-all-start.1 = ((bf16[128,16,128]{2,1,0:T(8,128)(2,1)}), bf16[128,16,128]{2,1,0:T(8,128)(2,1)S(1)}, u32[]{:S(2)}, u32[]{:S(2)}) async-start(bf16[128,16,128]{2,1,0:T(8,128)(2,1)} %bitcast.4), calls=%async_computation.1 | async-start | bytes 1048576 | tf_op jit(solution)/shard_map/all_to_all | solution.py:422
  38.4 1.9 %copy-start = (bf16[768,2048]{1,0:T(8,128)(2,1)S(1)}, bf16[768,2048]{1,0:T(8,128)(2,1)}, u32[]{:S(2)}) copy-start(bf16[768,2048]{1,0:T(8,128)(2,1)} %w_in_ref.3) | copy-start | bytes 9437188
  40.3 15.0 %copy-start.1 = (f32[2048]{0:T(1024)S(1)}, f32[2048]{0:T(1024)}, u32[]{:S(2)}) copy-start(f32[2048]{0:T(1024)} %param.11) | copy-start | bytes 24580
  40.3 15.0 %copy-start.2 = (f32[2048]{0:T(1024)S(1)}, f32[2048]{0:T(1024)}, u32[]{:S(2)}) copy-start(f32[2048]{0:T(1024)} %param.12) | copy-start | bytes 24580
  60.2 3.1 %collective-permute-start = (bf16[320,2048]{1,0:T(8,128)(2,1)S(1)}, bf16[320,2048]{1,0:T(8,128)(2,1)S(1)}, u32[]{:S(2)}, u32[]{:S(2)}) collective-permute-start(bf16[320,2048]{1,0:T(8,128)(2,1)S(1)} %get-tuple-element.23.own_ref), channel_id=1, source_target_pairs={{0,1},{1,0},{2,3},{3,2},{4,5},{5,4},{6,7},{7,6},{8,9},{9,8},{10,11... | collective-permute-start | bytes 3932168 | tf_op jit(solution)/shard_map/ppermute | solution.py:461

commit v11 on v9

--- a/solution.py
+++ b/solution.py
@@ -73,9 +73,9 @@
             jnp.where(hit & (rank == float(c)), position, 0.0), axis=1, keepdims=True
         )
         wanted.append(flag(row.astype(F32) + 1.0 == place).astype(BF16))
-    half = N_TM // 2
+    half = N_TM // 4
     copies = []
-    for h in range(2):
+    for h in range(4):
         part = jnp.concatenate([w[h * half : (h + 1) * half] for w in wanted], axis=0)
         picked = dot(part, table_ref[...])
         for c in range(CAP):
@@ -399,7 +399,7 @@
         [
             pltpu.VMEM((N_TM * 16 + 16, LANES), F32),
             pltpu.VMEM((N_TM * 16, LANES), BF16),
-            pltpu.SemaphoreType.DMA((2,)),
+            pltpu.SemaphoreType.DMA((4,)),
         ],
         10**8,
         8,

time: 107 us -> 107 us (level)
  no operation moved by 1% of the time
where the time goes in v11:
time: 107 us
  blocking collectives  41.8 us (39%)
  waiting for transfers between devices  27.7 us (26%)
  starting transfers between devices  22.7 us (21%)
  Pallas kernels  10.4 us (10%)
  local copies, waits for them, and re-layouts  3.03 us (3%)
  between operations  1.4 us (1%)
    all_to_all x1, blocking collectives, body(): lax.all_to_all(packs.reshape(N_PLANE, PACK, LANES), PLANE, split_axis=0,...  29.5 us
    all_to_all x1, starting transfers between devices, body(): known = lax.all_to_all(many, TM, split_axis=0, concat_axis=0, tiled=True)  15.6 us
    all_to_all x1, waiting for transfers between devices, body(): lax.all_to_all(picked.reshape(N_TM, 16, LANES), TM, split_axis=0, concat_...  14.4 us
    all_to_all x1, blocking collectives, body(): lax.all_to_all(lines.reshape(N_LINE, BLOCK, LANES), LINE, split_axis=0, c...  12.2 us
    pallas_call x7, Pallas kernels, call(): pl.pallas_call(kernel, out_shape=outs, in_specs=specs, out_specs=back, sc...  10.4 us
    all_to_all x1, waiting for transfers between devices, body(): known = lax.all_to_all(many, TM, split_axis=0, concat_axis=0, tiled=True)  10.2 us
    all_to_all x1, starting transfers between devices, body(): lax.all_to_all(picked.reshape(N_TM, 16, LANES), TM, split_axis=0, concat_...  7.02 us
    ppermute x1, waiting for transfers between devices, body(): other = lax.ppermute(send, 'dp', [(0, 1), (1, 0)])  3.02 us
  transfers between devices with their start and end apart: 3, of which 3 were waited for; matrix products, arithmetic and copies ran while one was open for 1% of the time, Pallas kernels for 1%

profile of v11, /device:TPU:2, one launch (start us, length us, event | category | flops | bytes accessed | tf_op | source)
XLA Modules:
  0.0 107.0 jit_solution(2791260457380197941)
XLA Ops:
  0.6 0.0 copy-start.4
  0.6 1.5 %shard_map.110 = (s32[128,1,256]{2,1,0:T(1,128)}, s32[1,256]{1,0:T(1,128)}) custom-call(s32[4,64]{1,0:T(4,128)} %bitcast.27), custom_call_target="tpu_custom_call" | custom-call | flops 1000000 | bytes 1048576 | tf_op jit(solution)/shard_map/pallas_call | solution.py:370
  2.2 0.0 copy-start.3
  2.2 15.6 %all-to-all-start = ((s32[128,1,256]{2,1,0:T(1,128)}), s32[128,1,256]{2,1,0:T(1,128)S(1)}, u32[]{:S(2)}, u32[]{:S(2)}) async-start(s32[128,1,256]{2,1,0:T(1,128)} %get-tuple-element.17), calls=%async_computation | async-start | bytes 262144 | tf_op jit(solution)/shard_map/all_to_all | solution.py:394
  17.8 1.0 reshape.50.table_ref
  18.8 0.1 pad_add_fusion
  18.9 10.2 %all-to-all-done.offs_ref = s32[128,1,256]{2,1,0:T(1,128)S(1)} async-done(((s32[128,1,256]{2,1,0:T(1,128)}), s32[128,1,256]{2,1,0:T(1,128)S(1)}, u32[]{:S(2)}, u32[]{:S(2)}) %all-to-all-start) | async-done | bytes 131104 | tf_op jit(solution)/shard_map/all_to_all | solution.py:394
  29.1 0.1 broadcast_in_dim.6.place_ref
  29.2 1.4 %shard_map.111 = bf16[2048,128]{1,0:T(8,128)(2,1)} custom-call(s32[2,128]{1,0:T(2,128)S(1)} %broadcast_in_dim.6.place_ref, s32[128,1,256]{2,1,0:T(1,128)S(1)} %all-to-all-done.offs_ref, bf16[256,512]{1,0:T(8,128)(2,1)S(1)} %reshape.50.table_ref), custom_call_target="tpu_custom_call" | custom-call | flops 100000000 | bytes 1048576 | tf_op jit(solution)/shard_map/pallas_call | solution.py:370
  30.6 7.0 %all-to-all-start.1 = ((bf16[128,16,128]{2,1,0:T(8,128)(2,1)}), bf16[128,16,128]{2,1,0:T(8,128)(2,1)S(1)}, u32[]{:S(2)}, u32[]{:S(2)}) async-start(bf16[128,16,128]{2,1,0:T(8,128)(2,1)} %bitcast.4), calls=%async_computation.1 | async-start | bytes 1048576 | tf_op jit(solution)/shard_map/all_to_all | solution.py:417
  38.3 0.0 copy-done.4
  38.3 0.0 copy-done.3
  38.4 0.0 copy-start
  38.4 1.9 %copy-done = bf16[768,2048]{1,0:T(8,128)(2,1)S(1)} copy-done((bf16[768,2048]{1,0:T(8,128)(2,1)S(1)}, bf16[768,2048]{1,0:T(8,128)(2,1)}, u32[]{:S(2)}) %copy-start) | copy-done | bytes 3145752
  40.2 0.0 copy-start.1
  40.2 0.0 copy-start.2
  40.3 0.6 shard_map.112
  40.8 14.4 %all-to-all-done.1 = bf16[128,16,128]{2,1,0:T(8,128)(2,1)S(1)} async-done(((bf16[128,16,128]{2,1,0:T(8,128)(2,1)}), bf16[128,16,128]{2,1,0:T(8,128)(2,1)S(1)}, u32[]{:S(2)}, u32[]{:S(2)}) %all-to-all-start.1) | async-done | bytes 524320 | tf_op jit(solution)/shard_map/all_to_all | solution.py:417
  55.2 0.0 copy-done.1
  55.2 0.0 copy-done.2
  55.2 5.0 %shard_map.113 = (f32[4,64]{1,0:T(4,128)}, bf16[320,2048]{1,0:T(8,128)(2,1)S(1)}, bf16[384,256]{1,0:T(8,128)(2,1)S(1)}) custom-call(s32[2,128]{1,0:T(2,128)S(1)} %broadcast_in_dim.6.place_ref, f32[1,128]{1,0:T(1,128)S(1)} %broadcast_in_dim.16.b_out_ref, bf16[2048,128]{1,0:T(8,128)(2,1)S(1)} %bitcast.22, bf16[512,2048]{1,0:T(8,128)(2,1)S(1)} %get-tuple-element.19.goal_w_ref, ...), custom_call_target="tpu_custom_call" | custom-call | flops 2000000000 | bytes 1048576 | tf_op jit(solution)/shard_map/pallas_call | solution.py:370
  60.2 0.1 collective-permute-start
  60.3 3.0 %collective-permute-done.other_ref = bf16[320,2048]{1,0:T(8,128)(2,1)S(1)} collective-permute-done((bf16[320,2048]{1,0:T(8,128)(2,1)S(1)}, bf16[320,2048]{1,0:T(8,128)(2,1)S(1)}, u32[]{:S(2)}, u32[]{:S(2)}) %collective-permute-start) | collective-permute-done | bytes 1310752 | tf_op jit(solution)/shard_map/ppermute | solution.py:456
  63.3 1.0 shard_map.114
  64.3 29.5 %all_to_all.20 = bf16[16,424,128]{2,1,0:T(8,128)(2,1)S(1)} all-to-all(bf16[16,424,128]{2,1,0:T(8,128)(2,1)S(1)} %bitcast.18), channel_id=1, replica_groups=mesh['tm_0'=4,'tm_1'=4,'tm_2'=8,'dp'=2] {'tm_0','tm_1'}, dimensions={0} | all-to-all | bytes 3473408 | tf_op jit(solution)/shard_map/all_to_all | solution.py:465
  93.9 0.3 shard_map.115
  94.1 12.2 %all_to_all.21 = bf16[8,88,128]{2,1,0:T(8,128)(2,1)S(1)} all-to-all(bf16[8,88,128]{2,1,0:T(8,128)(2,1)S(1)} %bitcast.21), channel_id=1, replica_groups=mesh['tm_0'=4,'tm_1'=4,'tm_2'=8,'dp'=2] {'tm_2'}, dimensions={0} | all-to-all | bytes 360448 | tf_op jit(solution)/shard_map/all_to_all | solution.py:476
  106.4 0.7 shard_map.116
  (2 shorter events, 0.0 us)
Async XLA Ops:
  0.6 37.7 %copy-start.4 = (bf16[64,4,256]{2,1,0:T(4,128)(2,1)S(1)}, bf16[64,4,256]{2,1,0:T(4,128)(2,1)}, u32[]{:S(2)}) copy-start(bf16[64,4,256]{2,1,0:T(4,128)(2,1)} %param.7) | copy-start | bytes 393220
  2.2 36.2 %copy-start.3 = (s32[1,256]{1,0:T(1,128)S(1)}, s32[1,256]{1,0:T(1,128)}, u32[]{:S(2)}) copy-start(s32[1,256]{1,0:T(1,128)} %get-tuple-element.18.offs_ref) | copy-start | bytes 3076
  2.2 26.9 %all-to-all-start = ((s32[128,1,256]{2,1,0:T(1,128)}), s32[128,1,256]{2,1,0:T(1,128)S(1)}, u32[]{:S(2)}, u32[]{:S(2)}) async-start(s32[128,1,256]{2,1,0:T(1,128)} %get-tuple-element.17), calls=%async_computation | async-start | bytes 262144 | tf_op jit(solution)/shard_map/all_to_all | solution.py:394
  30.6 24.6 %all-to-all-start.1 = ((bf16[128,16,128]{2,1,0:T(8,128)(2,1)}), bf16[128,16,128]{2,1,0:T(8,128)(2,1)S(1)}, u32[]{:S(2)}, u32[]{:S(2)}) async-start(bf16[128,16,128]{2,1,0:T(8,128)(2,1)} %bitcast.4), calls=%async_computation.1 | async-start | bytes 1048576 | tf_op jit(solution)/shard_map/all_to_all | solution.py:417
  38.4 1.9 %copy-start = (bf16[768,2048]{1,0:T(8,128)(2,1)S(1)}, bf16[768,2048]{1,0:T(8,128)(2,1)}, u32[]{:S(2)}) copy-start(bf16[768,2048]{1,0:T(8,128)(2,1)} %w_in_ref.3) | copy-start | bytes 9437188
  40.2 15.0 %copy-start.1 = (f32[2048]{0:T(1024)S(1)}, f32[2048]{0:T(1024)}, u32[]{:S(2)}) copy-start(f32[2048]{0:T(1024)} %param.11) | copy-start | bytes 24580
  40.2 15.0 %copy-start.2 = (f32[2048]{0:T(1024)S(1)}, f32[2048]{0:T(1024)}, u32[]{:S(2)}) copy-start(f32[2048]{0:T(1024)} %param.12) | copy-start | bytes 24580
  60.2 3.1 %collective-permute-start = (bf16[320,2048]{1,0:T(8,128)(2,1)S(1)}, bf16[320,2048]{1,0:T(8,128)(2,1)S(1)}, u32[]{:S(2)}, u32[]{:S(2)}) collective-permute-start(bf16[320,2048]{1,0:T(8,128)(2,1)S(1)} %get-tuple-element.23.own_ref), channel_id=1, source_target_pairs={{0,1},{1,0},{2,3},{3,2},{4,5},{5,4},{6,7},{7,6},{8,9},{9,8},{10,11... | collective-permute-start | bytes 3932168 | tf_op jit(solution)/shard_map/ppermute | solution.py:456
